TPU v7x, 128 devices: a whole 4x4x4 slice. The times are simulated.
128 devices in a mesh: dp: 8 (over z, core), cp: 16 (over x, y).
Axes of the slice: x: 4, y: 4, z: 4, core: 2. Of those that a mesh axis runs over, the one named last changes fastest.
Arguments:
- row_owner: int32 [16384, 1], P(('dp', 'cp')), may hold values from 0 to 127; in each aligned block of 128 rows (0 to 127, 128 to 255, ...) at most 4 rows name the same one
- slot_row: int32 [16384], P(('dp', 'cp')), may hold values from 0 to 2559
- hot_table: bfloat16 [65536, 512], P(('dp', 'cp')), may hold values from -6 to 6
- cold_table: bfloat16 [262144, 128], P(('dp', 'cp')), may hold values from -6 to 6
- cold_projection: bfloat16 [128, 512], replicated, may hold values from -0.5 to 0.5
- joined_weight: bfloat16 [512, 2048], replicated, may hold values from -0.25 to 0.25
- output_weight: bfloat16 [512, 512], replicated, may hold values from -0.25 to 0.25
- cotangent: bfloat16 [16384, 512], P(('dp', 'cp')), may hold values from -6 to 6
Outputs:
- layer_out: bfloat16 [16384, 512], P(('dp', 'cp'))
- hot_gradient: float32 [65536, 512], P(('dp', 'cp'))
- cold_gradient: float32 [262144, 128], P(('dp', 'cp'))
- projection_gradient: float32 [128, 512], replicated
- joined_gradient: float32 [512, 2048], replicated
- output_gradient: float32 [512, 512], replicated
Inputs may be any that keep to these rules, and one draw needn't show every extreme that they name: `row_owner`: in each aligned block of 128 rows (the rows of one device) no owner is named by more than 4 rows.
All inputs are finite; a program needn't handle non-finite values.
Results may differ from a plain program's by a relative error of at most 0.013.
Values may be sent and summed in bfloat16 or wider, within the bound.
A program may use at most 128 MiB of HBM per device.

v0:
```python
import math

import jax
import jax.numpy as jnp
from jax import lax
from jax.sharding import PartitionSpec as P

HEADS = 8


EPSILON = 1e-05
block_limit = 1024


def side_by_side(arrays, axis, dim, along):
    ends, at = ([], 0)
    for a in arrays[:-1]:
        at += a.shape[along]
        ends.append(at)
    both = jnp.concatenate(arrays, axis=along)
    return tuple(jnp.split(lax.all_gather(both, axis, axis=dim, tiled=True), ends, axis=along))


def cut_along(x, dim, length):
    dims = x.shape
    blocks = x.reshape(*dims[:dim], length, dims[dim] // length, *dims[dim + 1 :])
    return jnp.moveaxis(blocks, dim, 0)


def edges_of(length, count):
    unit = 8 if length >= 8 * count else 1
    return [length // unit * k // count * unit for k in range(1, count)]


def in_order(blocks, dim):
    blocks = jnp.moveaxis(blocks, 0, dim)
    dims = blocks.shape
    return blocks.reshape(*dims[:dim], dims[dim] * dims[dim + 1], *dims[dim + 2 :])


def several_exchanges(x, axis, pieces, split_dim, concat_dim):
    blocks = cut_along(x, split_dim, lax.axis_size(axis))
    split_at = max(range(1, max(2, blocks.ndim - 1)), key=lambda d: blocks.shape[d])
    gathered = []
    for piece in jnp.split(blocks, edges_of(blocks.shape[split_at], pieces), axis=split_at):
        if piece.size:
            gathered.append(lax.all_to_all(piece, axis, split_axis=0, concat_axis=0, tiled=True))
    return in_order(jnp.concatenate(gathered, axis=split_at), concat_dim)


def silu_slope(values):
    sigmoid_v = jax.nn.sigmoid(values)
    return sigmoid_v * (1.0 + values * (1.0 - sigmoid_v))


def layer_normalize(values):
    average = jnp.mean(values, axis=-1, keepdims=True)
    centred = values - average
    inverse = lax.rsqrt(jnp.mean(centred * centred, axis=-1, keepdims=True) + EPSILON)
    return (centred * inverse, inverse)


def normalize_back(gradient, normed, inverse):
    first_term = jnp.mean(gradient, axis=-1, keepdims=True)
    second_term = jnp.mean(gradient * normed, axis=-1, keepdims=True)
    return (gradient - first_term - normed * second_term) * inverse


def masked_scores(query_heads, key_heads, query_index, key_index, score_scale):
    scores = (
        jnp.einsum("qhd,khd->hqk", query_heads, key_heads, preferred_element_type=jnp.float32)
        * score_scale
    )
    allowed = (key_index[None, :] <= query_index[:, None])[None]
    weights = jnp.where(allowed, jax.nn.silu(scores), 0.0).astype(jnp.bfloat16)
    return (scores, allowed, weights)


def score_deltas(
    query_heads, key_heads, value_heads, delta_heads, query_index, key_index, score_scale
):
    scores, allowed, weights = masked_scores(
        query_heads, key_heads, query_index, key_index, score_scale
    )
    delta_weights = jnp.einsum(
        "qhd,khd->hqk", delta_heads, value_heads, preferred_element_type=jnp.float32
    )
    delta_scores = jnp.where(allowed, delta_weights * silu_slope(scores) * score_scale, 0.0).astype(
        jnp.bfloat16
    )
    return (weights, delta_scores)


def local(
    row_owner,
    slot_row,
    hot_table,
    cold_table,
    cold_projection,
    joined_weight,
    output_weight,
    cotangent,
):
    tokens_here = slot_row.shape[0]
    model_width = output_weight.shape[0]
    hot_count = hot_table.shape[0]
    cold_count = cold_table.shape[0]
    cold_width = cold_table.shape[1]
    head_count = HEADS
    head_size = model_width // head_count
    score_scale = 1.0 / math.sqrt(head_size)
    devices = lax.axis_size(("dp", "cp"))
    group_index = lax.axis_index("cp")
    capacity = 2 * tokens_here // devices + 2
    owners = row_owner[:, 0]
    is_hot = slot_row < hot_count
    is_cold = jnp.logical_not(is_hot)
    onehot = (owners[:, None] == jnp.arange(devices, dtype=jnp.int32)[None, :]).astype(jnp.bfloat16)
    lower_mask = (jnp.arange(tokens_here)[:, None] > jnp.arange(tokens_here)[None, :]).astype(
        jnp.bfloat16
    )
    earlier = jnp.dot(lower_mask, onehot, preferred_element_type=jnp.float32)
    rank_in_owner = jnp.sum(earlier * onehot.astype(jnp.float32), axis=1).astype(jnp.int32)
    slot_index = owners * capacity + rank_in_owner
    requests = (
        jnp.full((devices * capacity,), -1, jnp.int32)
        .at[slot_index]
        .set(slot_row)
        .reshape(devices, capacity)
    )
    asked_rows = lax.all_to_all(requests, ("dp", "cp"), split_axis=0, concat_axis=0, tiled=True)
    valid_hot = (asked_rows >= 0) & (asked_rows < hot_count)
    valid_cold = asked_rows >= hot_count
    nothing = jnp.zeros((), jnp.bfloat16)
    hot_pick = jnp.where(
        valid_hot[..., None], hot_table[jnp.clip(asked_rows, 0, hot_count - 1)], nothing
    )
    cold_pick = jnp.where(
        valid_cold[..., None],
        cold_table[jnp.clip(asked_rows - hot_count, 0, cold_count - 1)],
        nothing,
    )
    padded = jnp.pad(cold_pick, ((0, 0), (0, 0), (0, model_width - cold_width)))
    packed = jnp.where(valid_hot[..., None], hot_pick, padded)
    returned = lax.all_to_all(packed, ("dp", "cp"), split_axis=0, concat_axis=0, tiled=True)
    fetched = returned.reshape(devices * capacity, model_width)[slot_index]
    cold_vector = fetched[:, :cold_width]
    cold_embed = jnp.dot(cold_vector, cold_projection, preferred_element_type=jnp.float32)
    embedded = jnp.where(is_hot[:, None], fetched.astype(jnp.float32), cold_embed)
    normed, inverse = layer_normalize(embedded)
    normed_low = normed.astype(jnp.bfloat16)
    hidden = jnp.dot(normed_low, joined_weight, preferred_element_type=jnp.float32)
    active = jax.nn.silu(hidden).astype(jnp.bfloat16)
    gate_part = active[:, :model_width]
    attention_rows = active[:, model_width:]
    segments = [(0, tokens_here, group_index * tokens_here)]
    value_rows = attention_rows[:, :model_width]
    query_rows = attention_rows[:, model_width : 2 * model_width]
    key_rows = attention_rows[:, 2 * model_width :]
    local_index = jnp.concatenate(
        [first + jnp.arange(count, dtype=jnp.int32) for start, count, first in segments]
    )
    all_keys, all_values = side_by_side((key_rows, value_rows), "cp", 0, 1)
    length = all_keys.shape[0]
    key_span = min(length, block_limit)
    heads_shape = (tokens_here, head_count, head_size)
    query_heads = query_rows.reshape(heads_shape)

    def key_slices(counter):
        offset = counter * key_span
        key_block = lax.dynamic_slice_in_dim(all_keys, offset, key_span, 0).reshape(
            key_span, head_count, head_size
        )
        value_block = lax.dynamic_slice_in_dim(all_values, offset, key_span, 0).reshape(
            key_span, head_count, head_size
        )
        key_index = offset + jnp.arange(key_span, dtype=jnp.int32)
        return (offset, key_block, value_block, key_index)

    def blocks_needed(first, count):
        return (first + count + key_span - 1) // key_span

    start, count, first = segments[0]
    segment_queries = query_heads
    segment_index = first + jnp.arange(count, dtype=jnp.int32)

    def forward_step(
        counter, running, segment_queries=segment_queries, segment_index=segment_index
    ):
        offset, key_block, value_block, key_index = key_slices(counter)
        scores, allowed, weights = masked_scores(
            segment_queries, key_block, segment_index, key_index, score_scale
        )
        return running + jnp.einsum(
            "hqk,khd->qhd", weights, value_block, preferred_element_type=jnp.float32
        )

    empty_part = jnp.zeros((count, head_count, head_size), jnp.float32)
    attended_parts = lax.fori_loop(0, blocks_needed(first, count), forward_step, empty_part)
    attended = attended_parts.reshape(tokens_here, model_width)
    mixed, inverse_mix = layer_normalize(attended)
    gated = (mixed * gate_part.astype(jnp.float32)).astype(jnp.bfloat16)
    branch = jnp.dot(gated, output_weight, preferred_element_type=jnp.float32)
    layer_out = (embedded + branch).astype(jnp.bfloat16)
    delta_gated = jnp.dot(cotangent, output_weight.T, preferred_element_type=jnp.float32)
    delta_gate = delta_gated * mixed
    delta_attended = normalize_back(
        delta_gated * gate_part.astype(jnp.float32), mixed, inverse_mix
    ).astype(jnp.bfloat16)
    delta_heads = delta_attended.reshape(heads_shape)
    empty_heads = jnp.zeros(heads_shape, jnp.float32)
    start, count, first = segments[0]
    segment_queries = query_heads
    segment_deltas = delta_heads
    segment_index = first + jnp.arange(count, dtype=jnp.int32)

    def query_step(
        counter,
        running,
        segment_queries=segment_queries,
        segment_deltas=segment_deltas,
        segment_index=segment_index,
    ):
        offset, key_block, value_block, key_index = key_slices(counter)
        weights, delta_scores = score_deltas(
            segment_queries,
            key_block,
            value_block,
            segment_deltas,
            segment_index,
            key_index,
            score_scale,
        )
        return running + jnp.einsum(
            "hqk,khd->qhd", delta_scores, key_block, preferred_element_type=jnp.float32
        )

    empty_part = jnp.zeros((count, head_count, head_size), jnp.float32)
    query_parts = lax.fori_loop(0, blocks_needed(first, count), query_step, empty_part)
    key_heads = key_rows.reshape(heads_shape)
    value_heads = value_rows.reshape(heads_shape)
    key_lowest = jnp.min(local_index)
    query_piece, delta_piece = side_by_side((query_rows, delta_attended), "cp", 0, 1)
    row_count = query_piece.shape[0]
    sub_rows = math.gcd(row_count, block_limit)

    def inner_step(counter, partial_sums):
        start_row = counter * sub_rows
        query_block = lax.dynamic_slice_in_dim(query_piece, start_row, sub_rows, 0).reshape(
            sub_rows, head_count, head_size
        )
        delta_block = lax.dynamic_slice_in_dim(delta_piece, start_row, sub_rows, 0).reshape(
            sub_rows, head_count, head_size
        )
        query_index = start_row + jnp.arange(sub_rows, dtype=jnp.int32)

        def accumulate(sums_in):
            weights, delta_scores = score_deltas(
                query_block,
                key_heads,
                value_heads,
                delta_block,
                query_index,
                local_index,
                score_scale,
            )
            key_sum = sums_in[0] + jnp.einsum(
                "hqk,qhd->khd", delta_scores, query_block, preferred_element_type=jnp.float32
            )
            value_sum = sums_in[1] + jnp.einsum(
                "hqk,qhd->khd", weights, delta_block, preferred_element_type=jnp.float32
            )
            return (key_sum, value_sum)

        return lax.cond(
            jnp.max(query_index) >= key_lowest, accumulate, lambda sums_in: sums_in, partial_sums
        )

    key_sum, value_sum = lax.fori_loop(
        0, row_count // sub_rows, inner_step, (empty_heads, empty_heads)
    )
    delta_key = key_sum.reshape(tokens_here, model_width)
    delta_value = value_sum.reshape(tokens_here, model_width)
    attention_grads = jnp.concatenate(
        [delta_value, query_parts.reshape(tokens_here, model_width), delta_key], axis=1
    )
    delta_active = jnp.concatenate([delta_gate, attention_grads], axis=1)
    delta_hidden = (delta_active * silu_slope(hidden)).astype(jnp.bfloat16)
    delta_normed = jnp.dot(delta_hidden, joined_weight.T, preferred_element_type=jnp.float32)
    delta_embed = normalize_back(delta_normed, normed, inverse) + cotangent.astype(jnp.float32)
    cold_float = jnp.where(is_cold[:, None], cold_vector.astype(jnp.float32), 0.0)
    joined_local = jnp.dot(normed_low.T, delta_hidden, preferred_element_type=jnp.float32)
    output_local = jnp.dot(gated.T, cotangent, preferred_element_type=jnp.float32)
    projection_local = jnp.dot(cold_float.T, delta_embed, precision=lax.Precision.HIGHEST)
    joined_sum, output_sum, projection_sum = (
        lax.psum(joined_local.astype(jnp.bfloat16), ("dp", "cp")).astype(jnp.float32),
        lax.psum(output_local.astype(jnp.bfloat16), ("dp", "cp")).astype(jnp.float32),
        lax.psum(projection_local.astype(jnp.bfloat16), ("dp", "cp")).astype(jnp.float32),
    )
    norm_scale = (tokens_here * devices) ** (-0.5)
    cold_event = jnp.where(
        is_cold[:, None],
        jnp.dot(
            delta_embed, cold_projection.astype(jnp.float32).T, precision=lax.Precision.HIGHEST
        ),
        0.0,
    )
    hot_event = jnp.where(is_hot[:, None], delta_embed, 0.0)
    padded_event = jnp.pad(cold_event, ((0, 0), (0, model_width - cold_width)))
    packed_event = jnp.where(is_hot[:, None], hot_event, padded_event)
    buffer = (
        jnp.zeros((devices * capacity, model_width), jnp.float32)
        .at[slot_index]
        .set(packed_event)
        .reshape(devices, capacity, model_width)
    )
    arrived = several_exchanges(buffer.astype(jnp.bfloat16), ("dp", "cp"), 2, 0, 0).astype(
        buffer.dtype
    )
    cold_arrived = arrived[..., :cold_width]
    hot_target = jnp.where(valid_hot, asked_rows, hot_count).reshape(-1)
    cold_target = jnp.where(valid_cold, asked_rows - hot_count, cold_count).reshape(-1)
    hot_gradient = (
        jnp.zeros((hot_count, model_width), jnp.float32)
        .at[hot_target]
        .add(arrived.reshape(-1, model_width), mode="drop")
    )
    cold_gradient = (
        jnp.zeros((cold_count, cold_width), jnp.float32)
        .at[cold_target]
        .add(cold_arrived.reshape(-1, cold_width), mode="drop")
    )
    return (
        layer_out,
        hot_gradient,
        cold_gradient,
        projection_sum * norm_scale,
        joined_sum * norm_scale,
        output_sum * norm_scale,
    )


def solution(mesh):
    placed = (
        P(("dp", "cp"), None),
        P(("dp", "cp")),
        P(("dp", "cp"), None),
        P(("dp", "cp"), None),
        P(),
        P(),
        P(),
        P(("dp", "cp"), None),
    )
    return jax.shard_map(
        local,
        mesh=mesh,
        in_specs=placed,
        out_specs=(
            P(("dp", "cp"), None),
            P(("dp", "cp"), None),
            P(("dp", "cp"), None),
            P(),
            P(),
            P(),
        ),
        check_vma=False,
    )
```

profile of v0, /device:TPU:1, one launch (start us, length us, event | category | flops | bytes accessed | tf_op | source)
XLA Modules:
  0.0 425.6 jit_solution(10073714078295284084)
XLA Ops:
  10.1 20.9 %all_to_all.27 = s32[128,1,4]{2,1,0:T(1,128)S(1)} all-to-all(s32[128,1,4]{2,1,0:T(1,128)S(1)} %bitcast.196), channel_id=1, replica_groups=mesh['dp'=8,'cp'=16] {'dp','cp'}, dimensions={0} | all-to-all | bytes 4096 | tf_op jit(solution)/shard_map/all_to_all | solution.py:131
  31.7 3.1 gather_fusion
  39.7 4.5 %all-to-all-start.1 = ((bf16[128,4,512]{2,1,0:T(4,128)(2,1)}), bf16[128,4,512]{2,1,0:T(4,128)(2,1)S(1)}, u32[]{:S(2)}, u32[]{:S(2)}) async-start(bf16[128,4,512]{2,1,0:T(4,128)(2,1)} %pad_select_fusion), calls=%async_computation.1 | async-start | bytes 1048576 | tf_op jit(solution)/shard_map/all_to_all | solution.py:145
  44.9 12.7 %all-to-all-done.1 = bf16[128,4,512]{2,1,0:T(4,128)(2,1)S(1)} async-done(((bf16[128,4,512]{2,1,0:T(4,128)(2,1)}), bf16[128,4,512]{2,1,0:T(4,128)(2,1)S(1)}, u32[]{:S(2)}, u32[]{:S(2)}) %all-to-all-start.1) | async-done | bytes 524320 | tf_op jit(solution)/shard_map/all_to_all | solution.py:145
  63.7 45.9 %all-gather.3.cloned.1.call-done = bf16[2048,1024]{1,0:T(8,128)(2,1)} async-done(((bf16[128,1024]{1,0:T(8,128)(2,1)}), bf16[2048,1024]{1,0:T(8,128)(2,1)}) %all-gather.3.cloned.1.call-update) | async-done | bytes 4194320 | tf_op jit(solution)/shard_map/all_gather | solution.py:21
  109.6 4.5 %fusion.84 = (bf16[2048,512]{1,0:T(8,128)(2,1)}, bf16[2048,512]{1,0:T(8,128)(2,1)}) fusion(bf16[2048,1024]{1,0:T(8,128)(2,1)} %all-gather.3.cloned.1.call-done), kind=kLoop, calls=%fused_computation.161 | loop fusion | bytes 8388608 | tf_op jit(solution)/shard_map/split | solution.py:21
  114.2 4.0 copy.83
  118.1 4.0 copy.84
  122.8 6.8 %while.38 = (s32[]{:T(128)}, f32[128,8,64]{0,2,1:T(8,128)}, s32[]{:T(128)}, bf16[2048,512]{0,1:T(8,128)(2,1)}, bf16[2048,512]{0,1:T(8,128)(2,1)}, /*index=5*/bf1...) while((s32[]{:T(128)}, f32[128,8,64]{0,2,1:T(8,128)}, ...), condition=%wide.region_5.6_spmd.clone, body=%wide.region_4.5_spmd.clone.sunk | while | flops 275973248 | bytes 7218343 | solution.py:199
  125.7 3.9 fusion.132
  139.3 11.6 %while.40 = (s32[]{:T(128)}, f32[128,8,64]{0,2,1:T(8,128)}, s32[]{:T(128)}, bf16[2048,512]{0,1:T(8,128)(2,1)}, bf16[2048,512]{0,1:T(8,128)(2,1)}, /*index=5*/bf1...) while((s32[]{:T(128)}, f32[128,8,64]{0,2,1:T(8,128)}, ...), condition=%wide.region_17.18_spmd.clone, body=%wide.region_16.17_spmd.clone.sunk | while | flops 415433856 | bytes 16786608 | solution.py:239
  145.0 5.8 %fusion.139 = f32[128,8,64]{0,2,1:T(8,128)} fusion(f32[128,8,64]{0,2,1:T(8,128)} %get-tuple-element.860, bf16[1024,8,64]{0,2,1:T(8,128)(2,1)S(1)} %bitcast.180, f32[8,1024,128]{2,1,0:T(8,128)} %fusion.138, bf16[1024,8,64]{0,2,1:T(8,128)(2,1)} %bitcast.183, bf16[128,8,64]{0,2,1:T(8,128)(2,1)} %get-tuple-element.876, ...), kind=kOutput, calls=%fused_computation.62.clone.1 | convolution fusion | flops 281083904 | bytes 7077888 | tf_op jit(solution)/shard_map/while/body/hqk,khd->qhd/dot_general | solution.py:234
  154.7 41.7 %all-gather.5.cloned.1.call-done = bf16[2048,1024]{1,0:T(8,128)(2,1)} async-done(((bf16[128,1024]{1,0:T(8,128)(2,1)}), bf16[2048,1024]{1,0:T(8,128)(2,1)}) %all-gather.5.cloned.1.call-update) | async-done | bytes 4194320 | tf_op jit(solution)/shard_map/all_gather | solution.py:21
  196.4 4.5 %fusion.83 = (bf16[2048,512]{1,0:T(8,128)(2,1)}, bf16[2048,512]{1,0:T(8,128)(2,1)}) fusion(bf16[2048,1024]{1,0:T(8,128)(2,1)} %all-gather.5.cloned.1.call-done), kind=kLoop, calls=%fused_computation.160 | loop fusion | bytes 8388608 | tf_op jit(solution)/shard_map/split | solution.py:21
  200.9 4.0 copy.88
  204.9 4.0 copy.89
  209.6 39.0 %while.39 = (s32[]{:T(128)}, f32[128,8,64]{0,2,1:T(8,128)S(1)}, f32[128,8,64]{0,2,1:T(8,128)}, s32[]{:T(128)}, bf16[2048,512]{0,1:T(8,128)(2,1)}, /*index=5*/bf1...) while((s32[]{:T(128)}, f32[128,8,64]{0,2,1:T(8,128)S(1)}, ...), condition=%wide.region_15.16_spmd.clone, body=%wide.region_11.15_spmd.clone.sunk | while | flops 557058176 | bytes 24783208 | solution.py:279
  211.5 17.6 %conditional.3 = ((f32[128,8,64]{0,2,1:T(8,128)S(1)}, f32[128,8,64]{0,2,1:T(8,128)})) conditional(s32[]{:T(128)} %convert_element_type.220, (f32[128,8,64]{0,2,1:T(8,128)S(1)}, f32[128,8,64]{0,2,1:T(8,128)}) %tuple.126, (s32[]{:T(128)}, s32[1024]{0:T(1024)S(1)}, s32[]{:T(128)}, bf16[2048,512]{0,1:T(8,128)(2,1)}, bf16[128,8,64]{0,2,1:T(8,128)(2,1)}, ...), branch_computations={%region_13.13_spmd, %region_14.14_spmd} | conditional | flops 557056128 | bytes 24778362 | solution.py:275
  214.9 2.8 fusion.88
  218.6 5.9 %fusion.11 = f32[128,8,64]{0,2,1:T(8,128)} fusion(f32[128,8,64]{0,2,1:T(8,128)} %copy-done.8, bf16[1024,8,64]{0,2,1:T(8,128)(2,1)S(1)} %bitcast.182, f32[8,1024,128]{2,1,0:T(8,128)} %fusion.88, bf16[1024,8,64]{0,2,1:T(8,128)(2,1)} %bitcast.186, bf16[128,8,64]{0,2,1:T(8,128)(2,1)} %get-tuple-element.319, pred[1024,128]{1,0:T(8,128)(4,1)} %broadcast_compare_fusion), kind=kOutput, calls=%fused_computation.18 | convolution fusion | flops 281083904 | bytes 7077888 | tf_op jit(solution)/shard_map/while/body/eval_jaxpr/cond/branch_1_fun/hqk,qhd->khd/dot_general | solution.py:267
  224.4 4.7 %fusion.10 = f32[128,8,64]{0,2,1:T(8,128)} fusion(f32[128,8,64]{0,2,1:T(8,128)} %get-tuple-element.322, bf16[1024,8,64]{0,2,1:T(8,128)(2,1)} %bitcast.187, f32[8,1024,128]{2,1,0:T(8,128)} %fusion.88, pred[1024,128]{1,0:T(8,128)(4,1)} %broadcast_compare_fusion), kind=kOutput, calls=%fused_computation.17 | convolution fusion | flops 141623296 | bytes 5898240 | tf_op jit(solution)/shard_map/while/body/eval_jaxpr/cond/branch_1_fun/hqk,qhd->khd/dot_general | solution.py:270
  231.0 17.6 %conditional.3 = ((f32[128,8,64]{0,2,1:T(8,128)S(1)}, f32[128,8,64]{0,2,1:T(8,128)})) conditional(s32[]{:T(128)} %convert_element_type.220, (f32[128,8,64]{0,2,1:T(8,128)S(1)}, f32[128,8,64]{0,2,1:T(8,128)}) %tuple.126, (s32[]{:T(128)}, s32[1024]{0:T(1024)S(1)}, s32[]{:T(128)}, bf16[2048,512]{0,1:T(8,128)(2,1)}, bf16[128,8,64]{0,2,1:T(8,128)(2,1)}, ...), branch_computations={%region_13.13_spmd, %region_14.14_spmd} | conditional | flops 557056128 | bytes 24778362 | solution.py:275
  238.1 5.9 %fusion.11 = f32[128,8,64]{0,2,1:T(8,128)} fusion(f32[128,8,64]{0,2,1:T(8,128)} %copy-done.8, bf16[1024,8,64]{0,2,1:T(8,128)(2,1)S(1)} %bitcast.182, f32[8,1024,128]{2,1,0:T(8,128)} %fusion.88, bf16[1024,8,64]{0,2,1:T(8,128)(2,1)} %bitcast.186, bf16[128,8,64]{0,2,1:T(8,128)(2,1)} %get-tuple-element.319, pred[1024,128]{1,0:T(8,128)(4,1)} %broadcast_compare_fusion), kind=kOutput, calls=%fused_computation.18 | convolution fusion | flops 281083904 | bytes 7077888 | tf_op jit(solution)/shard_map/while/body/eval_jaxpr/cond/branch_1_fun/hqk,qhd->khd/dot_general | solution.py:267
  243.9 4.7 %fusion.10 = f32[128,8,64]{0,2,1:T(8,128)} fusion(f32[128,8,64]{0,2,1:T(8,128)} %get-tuple-element.322, bf16[1024,8,64]{0,2,1:T(8,128)(2,1)} %bitcast.187, f32[8,1024,128]{2,1,0:T(8,128)} %fusion.88, pred[1024,128]{1,0:T(8,128)(4,1)} %broadcast_compare_fusion), kind=kOutput, calls=%fused_computation.17 | convolution fusion | flops 141623296 | bytes 5898240 | tf_op jit(solution)/shard_map/while/body/eval_jaxpr/cond/branch_1_fun/hqk,qhd->khd/dot_general | solution.py:270
  264.5 7.3 %all-to-all-start.2 = ((bf16[128,1,2,512]{3,2,1,0:T(2,128)(2,1)}), bf16[128,1,2,512]{3,2,1,0:T(2,128)(2,1)S(1)}, u32[]{:S(2)}, u32[]{:S(2)}) async-start(bf16[128,1,2,512]{3,2,1,0:T(2,128)(2,1)} %get-tuple-element.591), calls=%async_computation.2 | async-start | bytes 524288 | tf_op jit(solution)/shard_map/all_to_all | solution.py:47
  274.0 9.4 %all-to-all-done.2 = bf16[128,1,2,512]{3,2,1,0:T(2,128)(2,1)S(1)} async-done(((bf16[128,1,2,512]{3,2,1,0:T(2,128)(2,1)}), bf16[128,1,2,512]{3,2,1,0:T(2,128)(2,1)S(1)}, u32[]{:S(2)}, u32[]{:S(2)}) %all-to-all-start.2) | async-done | bytes 262176 | tf_op jit(solution)/shard_map/all_to_all | solution.py:47
  283.5 5.3 %all-to-all-start.3 = ((bf16[128,1,2,512]{3,2,1,0:T(2,128)(2,1)}), bf16[128,1,2,512]{3,2,1,0:T(2,128)(2,1)}, u32[]{:S(2)}, u32[]{:S(2)}) async-start(bf16[128,1,2,512]{3,2,1,0:T(2,128)(2,1)} %get-tuple-element.592), calls=%async_computation.3 | async-start | bytes 524288 | tf_op jit(solution)/shard_map/all_to_all | solution.py:47
  290.8 8.9 %all-to-all-done.3 = bf16[128,1,2,512]{3,2,1,0:T(2,128)(2,1)} async-done(((bf16[128,1,2,512]{3,2,1,0:T(2,128)(2,1)}), bf16[128,1,2,512]{3,2,1,0:T(2,128)(2,1)}, u32[]{:S(2)}, u32[]{:S(2)}) %all-to-all-start.3) | async-done | bytes 262176 | tf_op jit(solution)/shard_map/all_to_all | solution.py:47
  304.4 5.2 %scatter_custom_fusion.2 = f32[512,512]{1,0:T(8,128)} fusion(s32[512]{0:T(512)S(1)} %bitcast.200, f32[512,512]{1,0:T(8,128)} %reshape.449, f32[]{:T(128)} %constant.155.clone.1), kind=kCustom, calls=%fused_computation.89 | custom fusion | flops 262144 | bytes 1049088 | tf_op jit(solution)/shard_map/scatter-add | solution.py:326
  309.6 3.2 scatter_custom_fusion.3
  312.9 100.2 %all-reduce.5.cloned.1.call-done = (bf16[128,512]{1,0:T(8,128)(2,1)}, bf16[512,2048]{1,0:T(8,128)(2,1)}, bf16[512,512]{1,0:T(8,128)(2,1)}) async-done(((bf16[128,512]{1,0:T(8,128)(2,1)}, bf16[512,2048]{1,0:T(8,128)(2,1)}, bf16[512,512]{1,0:T(8,128)(2,1)}), (bf16[128,512]{1,0:T(8,128)(2,1)}, bf16[512,2048]{1,0:T(8,128)(2,1)}, bf16[512,512]{1,0:T(8,128)(2,1)})) %all-reduce.5.cloned.1.call-update) | async-done | bytes 2752528 | tf_op jit(solution)/shard_map/psum | solution.py:298
  413.0 4.2 convert_multiply_fusion
  (160 shorter events, 77.7 us)
Async XLA Ops:
  7.2 52.4 %copy-start = (bf16[512,2048]{1,0:T(8,128)(2,1)S(1)}, bf16[512,2048]{1,0:T(8,128)(2,1)}, u32[]{:S(2)}) copy-start(bf16[512,2048]{1,0:T(8,128)(2,1)} %param.21) | copy-start | bytes 6291460
  7.2 28.7 %copy-start.4 = (bf16[2048,128]{1,0:T(8,128)(2,1)S(1)}, bf16[2048,128]{1,0:T(8,128)(2,1)}, u32[]{:S(2)}) copy-start(bf16[2048,128]{1,0:T(8,128)(2,1)} %param.19) | copy-start | bytes 1572868
  8.9 35.4 %copy-start.26 = (s32[128]{0:T(128)}, s32[128]{0:T(128)S(1)}, u32[]{:S(2)}) copy-start(s32[128]{0:T(128)S(1)} %fusion.76) | copy-start | bytes 1540
  31.7 12.6 %copy-start.27 = (s32[128]{0:T(128)S(1)}, s32[128]{0:T(128)}, u32[]{:S(2)}) copy-start(s32[128]{0:T(128)} %param.17) | copy-start | bytes 1540
  34.8 23.7 %copy-start.15 = (bf16[128,512]{1,0:T(8,128)(2,1)S(1)}, bf16[128,512]{1,0:T(8,128)(2,1)}, u32[]{:S(2)}) copy-start(bf16[128,512]{1,0:T(8,128)(2,1)} %param.20) | copy-start | bytes 393220
  39.7 17.9 %all-to-all-start.1 = ((bf16[128,4,512]{2,1,0:T(4,128)(2,1)}), bf16[128,4,512]{2,1,0:T(4,128)(2,1)S(1)}, u32[]{:S(2)}, u32[]{:S(2)}) async-start(bf16[128,4,512]{2,1,0:T(4,128)(2,1)} %pad_select_fusion), calls=%async_computation.1 | async-start | bytes 1048576 | tf_op jit(solution)/shard_map/all_to_all | solution.py:145
  44.2 65.4 %all-gather.3.cloned.1.call-start = ((), (), s32[]{:S(2)}) async-start(), calls=%async_computation.4 | async-start | bytes 4456448 | tf_op jit(solution)/shard_map/all_gather | solution.py:21
  44.9 16.2 %copy-start.23 = (pred[128]{0:T(512)(128)(4,1)}, pred[128]{0:T(512)(128)(4,1)S(1)}, u32[]{:S(2)}) copy-start(pred[128]{0:T(512)(128)(4,1)S(1)} %get-tuple-element.603) | copy-start | bytes 388
  58.8 0.7 copy-start.1
  58.8 2.2 copy-start.19
  59.5 1.5 copy-start.21
  61.0 53.1 %copy-start.12 = (bf16[128,2048]{1,0:T(8,128)(2,1)}, bf16[128,2048]{1,0:T(8,128)(2,1)S(1)}, u32[]{:S(2)}) copy-start(bf16[128,2048]{1,0:T(8,128)(2,1)S(1)} %get-tuple-element.606) | copy-start | bytes 1572868
  61.1 53.1 %copy-start.6 = (bf16[128,512]{1,0:T(8,128)(2,1)}, bf16[128,512]{1,0:T(8,128)(2,1)S(1)}, u32[]{:S(2)}) copy-start(bf16[128,512]{1,0:T(8,128)(2,1)S(1)} %get-tuple-element.593) | copy-start | bytes 393220
  62.0 134.4 %all-gather.5.cloned.1.call-start = ((), (), s32[]{:S(2)}) async-start(), calls=%async_computation.5 | async-start | bytes 4456448 | tf_op jit(solution)/shard_map/all_gather | solution.py:21
  138.5 274.5 %all-reduce.5.cloned.1.call-start = ((), (), s32[]{:S(2)}) async-start(), calls=%async_computation.6 | async-start | bytes 5505024 | tf_op jit(solution)/shard_map/psum | solution.py:298
  209.6 43.7 %copy-start.2 = (f32[128,512]{1,0:T(8,128)S(1)}, f32[128,512]{1,0:T(8,128)}, u32[]{:S(2)}) copy-start(f32[128,512]{1,0:T(8,128)} %copy-done.1) | copy-start | bytes 786436
  209.6 43.7 %copy-start.20 = (f32[128]{0:T(128)S(1)}, f32[128]{0:T(128)}, u32[]{:S(2)}) copy-start(f32[128]{0:T(128)} %copy-done.19) | copy-start | bytes 1540
  209.6 43.7 %copy-start.22 = (f32[128]{0:T(128)S(1)}, f32[128]{0:T(128)}, u32[]{:S(2)}) copy-start(f32[128]{0:T(128)} %copy-done.21) | copy-start | bytes 1540
  211.5 0.7 copy-start.8
  224.4 4.7 %copy-start.9 = (f32[128,8,64]{0,2,1:T(8,128)S(1)}, f32[128,8,64]{0,2,1:T(8,128)}, u32[]{:S(2)}) copy-start(f32[128,8,64]{0,2,1:T(8,128)} %fusion.11) | copy-start | bytes 786436 | tf_op jit(solution)/shard_map/while/body/eval_jaxpr/cond
  243.9 4.7 %copy-start.9 = (f32[128,8,64]{0,2,1:T(8,128)S(1)}, f32[128,8,64]{0,2,1:T(8,128)}, u32[]{:S(2)}) copy-start(f32[128,8,64]{0,2,1:T(8,128)} %fusion.11) | copy-start | bytes 786436 | tf_op jit(solution)/shard_map/while/body/eval_jaxpr/cond
  251.5 4.9 %copy-start.5 = (bf16[128,512]{1,0:T(8,128)(2,1)S(1)}, bf16[128,512]{1,0:T(8,128)(2,1)}, u32[]{:S(2)}) copy-start(bf16[128,512]{1,0:T(8,128)(2,1)} %param.23) | copy-start | bytes 393220
  251.5 5.1 %copy-start.25 = (pred[128]{0:T(512)(128)(4,1)S(1)}, pred[128]{0:T(512)(128)(4,1)}, u32[]{:S(2)}) copy-start(pred[128]{0:T(512)(128)(4,1)} %get-tuple-element.602) | copy-start | bytes 388
  255.5 3.1 copy-start.16
  255.5 4.0 copy-start.24
  256.6 2.0 copy-start.3
  258.5 30.3 %copy-start.7 = (bf16[128,512]{1,0:T(8,128)(2,1)S(1)}, bf16[128,512]{1,0:T(8,128)(2,1)}, u32[]{:S(2)}) copy-start(bf16[128,512]{1,0:T(8,128)(2,1)} %get-tuple-element.587) | copy-start | bytes 393220
  264.5 19.0 %all-to-all-start.2 = ((bf16[128,1,2,512]{3,2,1,0:T(2,128)(2,1)}), bf16[128,1,2,512]{3,2,1,0:T(2,128)(2,1)S(1)}, u32[]{:S(2)}, u32[]{:S(2)}) async-start(bf16[128,1,2,512]{3,2,1,0:T(2,128)(2,1)} %get-tuple-element.591), calls=%async_computation.2 | async-start | bytes 524288 | tf_op jit(solution)/shard_map/all_to_all | solution.py:47
  283.5 7.3 %copy-start.11 = (bf16[128,1,2,512]{3,2,1,0:T(2,128)(2,1)}, bf16[128,1,2,512]{3,2,1,0:T(2,128)(2,1)S(1)}, u32[]{:S(2)}) copy-start(bf16[128,1,2,512]{3,2,1,0:T(2,128)(2,1)S(1)} %all-to-all-done.2) | copy-start | bytes 786436
  283.5 16.2 %all-to-all-start.3 = ((bf16[128,1,2,512]{3,2,1,0:T(2,128)(2,1)}), bf16[128,1,2,512]{3,2,1,0:T(2,128)(2,1)}, u32[]{:S(2)}, u32[]{:S(2)}) async-start(bf16[128,1,2,512]{3,2,1,0:T(2,128)(2,1)} %get-tuple-element.592), calls=%async_computation.3 | async-start | bytes 524288 | tf_op jit(solution)/shard_map/all_to_all | solution.py:47
  413.0 4.2 copy-start.14
  413.0 5.3 %copy-start.18 = (bf16[128,512]{1,0:T(8,128)(2,1)S(1)}, bf16[128,512]{1,0:T(8,128)(2,1)}, u32[]{:S(2)}) copy-start(bf16[128,512]{1,0:T(8,128)(2,1)} %get-tuple-element.571) | copy-start | bytes 393220
  (4 other events, 2.8 us)
Sparse Core Ops, SparseCore 0:
  62.1 47.4 all-gather.2
  138.6 57.7 all-gather.4
  258.7 154.2 all-reduce.4
where the time goes:
time: 427 us; the launch traced here: 426 us
  waiting for transfers between devices  219 us (51%)
  local copies, waits for them, and re-layouts  60.9 us (14%)
  matrix products  53.4 us (13%)
  other arithmetic  37.6 us (9%)
  blocking collectives  20.9 us (5%)
  starting transfers between devices  17.2 us (4%)
  between operations  14.2 us (3%)
    psum x1, waiting for transfers between devices, local(): lax.psum(projection_local.astype(jnp.bfloat16), ('dp', 'cp'))  100 us
    all_gather x2, waiting for transfers between devices, side_by_side(): lax.all_gather(both, axis, axis=dim, tiled=True)  87.6 us
    all_to_all x1, blocking collectives, local(): lax.all_to_all(requests, ('dp', 'cp'), split_axis=0, concat_axis=0, tiled...  20.9 us
    all_to_all x2, waiting for transfers between devices, several_exchanges(): lax.all_to_all(piece, axis, split_axis=0, concat_axis=0, tiled=True)  18.4 us
    unnamed x56, local copies, waits for them, and re-layouts  17.1 us
    all_to_all x1, waiting for transfers between devices, local(): lax.all_to_all(packed, ('dp', 'cp'), split_axis=0, concat_axis=0, tiled=T...  12.7 us
    all_to_all x2, starting transfers between devices, several_exchanges(): lax.all_to_all(piece, axis, split_axis=0, concat_axis=0, tiled=True)  12.6 us
    dot_general x2, matrix products, accumulate(): jnp.einsum('hqk,qhd->khd', delta_scores, query_block, preferred_element_t...  11.7 us
  transfers between devices with their start and end apart: 6, of which 6 were waited for; matrix products, arithmetic and copies ran while one was open for 10% of the time, Pallas kernels for 0%

commit v1 on v0

v1 whole, which is shorter than its diff:
```python
import math

import jax
import jax.numpy as jnp
from jax import lax
from jax.experimental import pallas as pl
from jax.experimental.pallas import tpu as pltpu
from jax.sharding import PartitionSpec as P

MESH = pl.DeviceIdType.MESH
BF = jnp.bfloat16
F32 = jnp.float32
I32 = jnp.int32
EPSILON = 1e-05

D = 512
HEADS = 8
HEAD = 64
TOK = 128
CAP = 4
HOT = 512
COLD = 2048
COLD_W = 128
N_DP = 8
N_CP = 16
DEVICES = N_DP * N_CP
SLOT = 16
SLOTS = DEVICES * SLOT
SHIFT = 4096
CHUNK = 256
PAIRS = HEADS * (HEADS + 1) // 2
W_ROWS = 4 * D + D + COLD_W
HALF_ROWS = W_ROWS // 2
COLOR_ROWS = HALF_ROWS // 3
PART_ROWS = COLOR_ROWS // 4


def nn(a, b):
    return jnp.dot(a, b, preferred_element_type=F32)


def nt(a, b, precision=None):
    return lax.dot_general(
        a, b, (((1,), (1,)), ((), ())), preferred_element_type=F32, precision=precision
    )


def sigmoid(v):
    return 0.5 * jnp.tanh(0.5 * v) + 0.5


def silu_slope(v):
    sig = sigmoid(v)
    return sig + v * sig * (1.0 - sig)


def iota(shape, dim):
    return lax.broadcasted_iota(I32, shape, dim)


def turned(v):
    return v.astype(F32).T


def column_norm(v):
    average = jnp.mean(v, axis=0, keepdims=True)
    centred = v - average
    inverse = lax.rsqrt(jnp.mean(centred * centred, axis=0, keepdims=True) + EPSILON)
    return centred * inverse, inverse


def column_norm_back(g, y, inverse):
    first = jnp.mean(g, axis=0, keepdims=True)
    second = jnp.mean(g * y, axis=0, keepdims=True)
    return (g - first - y * second) * inverse


def step_kernel(
    code_col, code_row, hot, cold, proj, joined, wout, cot,
    layer_out, rows_out, req_out, sums_out,
    ids_all, pick32, pick16, row_in, emb_nat, normed_t, inv_ref, cold_t, joined_t,
    hidden_t, active_t, dgated_t, cot_t, slots_1h,
    k_in, v_in, q_in, w_keep, slope_keep, att_out, att_in, da_out, da_in,
    dq_acc, dq_out, dk_out, dv_out, dq_in, dk_in, dv_in, dh_t, pack_ref, grad_out, grad_in,
    rows_buf, w_ref, r0, u1, r1, u2, r2, r3, g2, total,
    send, recv, ar_send, ar_recv, out_sem,
):
    dp, cp = lax.axis_index("dp"), lax.axis_index("cp")
    me = dp * N_CP + cp
    z, core, x, y = dp // 2, dp % 2, cp // 4, cp % 4
    head = cp // 2
    half = ((cp + 1) // 2) % 2

    def far(k):
        pz, pc = (z + k // 32) % 4, (core + (k // 16) % 2) % 2
        px, py = (x + (k // 4) % 4) % 4, (y + k % 4) % 4
        return pz * 2 + pc, px * 4 + py

    def remote(src, dst, send_sem, recv_sem, to):
        return pltpu.make_async_remote_copy(
            src_ref=src, dst_ref=dst, send_sem=send_sem, recv_sem=recv_sem,
            device_id=to, device_id_type=MESH,
        )

    def wait_sent(ref, i):
        remote(ref, ref, send.at[i], recv.at[i], (dp, cp)).wait_send()

    def wait_got(ref, i):
        remote(ref, ref, send.at[i], recv.at[i], (dp, cp)).wait_recv()

    def rows64(h):
        return pl.ds(pl.multiple_of(h * HEAD, HEAD), HEAD)

    def tile(o):
        return pl.ds(pl.multiple_of(o * SLOT, SLOT), SLOT)

    barrier = pltpu.get_barrier_semaphore()

    def greet(k, carry):
        pl.semaphore_signal(barrier, inc=1, device_id=far(k), device_id_type=MESH)
        return carry

    lax.fori_loop(1, DEVICES, greet, 0)
    pl.semaphore_wait(barrier, DEVICES - 1)

    def send_ids(k, carry):
        remote(code_row, ids_all.at[me], send.at[0], recv.at[0], far(k)).start()
        return carry

    lax.fori_loop(1, DEVICES, send_ids, 0)
    ids_all[pl.ds(me, 1)] = code_row[...].reshape(1, 1, TOK)

    owner_col, slot_col = code_col[...] // SHIFT, code_col[...] % SHIFT
    owner_row, slot_row = code_row[...] // SHIFT, code_row[...] % SHIFT
    same = owner_col == owner_row
    before_row = same & (iota((TOK, TOK), 0) < iota((TOK, TOK), 1))
    rank_row = jnp.sum(jnp.where(before_row, 1, 0), axis=0, keepdims=True)
    before_col = same & (iota((TOK, TOK), 1) < iota((TOK, TOK), 0))
    rank_col = jnp.sum(
        jnp.where(before_col, 1.0, 0.0), axis=1, keepdims=True
    ).astype(I32)
    place_col = owner_col * SLOT + rank_col
    place_row = owner_row * SLOT + rank_row
    for f in range(4):
        slots_1h[:, f * TOK : (f + 1) * TOK] = jnp.where(
            iota((SLOTS, TOK), 0) == place_row + CAP * f, 1.0, 0.0
        ).astype(BF)
    for b in range(4):
        joined_t[b * D : (b + 1) * D, :] = turned(joined[:, b * D : (b + 1) * D]).astype(BF)
    cot_t[...] = turned(cot[...])
    dgated_t[...] = nn(wout[...], cot_t[...].astype(BF))

    wait_got(ids_all.at[pl.ds(0, DEVICES - 1)], 0)
    wait_sent(ids_all.at[pl.ds(0, DEVICES - 1)], 0)

    ids = ids_all[:, 0, :]
    asked = (ids // SHIFT) == me
    slot_plus = ((ids % SHIFT) + 1).astype(F32)
    upper = jnp.where(iota((TOK, TOK), 0) < iota((TOK, TOK), 1), 1.0, 0.0).astype(BF)
    earlier = nn(jnp.where(asked, 1.0, 0.0).astype(BF), upper)
    lane_hot = iota((DEVICES, HOT), 1).astype(F32) + 1.0
    lane_cold = iota((DEVICES, COLD), 1).astype(F32) + (HOT + 1.0)
    asks = []
    for c in range(CAP):
        ask = jnp.where(asked & (earlier == float(c)), slot_plus, 0.0)
        asks.append(ask)
        wanted = jnp.sum(ask, axis=1, keepdims=True)
        hot_rows = nn(jnp.where(lane_hot == wanted, 1.0, 0.0).astype(BF), hot[...])
        cold_rows = nn(jnp.where(lane_cold == wanted, 1.0, 0.0).astype(BF), cold[...])
        for f in range(4):
            piece = hot_rows[:, f * 128 : (f + 1) * 128]
            if f == 0:
                piece = piece + cold_rows
            pick32[pl.ds(CAP * f + c, DEVICES, stride=SLOT), :] = piece
    pick16[...] = pick32[...].astype(BF)

    def send_rows(k, carry):
        to = far(k)
        remote(
            pick16.at[tile(to[0] * N_CP + to[1])], row_in.at[tile(me)], send.at[1], recv.at[1], to
        ).start()
        return carry

    lax.fori_loop(1, DEVICES, send_rows, 0)
    row_in[tile(me), :] = pick16[tile(me), :]
    req_out[...] = jnp.zeros(req_out.shape, I32)
    for c in range(CAP):
        wanted_row = jnp.sum(asks[c].T, axis=0, keepdims=True)
        req_out[c : c + 1, :] = wanted_row.astype(I32) - 1

    wait_got(row_in.at[pl.ds(0, SLOTS - SLOT)], 1)
    wait_sent(row_in.at[pl.ds(0, SLOTS - SLOT)], 1)

    fetched = []
    for f in range(4):
        take = jnp.where(iota((TOK, SLOTS), 1) == place_col + CAP * f, 1.0, 0.0).astype(BF)
        fetched.append(nn(take, row_in[...]))
    cold_vec = fetched[0]
    cold_embed = nn(cold_vec.astype(BF), proj[...])
    hot_col = slot_col < HOT
    embedded = jnp.where(hot_col, jnp.concatenate(fetched, axis=1), cold_embed)
    emb_nat[...] = embedded
    cold_t[...] = jnp.where(slot_row < HOT, 0.0, cold_vec.T)
    normed, inverse = column_norm(embedded.T)
    normed_t[...] = normed
    inv_ref[...] = jnp.broadcast_to(inverse, inv_ref.shape)
    normed_low = normed.astype(BF)
    for b in (3, 1, 2, 0):
        hid = nn(joined_t[b * D : (b + 1) * D, :], normed_low)
        hidden_t[b * D : (b + 1) * D, :] = hid
        active_t[b * D : (b + 1) * D, :] = (hid * sigmoid(hid)).astype(BF)

    def k_rows(h):
        return pl.ds(pl.multiple_of(3 * D + h * HEAD, HEAD), HEAD)

    def v_rows(h):
        return pl.ds(pl.multiple_of(D + h * HEAD, HEAD), HEAD)

    def q_rows(h):
        return pl.ds(pl.multiple_of(2 * D + h * HEAD, HEAD), HEAD)

    def send_kv(j, carry):
        pcp = ((x + j // 4) % 4) * 4 + (y + j % 4) % 4
        remote(active_t.at[k_rows(pcp // 2)], k_in.at[cp], send.at[2], recv.at[2], (dp, pcp)).start()
        remote(active_t.at[v_rows(pcp // 2)], v_in.at[cp], send.at[3], recv.at[3], (dp, pcp)).start()
        return carry

    def same_half(d):
        h = (head + d) % HEADS
        return h, (dp, 2 * h + (half + h) % 2)

    def send_q(d, carry):
        h, to = same_half(d)
        remote(active_t.at[q_rows(h)], q_in.at[head], send.at[4], recv.at[4], to).start()
        return carry

    lax.fori_loop(1, N_CP, send_kv, 0)
    lax.fori_loop(1, HEADS, send_q, 0)
    k_in[pl.ds(cp, 1)] = active_t[k_rows(head), :].reshape(1, HEAD, TOK)
    v_in[pl.ds(cp, 1)] = active_t[v_rows(head), :].reshape(1, HEAD, TOK)
    q_in[pl.ds(head, 1)] = active_t[q_rows(head), :].reshape(1, HEAD, TOK)
    wait_got(k_in.at[pl.ds(0, N_CP - 1)], 2)
    wait_got(v_in.at[pl.ds(0, N_CP - 1)], 3)
    wait_got(q_in.at[pl.ds(0, HEADS - 1)], 4)

    def block_of(i):
        return 4 * (i // 2) + (half if i % 2 == 0 else 3 - half)

    def pair(ref, c):
        return jnp.concatenate([ref[2 * c], ref[2 * c + 1]], axis=1)

    for i in range(HEADS):
        q_nat = turned(q_in[i]).astype(BF)
        total_t = jnp.zeros((HEAD, TOK), F32)
        for c in range(i + 1):
            s = nn(q_nat, pair(k_in, c)) * (1.0 / math.sqrt(HEAD))
            sig = sigmoid(s)
            w = s * sig
            slope = (sig + w * (1.0 - sig)) * (1.0 / math.sqrt(HEAD))
            if c == i:
                ok = (iota((TOK, CHUNK), 1) + c * CHUNK) <= (
                    iota((TOK, CHUNK), 0) + block_of(i) * TOK
                )
                w = jnp.where(ok, w, 0.0)
                slope = jnp.where(ok, slope, 0.0)
            w = w.astype(BF)
            at = i * (i + 1) // 2 + c
            w_keep[at] = w
            slope_keep[at] = slope
            total_t = total_t + nt(pair(v_in, c), w)
        att_out[i] = total_t.astype(BF)

        @pl.when(head != i)
        def _():
            remote(
                att_out.at[i], att_in.at[rows64(head)], send.at[5], recv.at[5], (dp, block_of(i))
            ).start()

    att_in[rows64(head), :] = att_out[pl.ds(head, 1)].reshape(HEAD, TOK)
    wait_got(att_in.at[pl.ds(0, D - HEAD)], 5)

    mixed, inv_mix = column_norm(att_in[...].astype(F32))
    gate = active_t[0:D, :].astype(F32)
    gated = (mixed * gate).astype(BF)
    dgated = dgated_t[...]
    da = column_norm_back(dgated * gate, mixed, inv_mix).astype(BF)
    da_out[...] = da

    def send_da(d, carry):
        h, to = same_half(d)
        remote(da_out.at[rows64(h)], da_in.at[head], send.at[6], recv.at[6], to).start()
        return carry

    lax.fori_loop(1, HEADS, send_da, 0)
    da_in[pl.ds(head, 1)] = da_out[rows64(head), :].reshape(1, HEAD, TOK)

    low = normed_t[...].astype(BF)
    dh_gate = (dgated * mixed * silu_slope(hidden_t[0:D, :])).astype(BF)
    dh_t[0:D, :] = dh_gate
    w_ref[0:D, :] = nt(low, dh_gate).astype(BF)
    w_ref[4 * D : 5 * D, :] = nn(gated, cot[...]).astype(BF)
    branch = nn(turned(gated).astype(BF), wout[...])
    layer_out[...] = (emb_nat[...] + branch).astype(BF)

    wait_got(da_in.at[pl.ds(0, HEADS - 1)], 6)

    dq_acc[...] = jnp.zeros(dq_acc.shape, F32)
    for c in range(HEADS):
        keys, values = pair(k_in, c), pair(v_in, c)
        dk = jnp.zeros((HEAD, CHUNK), F32)
        dv = jnp.zeros((HEAD, CHUNK), F32)
        for i in range(c, HEADS):
            at = i * (i + 1) // 2 + c
            dw = nn(turned(da_in[i]).astype(BF), values)
            ds = (dw * slope_keep[at]).astype(BF)
            dq_acc[i] += nt(keys, ds)
            dk = dk + nn(q_in[i], ds)
            dv = dv + nn(da_in[i], w_keep[at])
        dk, dv = dk.astype(BF), dv.astype(BF)
        dq_out[c] = dq_acc[c].astype(BF)
        for b in range(2):
            kb = 2 * c + b
            dk_out[kb] = dk[:, b * TOK : (b + 1) * TOK]
            dv_out[kb] = dv[:, b * TOK : (b + 1) * TOK]

            @pl.when(cp != kb)
            def _():
                remote(
                    dk_out.at[kb], dk_in.at[half, rows64(head)], send.at[7], recv.at[7], (dp, kb)
                ).start()
                remote(
                    dv_out.at[kb], dv_in.at[half, rows64(head)], send.at[8], recv.at[8], (dp, kb)
                ).start()

        @pl.when(head != c)
        def _():
            remote(
                dq_out.at[c], dq_in.at[rows64(head)], send.at[9], recv.at[9], (dp, block_of(c))
            ).start()

    dq_in[rows64(head), :] = dq_out[pl.ds(head, 1)].reshape(HEAD, TOK)
    dk_in[pl.ds(half, 1), rows64(head), :] = dk_out[pl.ds(cp, 1)]
    dv_in[pl.ds(half, 1), rows64(head), :] = dv_out[pl.ds(cp, 1)]
    wait_got(dk_out.at[pl.ds(0, N_CP - 1)], 7)
    wait_got(dv_out.at[pl.ds(0, N_CP - 1)], 8)
    wait_got(dq_in.at[pl.ds(0, D - HEAD)], 9)

    def column_back(b, grad):
        dh_t[b * D : (b + 1) * D, :] = (
            grad * silu_slope(hidden_t[b * D : (b + 1) * D, :])
        ).astype(BF)

    column_back(1, dv_in[0].astype(F32) + dv_in[1].astype(F32))
    column_back(2, dq_in[...].astype(F32))
    column_back(3, dk_in[0].astype(F32) + dk_in[1].astype(F32))
    dnormed = nn(joined[...], dh_t[...])
    dembed = column_norm_back(dnormed, normed_t[...], inv_ref[0:1, :]) + cot_t[...]

    exact = lax.Precision.HIGHEST
    cold_event = lax.dot_general(
        proj[...].astype(F32), dembed, (((1,), (0,)), ((), ())),
        preferred_element_type=F32, precision=exact,
    )
    is_hot = slot_row < HOT
    for f in range(4):
        piece = dembed[f * 128 : (f + 1) * 128, :]
        pack_ref[:, f * TOK : (f + 1) * TOK] = jnp.where(
            is_hot, piece, cold_event if f == 0 else 0.0
        ).astype(BF)
    grad_out[...] = nt(slots_1h[...], pack_ref[...]).astype(BF)

    def send_grads(k, carry):
        to = far(k)
        remote(
            grad_out.at[tile(to[0] * N_CP + to[1])], grad_in.at[tile(me)],
            send.at[10], recv.at[10], to,
        ).start()
        return carry

    lax.fori_loop(1, DEVICES, send_grads, 0)
    grad_in[tile(me), :] = grad_out[tile(me), :]

    for b in range(1, 4):
        w_ref[b * D : (b + 1) * D, :] = nt(low, dh_t[b * D : (b + 1) * D, :]).astype(BF)
    w_ref[5 * D :, :] = nt(cold_t[...], dembed, exact).astype(BF)

    def half_rows(c):
        return pl.ds(pl.multiple_of(c * HALF_ROWS, 16), HALF_ROWS)

    def ar(src, dst, stage, k, to):
        return remote(src, dst, ar_send.at[stage, k], ar_recv.at[stage, k], to)

    def ar_got(ref, stage, k):
        ar(ref, ref, stage, k, (dp, cp)).wait_recv()

    def ar_sent(ref, stage, k):
        ar(ref, ref, stage, k, (dp, cp)).wait_send()

    sibling = (z * 2 + (1 - core), cp)
    place = (x, y, z)

    def along(dim, d):
        moved = [x, y, z]
        moved[dim] = (moved[dim] + d) % 4
        return moved[dim], (moved[2] * 2 + core, moved[0] * 4 + moved[1])

    ar(w_ref.at[half_rows(1 - core)], r0, 0, 0, sibling).start()
    ar_got(r0, 0, 0)
    u1[...] = (w_ref[half_rows(core), :].astype(F32) + r0[...].astype(F32)).astype(BF)
    for k in range(3):
        for d in range(1, 4):
            a, to = along(k, d)
            rows = pl.ds(pl.multiple_of(k * COLOR_ROWS + a * PART_ROWS, 16), PART_ROWS)
            ar(u1.at[rows], r1.at[k, d - 1], 1, k, to).start()
    for k in range(3):
        ar_got(r1.at[k], 1, k)
        own = pl.ds(pl.multiple_of(k * COLOR_ROWS + place[k] * PART_ROWS, 16), PART_ROWS)
        part = u1[own, :].astype(F32)
        for d in range(3):
            part = part + r1[k, d].astype(F32)
        for b in range(4):
            u2[k, b] = part[:, b * 128 : (b + 1) * 128].astype(BF)
        for d in range(1, 4):
            b, to = along((k + 1) % 3, d)
            ar(u2.at[k, b], r2.at[k, d - 1], 2, k, to).start()
    for k in range(3):
        ar_got(r2.at[k], 2, k)
        b_me, c_me = place[(k + 1) % 3], place[(k + 2) % 3]
        part = u2[k, pl.ds(b_me, 1)].reshape(PART_ROWS, 128).astype(F32)
        for d in range(3):
            part = part + r2[k, d].astype(F32)
        r3[k, pl.ds(c_me, 1)] = part.astype(BF).reshape(1, PART_ROWS, 128)
        for d in range(1, 4):
            _, to = along((k + 2) % 3, d)
            ar(r3.at[k, c_me], r3.at[k, c_me], 3, k, to).start()
    for k in range(3):
        ar_got(r3.at[k, pl.ds(0, 3)], 3, k)
        b_me = place[(k + 1) % 3]
        part = r3[k, 0].astype(F32)
        for d in range(1, 4):
            part = part + r3[k, d].astype(F32)
        g2[k, pl.ds(b_me, 1)] = part.astype(BF).reshape(1, PART_ROWS, 128)
        for d in range(1, 4):
            _, to = along((k + 1) % 3, d)
            ar(g2.at[k, b_me], g2.at[k, b_me], 4, k, to).start()
    for k in range(3):
        ar_got(g2.at[k, pl.ds(0, 3)], 4, k)
        a_me = place[k]
        for d in range(1, 4):
            _, to = along(k, d)
            ar(g2.at[k], total.at[core, k, a_me], 5, k, to).start()
        total[pl.ds(core, 1), k, pl.ds(a_me, 1)] = g2[k].reshape(1, 1, 4, PART_ROWS, 128)

    wait_got(grad_in.at[pl.ds(0, SLOTS - SLOT)], 10)
    pick32[...] = grad_in[...].astype(F32)
    for c in range(CAP):
        for f in range(4):
            rows_buf[c * DEVICES : (c + 1) * DEVICES, f * 128 : (f + 1) * 128] = pick32[
                pl.ds(CAP * f + c, DEVICES, stride=SLOT), :
            ].astype(BF)
    rows_copy = pltpu.make_async_copy(rows_buf, rows_out, out_sem.at[0])
    rows_copy.start()

    for k in range(3):
        ar_got(total.at[0, 0, pl.ds(0, 3)], 5, k)
        ar(total.at[core, k], total.at[core, k], 6, k, sibling).start()
    for k in range(3):
        ar_got(total.at[0, 0], 6, k)
    sums_copy = pltpu.make_async_copy(total, sums_out, out_sem.at[1])
    sums_copy.start()

    wait_sent(k_in.at[pl.ds(0, N_CP - 1)], 2)
    wait_sent(v_in.at[pl.ds(0, N_CP - 1)], 3)
    wait_sent(q_in.at[pl.ds(0, HEADS - 1)], 4)
    wait_sent(att_in.at[pl.ds(0, D - HEAD)], 5)
    wait_sent(da_in.at[pl.ds(0, HEADS - 1)], 6)
    wait_sent(dk_out.at[pl.ds(0, N_CP - 1)], 7)
    wait_sent(dv_out.at[pl.ds(0, N_CP - 1)], 8)
    wait_sent(dq_in.at[pl.ds(0, D - HEAD)], 9)
    wait_sent(grad_in.at[pl.ds(0, SLOTS - SLOT)], 10)
    ar_sent(r0, 0, 0)
    for k in range(3):
        ar_sent(r1.at[k], 1, k)
        ar_sent(r2.at[k], 2, k)
        ar_sent(r3.at[k, pl.ds(0, 3)], 3, k)
        ar_sent(g2.at[k, pl.ds(0, 3)], 4, k)
        ar_sent(total.at[0, 0, pl.ds(0, 3)], 5, k)
        ar_sent(total.at[0, 0], 6, k)
    rows_copy.wait()
    sums_copy.wait()


def finish_kernel(
    rows, req, sums, hot_out, cold_out, proj_out, joined_out, wout_out,
    hot_buf, cold_buf, sum_buf, sem,
):
    picked = rows[...]

    def onehot(rows_here, first):
        index = iota((rows_here, DEVICES), 0) + first
        return jnp.concatenate(
            [jnp.where(index == req[c : c + 1, :], 1.0, 0.0).astype(BF) for c in range(CAP)],
            axis=1,
        )

    copies = []

    def put(src, dst, i):
        copy = pltpu.make_async_copy(src, dst, sem.at[i])
        copy.start()
        copies.append(copy)

    scale = (TOK * DEVICES) ** -0.5
    for core in range(2):
        for k in range(3):
            for a in range(4):
                top = core * HALF_ROWS + k * COLOR_ROWS + a * PART_ROWS
                for b in range(4):
                    sum_buf[top : top + PART_ROWS, b * 128 : (b + 1) * 128] = (
                        sums[core, k, a, b].astype(F32) * scale
                    )
    for b in range(4):
        put(sum_buf.at[pl.ds(b * D, D)], joined_out.at[:, pl.ds(b * D, D)], b)
    put(sum_buf.at[pl.ds(4 * D, D)], wout_out, 4)
    put(sum_buf.at[pl.ds(5 * D, COLD_W)], proj_out, 5)
    hot_buf[...] = nn(onehot(HOT, 0), picked)
    put(hot_buf, hot_out, 6)
    low = picked[:, 0:COLD_W]
    for t in range(4):
        part = pl.ds(t * (COLD // 4), COLD // 4)
        cold_buf[part, :] = nn(onehot(COLD // 4, HOT + t * (COLD // 4)), low)
        put(cold_buf.at[part], cold_out.at[part], 7 + t)
    for copy in copies:
        copy.wait()


def vmem(n):
    return [pl.BlockSpec(memory_space=pltpu.VMEM)] * n


def anywhere(n):
    return [pl.BlockSpec(memory_space=pl.ANY)] * n


def local(row_owner, slot_row, hot, cold, proj, joined, wout, cot):
    code = row_owner[:, 0] * SHIFT + slot_row
    v = pltpu.VMEM
    layer_out, rows, req, sums = pl.pallas_call(
        step_kernel,
        out_shape=(
            jax.ShapeDtypeStruct((TOK, D), BF),
            jax.ShapeDtypeStruct((CAP * DEVICES, D), BF),
            jax.ShapeDtypeStruct((8, DEVICES), I32),
            jax.ShapeDtypeStruct((2, 3, 4, 4, PART_ROWS, 128), BF),
        ),
        in_specs=vmem(8),
        out_specs=tuple(vmem(1) + anywhere(1) + vmem(1) + anywhere(1)),
        scratch_shapes=[
            v((DEVICES, 1, TOK), I32), v((SLOTS, 128), F32), v((SLOTS, 128), BF),
            v((SLOTS, 128), BF), v((TOK, D), F32), v((D, TOK), F32), v((8, TOK), F32),
            v((COLD_W, TOK), F32), v((4 * D, D), BF),
            v((4 * D, TOK), F32), v((4 * D, TOK), BF), v((D, TOK), F32), v((D, TOK), F32),
            v((SLOTS, 4 * TOK), BF),
            v((N_CP, HEAD, TOK), BF), v((N_CP, HEAD, TOK), BF), v((HEADS, HEAD, TOK), BF),
            v((PAIRS, TOK, CHUNK), BF), v((PAIRS, TOK, CHUNK), F32),
            v((HEADS, HEAD, TOK), BF), v((D, TOK), BF), v((D, TOK), BF),
            v((HEADS, HEAD, TOK), BF),
            v((HEADS, HEAD, TOK), F32), v((HEADS, HEAD, TOK), BF),
            v((N_CP, HEAD, TOK), BF), v((N_CP, HEAD, TOK), BF),
            v((D, TOK), BF), v((2, D, TOK), BF), v((2, D, TOK), BF),
            v((4 * D, TOK), BF), v((128, 4 * TOK), BF),
            v((SLOTS, 128), BF), v((SLOTS, 128), BF), v((CAP * DEVICES, D), BF),
            v((W_ROWS, D), BF), v((HALF_ROWS, D), BF), v((HALF_ROWS, D), BF),
            v((3, 3, PART_ROWS, D), BF), v((3, 4, PART_ROWS, 128), BF),
            v((3, 3, PART_ROWS, 128), BF), v((3, 4, PART_ROWS, 128), BF),
            v((3, 4, PART_ROWS, 128), BF), v((2, 3, 4, 4, PART_ROWS, 128), BF),
            pltpu.SemaphoreType.DMA((11,)), pltpu.SemaphoreType.DMA((11,)),
            pltpu.SemaphoreType.DMA((7, 3)), pltpu.SemaphoreType.DMA((7, 3)),
            pltpu.SemaphoreType.DMA((2,)),
        ],
        compiler_params=pltpu.CompilerParams(
            collective_id=0, has_side_effects=True, vmem_limit_bytes=60 << 20
        ),
        name="step",
    )(code[:, None], code[None, :], hot, cold, proj, joined, wout, cot)
    hot_grad, cold_grad, proj_grad, joined_grad, wout_grad = pl.pallas_call(
        finish_kernel,
        out_shape=(
            jax.ShapeDtypeStruct((HOT, D), F32),
            jax.ShapeDtypeStruct((COLD, COLD_W), F32),
            jax.ShapeDtypeStruct((COLD_W, D), F32),
            jax.ShapeDtypeStruct((D, 4 * D), F32),
            jax.ShapeDtypeStruct((D, D), F32),
        ),
        in_specs=vmem(3),
        out_specs=tuple(anywhere(5)),
        scratch_shapes=[
            v((HOT, D), F32), v((COLD, COLD_W), F32), v((W_ROWS, D), F32),
            pltpu.SemaphoreType.DMA((11,)),
        ],
        compiler_params=pltpu.CompilerParams(vmem_limit_bytes=40 << 20),
        name="finish",
    )(rows, req, sums)
    return layer_out, hot_grad, cold_grad, proj_grad, joined_grad, wout_grad


def solution(mesh):
    rows = P(("dp", "cp"), None)
    return jax.shard_map(
        local,
        mesh=mesh,
        in_specs=(rows, P(("dp", "cp")), rows, rows, P(), P(), P(), rows),
        out_specs=(rows, rows, rows, P(), P(), P()),
        check_vma=False,
    )
```

time: 427 us -> 134 us (0.31)
  waiting for transfers between devices: 219 us -> 0 us
  Pallas kernels: 0 us -> 127 us
  local copies, waits for them, and re-layouts: 60.9 us -> 4.89 us
  matrix products: 53.4 us -> 0 us
  other arithmetic: 37.6 us -> 1.19 us
  blocking collectives: 20.9 us -> 0 us
  starting transfers between devices: 17.2 us -> 0 us
  between operations: 14.2 us -> 0.67 us
    pallas_call x0 -> x2, Pallas kernels: none -> 127 us  [the longest x1 122 us: local(): pl.pallas_call(step_kernel, out_shape=(jax.ShapeDtypeStruct((TOK, D), BF)...]
    psum x1 -> x0, waiting for transfers between devices: 100 us -> none  [local(): lax.psum(projection_local.astype(jnp.bfloat16), ('dp', 'cp'))]
    all_gather x2 -> x0, waiting for transfers between devices: 87.6 us -> none  [side_by_side(): lax.all_gather(both, axis, axis=dim, tiled=True)]
    dot_general x19 -> x0, matrix products: 53.4 us -> none  [the longest x2 11.7 us: accumulate(): jnp.einsum('hqk,qhd->khd', delta_scores, query_block, preferred_element_t...]
    all_to_all x3 -> x0, waiting for transfers between devices: 31.1 us -> none  [the longest x2 18.4 us: several_exchanges(): lax.all_to_all(piece, axis, split_axis=0, concat_axis=0, tiled=True)]
    all_to_all x1 -> x0, blocking collectives: 20.9 us -> none  [local(): lax.all_to_all(requests, ('dp', 'cp'), split_axis=0, concat_axis=0, tiled...]
    all_to_all x3 -> x0, starting transfers between devices: 17.1 us -> none  [the longest x2 12.6 us: several_exchanges(): lax.all_to_all(piece, axis, split_axis=0, concat_axis=0, tiled=True)]
    unnamed x56 -> x9, local copies, waits for them, and re-layouts: 17.1 us -> 4.15 us
  transfers between devices with their start and end apart: 6 -> 0, of which waited for: 6 -> 0; matrix products, arithmetic and copies ran while one was open for 10% -> 0% of each run, Pallas kernels for 0% -> 0%
where the time goes in v1:
time: 134 us; the launch traced here: 133 us
  Pallas kernels  127 us (95%)
  local copies, waits for them, and re-layouts  4.89 us (4%)
    pallas_call x1, Pallas kernels, local(): pl.pallas_call(step_kernel, out_shape=(jax.ShapeDtypeStruct((TOK, D), BF)...  122 us
    pallas_call x1, Pallas kernels, local(): pl.pallas_call(finish_kernel, out_shape=(jax.ShapeDtypeStruct((HOT, D), F...  4.35 us
    unnamed x9, local copies, waits for them, and re-layouts  4.15 us

profile of v1, /device:TPU:1, one launch (start us, length us, event | category | flops | bytes accessed | tf_op | source)
XLA Modules:
  0.0 133.4 jit_solution(3479145394320949644)
XLA Ops:
  0.6 1.2 fusion
  1.8 0.7 copy.14.code_col
  2.6 122.4 %step.1 = (bf16[128,512]{1,0:T(8,128)(2,1)}, bf16[512,512]{1,0:T(8,128)(2,1)}, s32[8,128]{1,0:T(8,128)}, bf16[2,3,4,4,112,128]{5,4,3,2,1,0:T(8,128)(2,1)}) custom-call(s32[128,1]{1,0:T(8,128)} %copy.14.code_col, s32[1,128]{1,0:T(1,128)} %get-tuple-element.24.code_row, bf16[512,512]{1,0:T(8,128)(2,1)} %hot.1, bf16[2048,128]{1,0:T(8,128)(2,1)} %cold.1, ...), custom_call_target="tpu_custom_call" | custom-call | tf_op jit(solution)/shard_map/step/pallas_call | solution.py:548
  124.9 0.0 copy-start
  124.9 1.8 %copy-done = bf16[2,3,4,4,112,128]{5,4,3,2,1,0:T(8,128)(2,1)S(1)} copy-done((bf16[2,3,4,4,112,128]{5,4,3,2,1,0:T(8,128)(2,1)S(1)}, bf16[2,3,4,4,112,128]{5,4,3,2,1,0:T(8,128)(2,1)}, u32[]{:S(2)}) %copy-start) | copy-done | bytes 2752536
  126.7 0.0 copy-start.1
  126.7 1.0 copy-done.1
  127.7 0.0 copy-start.2
  127.7 0.7 copy-done.2
  128.4 0.0 copy-start.3
  128.4 4.3 %finish.1 = (f32[512,512]{1,0:T(8,128)}, f32[2048,128]{1,0:T(8,128)}, f32[128,512]{1,0:T(8,128)}, f32[512,2048]{1,0:T(8,128)}, f32[512,512]{1,0:T(8,128)}) custom-call(bf16[512,512]{1,0:T(8,128)(2,1)S(1)} %copy-done.1, s32[8,128]{1,0:T(8,128)S(1)} %copy-done.2, bf16[2,3,4,4,112,128]{5,4,3,2,1,0:T(8,128)(2,1)S(1)} %copy-done), custom_call_target="tpu_custom_call" | custom-call | tf_op jit(solution)/shard_map/finish/pallas_call | solution.py:586
  132.8 0.0 copy-done.3
  132.8 0.7 copy.16
Async XLA Ops:
  124.9 1.8 %copy-start = (bf16[2,3,4,4,112,128]{5,4,3,2,1,0:T(8,128)(2,1)S(1)}, bf16[2,3,4,4,112,128]{5,4,3,2,1,0:T(8,128)(2,1)}, u32[]{:S(2)}) copy-start(bf16[2,3,4,4,112,128]{5,4,3,2,1,0:T(8,128)(2,1)} %get-tuple-element.18.sums) | copy-start | bytes 8257540
  126.7 1.0 copy-start.1
  127.7 0.7 copy-start.2
  128.4 4.4 %copy-start.3 = (bf16[128,512]{1,0:T(8,128)(2,1)S(1)}, bf16[128,512]{1,0:T(8,128)(2,1)}, u32[]{:S(2)}) copy-start(bf16[128,512]{1,0:T(8,128)(2,1)} %get-tuple-element.32) | copy-start | bytes 393220

commit v2 on v1

v2 whole, which is shorter than its diff:
```python
import math

import jax
import jax.numpy as jnp
from jax import lax
from jax.experimental import pallas as pl
from jax.experimental.pallas import tpu as pltpu
from jax.sharding import PartitionSpec as P

MESH = pl.DeviceIdType.MESH
BF = jnp.bfloat16
F32 = jnp.float32
I32 = jnp.int32
EPSILON = 1e-05

D = 512
HEADS = 8
HEAD = 64
TOK = 128
CAP = 4
HOT = 512
COLD = 2048
COLD_W = 128
N_DP = 8
N_CP = 16
DEVICES = N_DP * N_CP
SLOT = 16
SLOTS = DEVICES * SLOT
SHIFT = 4096
CHUNK = 256
PAIRS = HEADS * (HEADS + 1) // 2
W_ROWS = 4 * D + D + COLD_W
LATE = 2 * D
SETS = (
    (0, 512, (48, 48, 32), (0, 48, 96)),
    (LATE, 832, (64, 64, 80), (128, 192, 256)),
)
PART_ROWS = 336
FAR_FIRST = sorted(
    (
        (dz, dc, dx, dy)
        for dz in range(4)
        for dc in range(2)
        for dx in range(4)
        for dy in range(4)
        if dz or dc or dx or dy
    ),
    key=lambda o: (-sum(min(v, 4 - v) for v in (o[0], o[2], o[3])), sum(o) * 53 % 7, o),
)


def nn(a, b):
    return jnp.dot(a, b, preferred_element_type=F32)


def nt(a, b, precision=None):
    return lax.dot_general(
        a, b, (((1,), (1,)), ((), ())), preferred_element_type=F32, precision=precision
    )


def sigmoid(v):
    return 0.5 * jnp.tanh(0.5 * v) + 0.5


def silu_slope(v):
    sig = sigmoid(v)
    return sig + v * sig * (1.0 - sig)


def iota(shape, dim):
    return lax.broadcasted_iota(I32, shape, dim)


def turned(v):
    return v.astype(F32).T


def column_norm(v):
    average = jnp.mean(v, axis=0, keepdims=True)
    centred = v - average
    inverse = lax.rsqrt(jnp.mean(centred * centred, axis=0, keepdims=True) + EPSILON)
    return centred * inverse, inverse


def column_norm_back(g, y, inverse):
    first = jnp.mean(g, axis=0, keepdims=True)
    second = jnp.mean(g * y, axis=0, keepdims=True)
    return (g - first - y * second) * inverse


def step_kernel(
    owner_in, slot_in, hot_hbm, cold_hbm, proj_hbm, joined_hbm, wout_hbm, cot_hbm,
    layer_out, rows_out, req_out, sums_out,
    hot, cold, proj, joined, wout, cot, code_row,
    ids_all, pick32, pick16, row_in, emb_nat, normed_t, inv_ref, cold_t, joined_t,
    hidden_t, active_t, dgated_t, cot_t, slots_1h,
    k_in, v_in, q_in, w_keep, slope_keep, att_out, att_in, da_out, da_in, da_nat,
    dq_acc, dq_out, dk_out, dv_out, dq_in, dk_in, dv_in, dh_t, pack_ref, grad_out, grad_in,
    rows_buf, layer_buf, req_buf, w_ref, r0, u1, r1, u2, r2, r3, g2, total,
    send, recv, ar_send, ar_recv, local_sem,
):
    dp, cp = lax.axis_index("dp"), lax.axis_index("cp")
    me = dp * N_CP + cp
    z, core, x, y = dp // 2, dp % 2, cp // 4, cp % 4
    head = cp // 2
    half = ((cp + 1) // 2) % 2
    xs, ys, zs = ([(v + d) % 4 for d in range(4)] for v in (x, y, z))
    cores = [core, (core + 1) % 2]
    dps = [[zs[dz] * 2 + cores[dc] for dc in range(2)] for dz in range(4)]
    cps = [[xs[dx] * 4 + ys[dy] for dy in range(4)] for dx in range(4)]
    plane = [(dx, dy) for dx in range(4) for dy in range(4) if dx or dy]
    plane.sort(key=lambda o: (-(min(o[0], 4 - o[0]) + min(o[1], 4 - o[1])), (o[0] * 3 + o[1]) % 4))

    def remote(src, dst, send_sem, recv_sem, to):
        return pltpu.make_async_remote_copy(
            src_ref=src, dst_ref=dst, send_sem=send_sem, recv_sem=recv_sem,
            device_id=to, device_id_type=MESH,
        )

    def wait_sent(ref, i):
        remote(ref, ref, send.at[i], recv.at[i], (dp, cp)).wait_send()

    def wait_got(ref, i):
        remote(ref, ref, send.at[i], recv.at[i], (dp, cp)).wait_recv()

    def rows64(h):
        return pl.ds(pl.multiple_of(h * HEAD, HEAD), HEAD)

    def tile(o):
        return pl.ds(pl.multiple_of(o * SLOT, SLOT), SLOT)

    barrier = pltpu.get_barrier_semaphore()
    everyone = [(dps[dz][dc], cps[dx][dy]) for dz, dc, dx, dy in FAR_FIRST]
    for to in everyone:
        pl.semaphore_signal(barrier, inc=1, device_id=to, device_id_type=MESH)
    loads = [
        pltpu.make_async_copy(src, dst, local_sem.at[i])
        for i, (src, dst) in enumerate(
            ((joined_hbm, joined), (cot_hbm, cot), (wout_hbm, wout), (hot_hbm, hot),
             (cold_hbm, cold), (proj_hbm, proj))
        )
    ]
    for load in loads:
        load.start()
    owner_row, slot_row = owner_in[...], slot_in[...]
    code_row[...] = owner_row * SHIFT + slot_row
    pl.semaphore_wait(barrier, DEVICES - 1)

    for to in everyone:
        remote(code_row, ids_all.at[me], send.at[0], recv.at[0], to).start()
    ids_all[pl.ds(me, 1)] = code_row[...].reshape(1, 1, TOK)

    diagonal = iota((TOK, TOK), 0) == iota((TOK, TOK), 1)

    def as_column(row):
        picked = jnp.where(diagonal, row.astype(F32), 0.0)
        return jnp.sum(picked, axis=1, keepdims=True).astype(I32)

    owner_col, slot_col = as_column(owner_row), as_column(slot_row)
    before_row = (owner_col == owner_row) & (iota((TOK, TOK), 0) < iota((TOK, TOK), 1))
    rank_row = jnp.sum(jnp.where(before_row, 1, 0), axis=0, keepdims=True)
    place_row = owner_row * SLOT + rank_row
    place_col = as_column(place_row)
    for f in range(4):
        slots_1h[:, f * TOK : (f + 1) * TOK] = jnp.where(
            iota((SLOTS, TOK), 0) == place_row + CAP * f, 1.0, 0.0
        ).astype(BF)
    for load in loads[:3]:
        load.wait()
    for b in range(4):
        joined_t[b * D : (b + 1) * D, :] = turned(joined[:, b * D : (b + 1) * D]).astype(BF)
    cot_t[...] = turned(cot[...])
    dgated_t[...] = nn(wout[...], cot_t[...].astype(BF))
    for load in loads[3:]:
        load.wait()

    wait_got(ids_all.at[pl.ds(0, DEVICES - 1)], 0)

    ids = ids_all[:, 0, :]
    asked = (ids // SHIFT) == me
    slot_plus = ((ids % SHIFT) + 1).astype(F32)
    upper = jnp.where(iota((TOK, TOK), 0) < iota((TOK, TOK), 1), 1.0, 0.0).astype(BF)
    earlier = nn(jnp.where(asked, 1.0, 0.0).astype(BF), upper)
    lane_hot = iota((DEVICES, HOT), 1).astype(F32) + 1.0
    lane_cold = iota((DEVICES, COLD), 1).astype(F32) + (HOT + 1.0)
    asks = []
    for c in range(CAP):
        ask = jnp.where(asked & (earlier == float(c)), slot_plus, 0.0)
        asks.append(ask)
        wanted = jnp.sum(ask, axis=1, keepdims=True)
        hot_rows = nn(jnp.where(lane_hot == wanted, 1.0, 0.0).astype(BF), hot[...])
        cold_rows = nn(jnp.where(lane_cold == wanted, 1.0, 0.0).astype(BF), cold[...])
        for f in range(4):
            piece = hot_rows[:, f * 128 : (f + 1) * 128]
            if f == 0:
                piece = piece + cold_rows
            pick32[pl.ds(CAP * f + c, DEVICES, stride=SLOT), :] = piece
    pick16[...] = pick32[...].astype(BF)

    for to in everyone:
        remote(
            pick16.at[tile(to[0] * N_CP + to[1])], row_in.at[tile(me)], send.at[1], recv.at[1], to
        ).start()
    row_in[tile(me), :] = pick16[tile(me), :]
    req_buf[...] = jnp.zeros(req_buf.shape, I32)
    for c in range(CAP):
        wanted_row = jnp.sum(asks[c].T, axis=0, keepdims=True)
        req_buf[c : c + 1, :] = wanted_row.astype(I32) - 1
    req_copy = pltpu.make_async_copy(req_buf, req_out, local_sem.at[6])
    req_copy.start()

    wait_got(row_in.at[pl.ds(0, SLOTS - SLOT)], 1)

    fetched = []
    for f in range(4):
        take = jnp.where(iota((TOK, SLOTS), 1) == place_col + CAP * f, 1.0, 0.0).astype(BF)
        fetched.append(nn(take, row_in[...]))
    cold_vec = fetched[0]
    cold_embed = nn(cold_vec.astype(BF), proj[...])
    embedded = jnp.where(slot_col < HOT, jnp.concatenate(fetched, axis=1), cold_embed)
    emb_nat[...] = embedded
    normed, inverse = column_norm(embedded.T)
    normed_t[...] = normed
    inv_ref[...] = jnp.broadcast_to(inverse, inv_ref.shape)
    low = normed.astype(BF)

    def k_rows(h):
        return pl.ds(pl.multiple_of(3 * D + h * HEAD, HEAD), HEAD)

    def v_rows(h):
        return pl.ds(pl.multiple_of(D + h * HEAD, HEAD), HEAD)

    def q_rows(h):
        return pl.ds(pl.multiple_of(2 * D + h * HEAD, HEAD), HEAD)

    def same_half(d):
        h = (head + d) % HEADS
        return h, (dp, 2 * h + (half + h) % 2)

    def project(b):
        hid = nn(joined_t[b * D : (b + 1) * D, :], low)
        hidden_t[b * D : (b + 1) * D, :] = hid
        active_t[b * D : (b + 1) * D, :] = (hid * sigmoid(hid)).astype(BF)

    project(3)
    for dx, dy in plane:
        pcp = cps[dx][dy]
        remote(active_t.at[k_rows(pcp // 2)], k_in.at[cp], send.at[2], recv.at[2], (dp, pcp)).start()
    project(1)
    for dx, dy in plane:
        pcp = cps[dx][dy]
        remote(active_t.at[v_rows(pcp // 2)], v_in.at[cp], send.at[3], recv.at[3], (dp, pcp)).start()
    project(2)
    for d in range(1, HEADS):
        h, to = same_half(d)
        remote(active_t.at[q_rows(h)], q_in.at[head], send.at[4], recv.at[4], to).start()
    k_in[pl.ds(cp, 1)] = active_t[k_rows(head), :].reshape(1, HEAD, TOK)
    v_in[pl.ds(cp, 1)] = active_t[v_rows(head), :].reshape(1, HEAD, TOK)
    q_in[pl.ds(head, 1)] = active_t[q_rows(head), :].reshape(1, HEAD, TOK)
    project(0)
    cold_t[...] = jnp.where(slot_row < HOT, 0.0, cold_vec.T)
    wait_got(k_in.at[pl.ds(0, N_CP - 1)], 2)
    wait_got(v_in.at[pl.ds(0, N_CP - 1)], 3)
    wait_got(q_in.at[pl.ds(0, HEADS - 1)], 4)

    def block_of(i):
        return 4 * (i // 2) + (half if i % 2 == 0 else 3 - half)

    def pair(ref, c):
        return jnp.concatenate([ref[2 * c], ref[2 * c + 1]], axis=1)

    shrink = 0.5 / math.sqrt(HEAD)
    for i in range(HEADS):
        q_nat = (turned(q_in[i]) * shrink).astype(BF)
        total_t = jnp.zeros((HEAD, TOK), F32)
        for c in range(i + 1):
            s = nn(q_nat, pair(k_in, c))
            up = 1.0 + jnp.tanh(s)
            w = s * up
            slope = up + w * (2.0 - up)
            if c == i:
                ok = (iota((TOK, CHUNK), 1) + c * CHUNK) <= (
                    iota((TOK, CHUNK), 0) + block_of(i) * TOK
                )
                w = jnp.where(ok, w, 0.0)
                slope = jnp.where(ok, slope, 0.0)
            w = w.astype(BF)
            at = i * (i + 1) // 2 + c
            w_keep[at] = w
            slope_keep[at] = slope
            total_t = total_t + nt(pair(v_in, c), w)
        att_out[i] = total_t.astype(BF)

        @pl.when(head != i)
        def _():
            remote(
                att_out.at[i], att_in.at[rows64(head)], send.at[5], recv.at[5], (dp, block_of(i))
            ).start()

    att_in[rows64(head), :] = att_out[pl.ds(head, 1)].reshape(HEAD, TOK)
    wait_got(att_in.at[pl.ds(0, D - HEAD)], 5)

    mixed, inv_mix = column_norm(att_in[...].astype(F32))
    gate = active_t[0:D, :].astype(F32)
    dgated = dgated_t[...]
    da_out[...] = column_norm_back(dgated * gate, mixed, inv_mix).astype(BF)
    for d in range(1, HEADS):
        h, to = same_half(d)
        remote(da_out.at[rows64(h)], da_in.at[head], send.at[6], recv.at[6], to).start()
    da_in[pl.ds(head, 1)] = da_out[rows64(head), :].reshape(1, HEAD, TOK)

    sibling = (z * 2 + (1 - core), cp)
    place = (x, y, z)

    def along(dim, d):
        moved = [xs[0], ys[0], zs[0]]
        moved[dim] = (xs, ys, zs)[dim][d]
        return moved[dim], (moved[2] * 2 + core, moved[0] * 4 + moved[1])

    def ar(src, dst, n, stage, k, to):
        return remote(src, dst, ar_send.at[n, stage, k], ar_recv.at[n, stage, k], to)

    def ar_got(ref, n, stage, k):
        ar(ref, ref, n, stage, k, (dp, cp)).wait_recv()

    def ar_sent(ref, n, stage, k):
        ar(ref, ref, n, stage, k, (dp, cp)).wait_send()

    def core_rows(n, c, first, count):
        base, rows = SETS[n][:2]
        return pl.ds(pl.multiple_of(base + c * rows + first, 16), count)

    def set_rows(n, first, count):
        return pl.ds(SETS[n][0] // 2 + first, count)

    def stage0(n, k, first, count):
        ar(
            w_ref.at[core_rows(n, 1 - core, first, count)], r0.at[set_rows(n, first, count)],
            n, 0, k, sibling,
        ).start()

    def stage1(n, k, first, count, colors):
        at = set_rows(n, first, count)
        ar_got(r0.at[at], n, 0, k)
        u1[at, :] = (
            w_ref[core_rows(n, core, first, count), :].astype(F32) + r0[at, :].astype(F32)
        ).astype(BF)
        for color in colors:
            start1(n, color)

    def piece(n, k):
        return pl.ds(SETS[n][3][k], SETS[n][2][k])

    def u1_rows(n, k, a):
        part = SETS[n][2][k]
        return pl.ds(
            pl.multiple_of(SETS[n][0] // 2 + sum(SETS[n][2][:k]) * 4 + a * part, 16), part
        )

    def start1(n, k):
        for d in (2, 1, 3):
            a, to = along(k, d)
            ar(u1.at[u1_rows(n, k, a)], r1.at[d - 1, piece(n, k)], n, 1, k, to).start()

    def stage2(n, k):
        at = piece(n, k)
        ar_got(r1.at[:, at], n, 1, k)
        part = u1[u1_rows(n, k, place[k]), :].astype(F32)
        for d in range(3):
            part = part + r1[d, at, :].astype(F32)
        for b in range(4):
            u2[b, at, :] = part[:, b * 128 : (b + 1) * 128].astype(BF)
        for d in (2, 1, 3):
            b, to = along((k + 1) % 3, d)
            ar(u2.at[b, at], r2.at[d - 1, at], n, 2, k, to).start()

    def stage3(n, k):
        at, rows = piece(n, k), SETS[n][2][k]
        ar_got(r2.at[:, at], n, 2, k)
        b_me, c_me = place[(k + 1) % 3], place[(k + 2) % 3]
        part = u2[pl.ds(b_me, 1), at, :].astype(F32)
        for d in range(3):
            part = part + r2[d : d + 1, at, :].astype(F32)
        r3[pl.ds(c_me, 1), at, :] = part.astype(BF)
        for d in (2, 1, 3):
            _, to = along((k + 2) % 3, d)
            ar(r3.at[c_me, at], r3.at[c_me, at], n, 3, k, to).start()

    def stage4(n, k):
        at = piece(n, k)
        ar_got(r3.at[pl.ds(0, 3), at], n, 3, k)
        b_me = place[(k + 1) % 3]
        part = r3[0:1, at, :].astype(F32)
        for d in range(1, 4):
            part = part + r3[d : d + 1, at, :].astype(F32)
        g2[pl.ds(b_me, 1), at, :] = part.astype(BF)
        for d in (2, 1, 3):
            _, to = along((k + 1) % 3, d)
            ar(g2.at[b_me, at], g2.at[b_me, at], n, 4, k, to).start()

    def stage5(n, k):
        at = piece(n, k)
        ar_got(g2.at[pl.ds(0, 3), at], n, 4, k)
        a_me = place[k]
        for d in (2, 1, 3):
            _, to = along(k, d)
            ar(g2.at[:, at], total.at[core, a_me, :, at], n, 5, k, to).start()
        total[pl.ds(core, 1), pl.ds(a_me, 1), :, at, :] = g2[:, at, :].reshape(
            1, 1, 4, SETS[n][2][k], 128
        )

    def stage6(n, k):
        at = piece(n, k)
        ar_got(total.at[0, pl.ds(0, 3), :, at], n, 5, k)
        ar(total.at[core, :, :, at], total.at[core, :, :, at], n, 6, k, sibling).start()

    def stage7(n, k):
        ar_got(total.at[0, :, :, piece(n, k)], n, 6, k)

    def all_colors(stage, n):
        for k in range(3):
            stage(n, k)

    def settle(n, firsts):
        for k, count in firsts:
            ar_sent(r0.at[pl.ds(0, count)], n, 0, k)
        for k in range(3):
            at = piece(n, k)
            ar_sent(r1.at[:, at], n, 1, k)
            ar_sent(r2.at[:, at], n, 2, k)
            ar_sent(r3.at[pl.ds(0, 3), at], n, 3, k)
            ar_sent(g2.at[pl.ds(0, 3), at], n, 4, k)
            ar_sent(total.at[0, pl.ds(0, 3), :, at], n, 5, k)
            ar_sent(total.at[0, :, :, at], n, 6, k)

    gated = (mixed * gate).astype(BF)
    low = normed_t[...].astype(BF)
    dh_gate = (dgated * mixed * silu_slope(hidden_t[0:D, :])).astype(BF)
    dh_t[0:D, :] = dh_gate
    w_ref[0:D, :] = nt(low, dh_gate).astype(BF)
    w_ref[D : 2 * D, :] = nn(gated, cot[...]).astype(BF)
    stage0(0, 0, 0, D)
    branch = nn(turned(gated).astype(BF), wout[...])
    layer_buf[...] = (emb_nat[...] + branch).astype(BF)
    layer_copy = pltpu.make_async_copy(layer_buf, layer_out, local_sem.at[7])
    layer_copy.start()
    stage1(0, 0, 0, D, (0, 1, 2))

    wait_got(da_in.at[pl.ds(0, HEADS - 1)], 6)

    for i in range(HEADS):
        da_nat[i] = (turned(da_in[i]) * shrink).astype(BF)
    dq_acc[...] = jnp.zeros(dq_acc.shape, F32)
    for c in range(HEADS - 1, -1, -1):
        keys, values = pair(k_in, c), pair(v_in, c)
        dk = jnp.zeros((HEAD, CHUNK), F32)
        dv = jnp.zeros((HEAD, CHUNK), F32)
        for i in range(c, HEADS):
            at = i * (i + 1) // 2 + c
            ds = (nn(da_nat[i], values) * slope_keep[at]).astype(BF)
            dq = dq_acc[i] + nt(keys, ds)
            if c:
                dq_acc[i] = dq
            else:
                dq_out[i] = dq.astype(BF)

                @pl.when(head != i)
                def _():
                    remote(
                        dq_out.at[i], dq_in.at[rows64(head)], send.at[9], recv.at[9],
                        (dp, block_of(i)),
                    ).start()
            dk = dk + nn(q_in[i], ds)
            dv = dv + nn(da_in[i], w_keep[at])
        dk, dv = dk.astype(BF), dv.astype(BF)
        for b in range(2):
            kb = 2 * c + b
            dk_out[kb] = dk[:, b * TOK : (b + 1) * TOK]
            dv_out[kb] = dv[:, b * TOK : (b + 1) * TOK]

            @pl.when(cp != kb)
            def _():
                remote(
                    dk_out.at[kb], dk_in.at[half, rows64(head)], send.at[7], recv.at[7], (dp, kb)
                ).start()
                remote(
                    dv_out.at[kb], dv_in.at[half, rows64(head)], send.at[8], recv.at[8], (dp, kb)
                ).start()

        if c == 2:
            all_colors(stage2, 0)
        if c == 0:
            all_colors(stage3, 0)

    dq_in[rows64(head), :] = dq_out[pl.ds(head, 1)].reshape(HEAD, TOK)
    dk_in[pl.ds(half, 1), rows64(head), :] = dk_out[pl.ds(cp, 1)]
    dv_in[pl.ds(half, 1), rows64(head), :] = dv_out[pl.ds(cp, 1)]
    wait_got(dk_out.at[pl.ds(0, N_CP - 1)], 7)
    wait_got(dv_out.at[pl.ds(0, N_CP - 1)], 8)
    wait_got(dq_in.at[pl.ds(0, D - HEAD)], 9)

    def column_back(b, grad):
        dh = (grad * silu_slope(hidden_t[b * D : (b + 1) * D, :])).astype(BF)
        dh_t[b * D : (b + 1) * D, :] = dh
        grads = nt(low, dh).astype(BF)
        if b == 1:
            w_ref[LATE : LATE + D, :] = grads
        elif b == 2:
            w_ref[LATE + D : LATE + 768, :] = grads[0:256]
            w_ref[LATE + 832 : LATE + 1088, :] = grads[256:512]
        else:
            w_ref[LATE + 1088 : LATE + 1600, :] = grads

    column_back(1, dv_in[0].astype(F32) + dv_in[1].astype(F32))
    column_back(2, dq_in[...].astype(F32))
    column_back(3, dk_in[0].astype(F32) + dk_in[1].astype(F32))
    stage0(1, 0, 0, 768)
    all_colors(stage4, 0)

    dnormed = nn(joined[...], dh_t[...])
    dembed = column_norm_back(dnormed, normed_t[...], inv_ref[0:1, :]) + cot_t[...]
    exact = lax.Precision.HIGHEST
    proj_grads = nt(cold_t[...], dembed, exact).astype(BF)
    w_ref[LATE + 768 : LATE + 832, :] = proj_grads[0:64]
    w_ref[LATE + 1600 : LATE + 1664, :] = proj_grads[64:128]
    stage0(1, 1, 768, 64)
    stage1(1, 0, 0, 768, (0, 1))
    stage1(1, 1, 768, 64, (2,))

    cold_event = lax.dot_general(
        proj[...].astype(F32), dembed, (((1,), (0,)), ((), ())),
        preferred_element_type=F32, precision=exact,
    )
    is_hot = slot_row < HOT
    for f in range(4):
        part = dembed[f * 128 : (f + 1) * 128, :]
        pack_ref[:, f * TOK : (f + 1) * TOK] = jnp.where(
            is_hot, part, cold_event if f == 0 else 0.0
        ).astype(BF)
    grad_out[...] = nt(slots_1h[...], pack_ref[...]).astype(BF)
    all_colors(stage5, 0)
    for to in everyone:
        remote(
            grad_out.at[tile(to[0] * N_CP + to[1])], grad_in.at[tile(me)],
            send.at[10], recv.at[10], to,
        ).start()
    grad_in[tile(me), :] = grad_out[tile(me), :]

    all_colors(stage2, 1)
    all_colors(stage3, 1)
    all_colors(stage6, 0)
    all_colors(stage4, 1)
    all_colors(stage5, 1)

    wait_got(grad_in.at[pl.ds(0, SLOTS - SLOT)], 10)
    pick32[...] = grad_in[...].astype(F32)
    for c in range(CAP):
        for f in range(4):
            rows_buf[c * DEVICES : (c + 1) * DEVICES, f * 128 : (f + 1) * 128] = pick32[
                pl.ds(CAP * f + c, DEVICES, stride=SLOT), :
            ].astype(BF)
    rows_copy = pltpu.make_async_copy(rows_buf, rows_out, local_sem.at[8])
    rows_copy.start()
    all_colors(stage7, 0)

    wait_sent(ids_all.at[pl.ds(0, DEVICES - 1)], 0)
    wait_sent(row_in.at[pl.ds(0, SLOTS - SLOT)], 1)
    wait_sent(k_in.at[pl.ds(0, N_CP - 1)], 2)
    wait_sent(v_in.at[pl.ds(0, N_CP - 1)], 3)
    wait_sent(q_in.at[pl.ds(0, HEADS - 1)], 4)
    wait_sent(att_in.at[pl.ds(0, D - HEAD)], 5)
    wait_sent(da_in.at[pl.ds(0, HEADS - 1)], 6)
    wait_sent(dk_out.at[pl.ds(0, N_CP - 1)], 7)
    wait_sent(dv_out.at[pl.ds(0, N_CP - 1)], 8)
    wait_sent(dq_in.at[pl.ds(0, D - HEAD)], 9)
    wait_sent(grad_in.at[pl.ds(0, SLOTS - SLOT)], 10)
    settle(0, ((0, D),))
    all_colors(stage6, 1)
    near_copy = pltpu.make_async_copy(total.at[core], sums_out.at[core], local_sem.at[9])
    near_copy.start()
    all_colors(stage7, 1)
    far_copy = pltpu.make_async_copy(total.at[1 - core], sums_out.at[1 - core], local_sem.at[10])
    far_copy.start()
    settle(1, ((0, 768), (1, 64)))
    req_copy.wait()
    layer_copy.wait()
    rows_copy.wait()
    near_copy.wait()
    far_copy.wait()


def finish_kernel(
    layer_in, rows_in, req_in, sums_in,
    layer_out, hot_out, cold_out, proj_out, joined_out, wout_out,
    layer, rows, req, sums, hot_buf, cold_buf, sum_buf, in_sem, sem,
):
    loads = [
        pltpu.make_async_copy(src, dst, in_sem.at[i])
        for i, (src, dst) in enumerate(
            ((req_in, req), (rows_in, rows), (sums_in.at[0], sums.at[0]),
             (sums_in.at[1], sums.at[1]), (layer_in, layer))
        )
    ]
    for load in loads:
        load.start()
    copies = []

    def put(src, dst):
        copy = pltpu.make_async_copy(src, dst, sem.at[len(copies)])
        copy.start()
        copies.append(copy)

    loads[0].wait()
    loads[1].wait()
    picked = rows[...]

    def onehot(rows_here, first):
        index = iota((rows_here, DEVICES), 0) + first
        return jnp.concatenate(
            [jnp.where(index == req[c : c + 1, :], 1.0, 0.0).astype(BF) for c in range(CAP)],
            axis=1,
        )

    hot_buf[...] = nn(onehot(HOT, 0), picked)
    put(hot_buf, hot_out)
    low = picked[:, 0:COLD_W]
    for t in range(4):
        part = pl.ds(t * (COLD // 4), COLD // 4)
        cold_buf[part, :] = nn(onehot(COLD // 4, HOT + t * (COLD // 4)), low)
        put(cold_buf.at[part], cold_out.at[part])

    scale = (TOK * DEVICES) ** -0.5
    for core in range(2):
        loads[2 + core].wait()
        for n in range(2):
            for k in range(3):
                count, at = SETS[n][2][k], SETS[n][3][k]
                for a in range(4):
                    first = sum(SETS[n][2][:k]) * 4 + a * count
                    for source, target, length in targets(n, core, first, count):
                        for b in range(4):
                            sum_buf[target : target + length, b * 128 : (b + 1) * 128] = (
                                sums[core, a, b, at + source : at + source + length, :].astype(F32)
                                * scale
                            )
        if core == 0:
            for b in (0, 1):
                put(sum_buf.at[pl.ds(b * D, D)], joined_out.at[:, pl.ds(b * D, D)])
            loads[4].wait()
            put(layer, layer_out)
    for b in (2, 3):
        put(sum_buf.at[pl.ds(b * D, D)], joined_out.at[:, pl.ds(b * D, D)])
    put(sum_buf.at[pl.ds(4 * D, D)], wout_out)
    put(sum_buf.at[pl.ds(5 * D, COLD_W)], proj_out)
    for copy in copies:
        copy.wait()


def targets(n, core, first, count):
    if n == 0:
        return [(0, (4 * D if core else 0) + first, count)]
    runs = []
    if first < 768:
        length = min(count, 768 - first)
        runs.append((0, D + core * 768 + first, length))
    if first + count > 768:
        start = max(first, 768)
        runs.append((start - first, 5 * D + core * 64 + start - 768, first + count - start))
    return runs


def vmem(n):
    return [pl.BlockSpec(memory_space=pltpu.VMEM)] * n


def anywhere(n):
    return [pl.BlockSpec(memory_space=pl.ANY)] * n


def local(row_owner, slot_row, hot, cold, proj, joined, wout, cot):
    v = pltpu.VMEM
    layer, rows, req, sums = pl.pallas_call(
        step_kernel,
        out_shape=(
            jax.ShapeDtypeStruct((TOK, D), BF),
            jax.ShapeDtypeStruct((CAP * DEVICES, D), BF),
            jax.ShapeDtypeStruct((8, DEVICES), I32),
            jax.ShapeDtypeStruct((2, 4, 4, PART_ROWS, 128), BF),
        ),
        in_specs=vmem(2) + anywhere(6),
        out_specs=tuple(anywhere(4)),
        scratch_shapes=[
            v((HOT, D), BF), v((COLD, COLD_W), BF), v((COLD_W, D), BF), v((D, 4 * D), BF),
            v((D, D), BF), v((TOK, D), BF), v((1, TOK), I32),
            v((DEVICES, 1, TOK), I32), v((SLOTS, 128), F32), v((SLOTS, 128), BF),
            v((SLOTS, 128), BF), v((TOK, D), F32), v((D, TOK), F32), v((8, TOK), F32),
            v((COLD_W, TOK), F32), v((4 * D, D), BF),
            v((4 * D, TOK), F32), v((4 * D, TOK), BF), v((D, TOK), F32), v((D, TOK), F32),
            v((SLOTS, 4 * TOK), BF),
            v((N_CP, HEAD, TOK), BF), v((N_CP, HEAD, TOK), BF), v((HEADS, HEAD, TOK), BF),
            v((PAIRS, TOK, CHUNK), BF), v((PAIRS, TOK, CHUNK), F32),
            v((HEADS, HEAD, TOK), BF), v((D, TOK), BF), v((D, TOK), BF),
            v((HEADS, HEAD, TOK), BF), v((HEADS, TOK, HEAD), BF),
            v((HEADS, HEAD, TOK), F32), v((HEADS, HEAD, TOK), BF),
            v((N_CP, HEAD, TOK), BF), v((N_CP, HEAD, TOK), BF),
            v((D, TOK), BF), v((2, D, TOK), BF), v((2, D, TOK), BF),
            v((4 * D, TOK), BF), v((128, 4 * TOK), BF),
            v((SLOTS, 128), BF), v((SLOTS, 128), BF), v((CAP * DEVICES, D), BF),
            v((TOK, D), BF), v((8, DEVICES), I32),
            v((W_ROWS, D), BF), v((W_ROWS // 2, D), BF), v((W_ROWS // 2, D), BF),
            v((3, PART_ROWS, D), BF), v((4, PART_ROWS, 128), BF),
            v((3, PART_ROWS, 128), BF), v((4, PART_ROWS, 128), BF),
            v((4, PART_ROWS, 128), BF), v((2, 4, 4, PART_ROWS, 128), BF),
            pltpu.SemaphoreType.DMA((11,)), pltpu.SemaphoreType.DMA((11,)),
            pltpu.SemaphoreType.DMA((2, 7, 3)), pltpu.SemaphoreType.DMA((2, 7, 3)),
            pltpu.SemaphoreType.DMA((11,)),
        ],
        compiler_params=pltpu.CompilerParams(
            collective_id=0, has_side_effects=True, vmem_limit_bytes=60 << 20
        ),
        name="step",
    )(row_owner.reshape(1, TOK), slot_row.reshape(1, TOK), hot, cold, proj, joined, wout, cot)
    return pl.pallas_call(
        finish_kernel,
        out_shape=(
            jax.ShapeDtypeStruct((TOK, D), BF),
            jax.ShapeDtypeStruct((HOT, D), F32),
            jax.ShapeDtypeStruct((COLD, COLD_W), F32),
            jax.ShapeDtypeStruct((COLD_W, D), F32),
            jax.ShapeDtypeStruct((D, 4 * D), F32),
            jax.ShapeDtypeStruct((D, D), F32),
        ),
        in_specs=anywhere(4),
        out_specs=tuple(anywhere(6)),
        scratch_shapes=[
            v((TOK, D), BF), v((CAP * DEVICES, D), BF), v((8, DEVICES), I32),
            v((2, 4, 4, PART_ROWS, 128), BF),
            v((HOT, D), F32), v((COLD, COLD_W), F32), v((W_ROWS, D), F32),
            pltpu.SemaphoreType.DMA((5,)), pltpu.SemaphoreType.DMA((12,)),
        ],
        compiler_params=pltpu.CompilerParams(vmem_limit_bytes=60 << 20),
        name="finish",
    )(layer, rows, req, sums)


def solution(mesh):
    rows = P(("dp", "cp"), None)
    return jax.shard_map(
        local,
        mesh=mesh,
        in_specs=(rows, P(("dp", "cp")), rows, rows, P(), P(), P(), rows),
        out_specs=(rows, rows, rows, P(), P(), P()),
        check_vma=False,
    )
```

time: 134 us -> 107 us (0.80)
  Pallas kernels: 127 us -> 106 us
  local copies, waits for them, and re-layouts: 4.89 us -> 0 us
    pallas_call x1, Pallas kernels: 122 us -> 101 us  [local(): pl.pallas_call(step_kernel, out_shape=(jax.ShapeDtypeStruct((TOK, D), BF)...]
    unnamed x9 -> x0, local copies, waits for them, and re-layouts: 4.15 us -> none
where the time goes in v2:
time: 107 us
  Pallas kernels  106 us (99%)
    pallas_call x1, Pallas kernels, local(): pl.pallas_call(step_kernel, out_shape=(jax.ShapeDtypeStruct((TOK, D), BF)...  101 us
    pallas_call x1, Pallas kernels, local(): pl.pallas_call(finish_kernel, out_shape=(jax.ShapeDtypeStruct((TOK, D), B...  4.78 us

profile of v2, /device:TPU:1, one launch (start us, length us, event | category | flops | bytes accessed | tf_op | source)
XLA Modules:
  0.0 106.9 jit_solution(4248177351494634254)
XLA Ops:
  0.6 101.3 %step.1 = (bf16[128,512]{1,0:T(8,128)(2,1)}, bf16[512,512]{1,0:T(8,128)(2,1)}, s32[8,128]{1,0:T(8,128)}, bf16[2,4,4,336,128]{4,3,2,1,0:T(8,128)(2,1)}) custom-call(s32[1,128]{1,0:T(1,128)} %bitcast.2, s32[1,128]{1,0:T(1,128)} %bitcast.3, bf16[512,512]{1,0:T(8,128)(2,1)} %hot_hbm.1, bf16[2048,128]{1,0:T(8,128)(2,1)} %cold_hbm.1, bf16[128,512]{1,0:T(8,128)(2,1)} %proj_hbm.1, ...), custom_call_target="tpu_custom_call" | custom-call | tf_op jit(solution)/shard_map/step/pallas_call | solution.py:683
  101.9 4.8 %finish.1 = (bf16[128,512]{1,0:T(8,128)(2,1)}, f32[512,512]{1,0:T(8,128)}, f32[2048,128]{1,0:T(8,128)}, f32[128,512]{1,0:T(8,128)}, f32[512,2048]{1,0:T(8,128)}, /*index=5*/f32[512,512]{1,0:T(8,128)}) custom-call(bf16[128,512]{1,0:T(8,128)(2,1)} %get-tuple-element.10.layer_in, bf16[512,512]{1,0:T(8,128)(2,1)} %get-tuple-element.11.rows_in, ...), custom_call_target="tpu_custom_call" | custom-call | tf_op jit(solution)/shard_map/finish/pallas_call | solution.py:724

commit v3 on v2

--- a/solution.py
+++ b/solution.py
@@ -91,14 +91,14 @@
 
 def step_kernel(
     owner_in, slot_in, hot_hbm, cold_hbm, proj_hbm, joined_hbm, wout_hbm, cot_hbm,
-    layer_out, rows_out, req_out, sums_out,
-    hot, cold, proj, joined, wout, cot, code_row,
-    ids_all, pick32, pick16, row_in, emb_nat, normed_t, inv_ref, cold_t, joined_t,
+    layer_out, rows_out, req_out, total,
+    hot, cold, cold_wide, proj, joined, wout, cot, owner_ref, slot_ref, code_row,
+    ids_all, pick32, pick16, row_in, take_1h, rows_got, emb_nat, normed_t, inv_ref, cold_t, joined_t,
     hidden_t, active_t, dgated_t, cot_t, slots_1h,
-    k_in, v_in, q_in, w_keep, slope_keep, att_out, att_in, da_out, da_in, da_nat,
-    dq_acc, dq_out, dk_out, dv_out, dq_in, dk_in, dv_in, dh_t, pack_ref, grad_out, grad_in,
-    rows_buf, layer_buf, req_buf, w_ref, r0, u1, r1, u2, r2, r3, g2, total,
-    send, recv, ar_send, ar_recv, local_sem,
+    k_in, v_in, q_in, kv_nat, w_keep, slope_keep, att_out, att_in, da_out, da_in,
+    dk_acc, dv_acc, dq_out, dk_out, dv_out, dq_in, dk_in, dv_in, dh_t, pack_ref, grad_out, grad_in,
+    w_ref, r0, u1, r1, u2, r2, r3, g2,
+    send, recv, da_recv, ar_send, ar_recv, local_sem,
 ):
     dp, cp = lax.axis_index("dp"), lax.axis_index("cp")
     me = dp * N_CP + cp
@@ -130,6 +130,14 @@
     def tile(o):
         return pl.ds(pl.multiple_of(o * SLOT, SLOT), SLOT)
 
+    def by_rank(tiles, rows):
+        pick32[...] = tiles[...].astype(F32)
+        for c in range(CAP):
+            for f in range(4):
+                rows[c * DEVICES : (c + 1) * DEVICES, f * 128 : (f + 1) * 128] = pick32[
+                    pl.ds(CAP * f + c, DEVICES, stride=SLOT), :
+                ].astype(BF)
+
     barrier = pltpu.get_barrier_semaphore()
     everyone = [(dps[dz][dc], cps[dx][dy]) for dz, dc, dx, dy in FAR_FIRST]
     for to in everyone:
@@ -137,13 +145,15 @@
     loads = [
         pltpu.make_async_copy(src, dst, local_sem.at[i])
         for i, (src, dst) in enumerate(
-            ((joined_hbm, joined), (cot_hbm, cot), (wout_hbm, wout), (hot_hbm, hot),
+            ((owner_in, owner_ref), (slot_in, slot_ref), (joined_hbm, joined), (cot_hbm, cot), (wout_hbm, wout), (hot_hbm, hot),
              (cold_hbm, cold), (proj_hbm, proj))
         )
     ]
     for load in loads:
         load.start()
-    owner_row, slot_row = owner_in[...], slot_in[...]
+    for load in loads[:2]:
+        load.wait()
+    owner_row, slot_row = owner_ref[...], slot_ref[...]
     code_row[...] = owner_row * SHIFT + slot_row
     pl.semaphore_wait(barrier, DEVICES - 1)
 
@@ -161,19 +171,23 @@
     before_row = (owner_col == owner_row) & (iota((TOK, TOK), 0) < iota((TOK, TOK), 1))
     rank_row = jnp.sum(jnp.where(before_row, 1, 0), axis=0, keepdims=True)
     place_row = owner_row * SLOT + rank_row
-    place_col = as_column(place_row)
+    take_1h[...] = jnp.where(
+        iota((TOK, CAP * DEVICES), 1) == as_column(rank_row) * DEVICES + owner_col, 1.0, 0.0
+    ).astype(BF)
     for f in range(4):
         slots_1h[:, f * TOK : (f + 1) * TOK] = jnp.where(
             iota((SLOTS, TOK), 0) == place_row + CAP * f, 1.0, 0.0
         ).astype(BF)
-    for load in loads[:3]:
+    for load in loads[2:5]:
         load.wait()
     for b in range(4):
         joined_t[b * D : (b + 1) * D, :] = turned(joined[:, b * D : (b + 1) * D]).astype(BF)
     cot_t[...] = turned(cot[...])
     dgated_t[...] = nn(wout[...], cot_t[...].astype(BF))
-    for load in loads[3:]:
+    for load in loads[5:]:
         load.wait()
+    for g in range(4):
+        cold_wide[:, g * 128 : (g + 1) * 128] = cold[g * HOT : (g + 1) * HOT, :]
 
     wait_got(ids_all.at[pl.ds(0, DEVICES - 1)], 0)
 
@@ -182,20 +196,20 @@
     slot_plus = ((ids % SHIFT) + 1).astype(F32)
     upper = jnp.where(iota((TOK, TOK), 0) < iota((TOK, TOK), 1), 1.0, 0.0).astype(BF)
     earlier = nn(jnp.where(asked, 1.0, 0.0).astype(BF), upper)
-    lane_hot = iota((DEVICES, HOT), 1).astype(F32) + 1.0
-    lane_cold = iota((DEVICES, COLD), 1).astype(F32) + (HOT + 1.0)
-    asks = []
+    asks = [jnp.where(asked & (earlier == float(c)), slot_plus, 0.0) for c in range(CAP)]
     for c in range(CAP):
-        ask = jnp.where(asked & (earlier == float(c)), slot_plus, 0.0)
-        asks.append(ask)
-        wanted = jnp.sum(ask, axis=1, keepdims=True)
-        hot_rows = nn(jnp.where(lane_hot == wanted, 1.0, 0.0).astype(BF), hot[...])
-        cold_rows = nn(jnp.where(lane_cold == wanted, 1.0, 0.0).astype(BF), cold[...])
+        wanted = jnp.sum(asks[c], axis=1, keepdims=True).astype(I32) - 1
+        group = jnp.where(wanted < 0, -1, wanted // HOT)
+        row = jnp.where(wanted < 0, -1, wanted % HOT)
+        chosen = jnp.where(iota((DEVICES, HOT), 1) == row, 1.0, 0.0).astype(BF)
+        hot_rows = nn(chosen, hot[...])
+        cold_rows = nn(chosen, cold_wide[...])
         for f in range(4):
-            piece = hot_rows[:, f * 128 : (f + 1) * 128]
+            part = jnp.where(group == 0, hot_rows[:, f * 128 : (f + 1) * 128], 0.0)
             if f == 0:
-                piece = piece + cold_rows
-            pick32[pl.ds(CAP * f + c, DEVICES, stride=SLOT), :] = piece
+                for g in range(4):
+                    part = jnp.where(group == g + 1, cold_rows[:, g * 128 : (g + 1) * 128], part)
+            pick32[pl.ds(CAP * f + c, DEVICES, stride=SLOT), :] = part
     pick16[...] = pick32[...].astype(BF)
 
     for to in everyone:
@@ -203,22 +217,18 @@
             pick16.at[tile(to[0] * N_CP + to[1])], row_in.at[tile(me)], send.at[1], recv.at[1], to
         ).start()
     row_in[tile(me), :] = pick16[tile(me), :]
-    req_buf[...] = jnp.zeros(req_buf.shape, I32)
+    req_out[...] = jnp.zeros(req_out.shape, I32)
     for c in range(CAP):
         wanted_row = jnp.sum(asks[c].T, axis=0, keepdims=True)
-        req_buf[c : c + 1, :] = wanted_row.astype(I32) - 1
-    req_copy = pltpu.make_async_copy(req_buf, req_out, local_sem.at[6])
-    req_copy.start()
+        req_out[c : c + 1, :] = wanted_row.astype(I32) - 1
 
     wait_got(row_in.at[pl.ds(0, SLOTS - SLOT)], 1)
 
-    fetched = []
-    for f in range(4):
-        take = jnp.where(iota((TOK, SLOTS), 1) == place_col + CAP * f, 1.0, 0.0).astype(BF)
-        fetched.append(nn(take, row_in[...]))
-    cold_vec = fetched[0]
+    by_rank(row_in, rows_got)
+    fetched = nn(take_1h[...], rows_got[...])
+    cold_vec = fetched[:, 0:COLD_W]
     cold_embed = nn(cold_vec.astype(BF), proj[...])
-    embedded = jnp.where(slot_col < HOT, jnp.concatenate(fetched, axis=1), cold_embed)
+    embedded = jnp.where(slot_col < HOT, fetched, cold_embed)
     emb_nat[...] = embedded
     normed, inverse = column_norm(embedded.T)
     normed_t[...] = normed
@@ -271,9 +281,9 @@
         return jnp.concatenate([ref[2 * c], ref[2 * c + 1]], axis=1)
 
     shrink = 0.5 / math.sqrt(HEAD)
-    for i in range(HEADS):
+    for i in range(HEADS - 1, -1, -1):
         q_nat = (turned(q_in[i]) * shrink).astype(BF)
-        total_t = jnp.zeros((HEAD, TOK), F32)
+        sums = jnp.zeros((HEAD, TOK), F32)
         for c in range(i + 1):
             s = nn(q_nat, pair(k_in, c))
             up = 1.0 + jnp.tanh(s)
@@ -289,8 +299,8 @@
             at = i * (i + 1) // 2 + c
             w_keep[at] = w
             slope_keep[at] = slope
-            total_t = total_t + nt(pair(v_in, c), w)
-        att_out[i] = total_t.astype(BF)
+            sums = sums + nt(pair(v_in, c), w)
+        att_out[i] = sums.astype(BF)
 
         @pl.when(head != i)
         def _():
@@ -307,7 +317,7 @@
     da_out[...] = column_norm_back(dgated * gate, mixed, inv_mix).astype(BF)
     for d in range(1, HEADS):
         h, to = same_half(d)
-        remote(da_out.at[rows64(h)], da_in.at[head], send.at[6], recv.at[6], to).start()
+        remote(da_out.at[rows64(h)], da_in.at[head], send.at[6], da_recv.at[head], to).start()
     da_in[pl.ds(head, 1)] = da_out[rows64(head), :].reshape(1, HEAD, TOK)
 
     sibling = (z * 2 + (1 - core), cp)
@@ -442,40 +452,37 @@
     w_ref[D : 2 * D, :] = nn(gated, cot[...]).astype(BF)
     stage0(0, 0, 0, D)
     branch = nn(turned(gated).astype(BF), wout[...])
-    layer_buf[...] = (emb_nat[...] + branch).astype(BF)
-    layer_copy = pltpu.make_async_copy(layer_buf, layer_out, local_sem.at[7])
-    layer_copy.start()
-    stage1(0, 0, 0, D, (0, 1, 2))
-
-    wait_got(da_in.at[pl.ds(0, HEADS - 1)], 6)
-
-    for i in range(HEADS):
-        da_nat[i] = (turned(da_in[i]) * shrink).astype(BF)
-    dq_acc[...] = jnp.zeros(dq_acc.shape, F32)
-    for c in range(HEADS - 1, -1, -1):
-        keys, values = pair(k_in, c), pair(v_in, c)
-        dk = jnp.zeros((HEAD, CHUNK), F32)
-        dv = jnp.zeros((HEAD, CHUNK), F32)
-        for i in range(c, HEADS):
+    layer_out[...] = (emb_nat[...] + branch).astype(BF)
+
+    for b in range(N_CP):
+        kv_nat[b * TOK : (b + 1) * TOK, :] = turned(
+            jnp.concatenate([k_in[b], v_in[b]], axis=0)
+        ).astype(BF)
+
+    for i in range(HEADS - 1, -1, -1):
+
+        @pl.when(head != i)
+        def _():
+            remote(
+                da_in.at[i], da_in.at[i], send.at[6], da_recv.at[i], (dp, cp)
+            ).wait_recv()
+
+        da_t, q_t = da_in[i], q_in[i]
+        da_nat = (turned(da_t) * shrink).astype(BF)
+        dq = jnp.zeros((TOK, 2 * HEAD), F32)
+        for c in range(i + 1):
             at = i * (i + 1) // 2 + c
-            ds = (nn(da_nat[i], values) * slope_keep[at]).astype(BF)
-            dq = dq_acc[i] + nt(keys, ds)
-            if c:
-                dq_acc[i] = dq
-            else:
-                dq_out[i] = dq.astype(BF)
-
-                @pl.when(head != i)
-                def _():
-                    remote(
-                        dq_out.at[i], dq_in.at[rows64(head)], send.at[9], recv.at[9],
-                        (dp, block_of(i)),
-                    ).start()
-            dk = dk + nn(q_in[i], ds)
-            dv = dv + nn(da_in[i], w_keep[at])
+            ds = (nn(da_nat, pair(v_in, c)) * slope_keep[at]).astype(BF)
+            dq = dq + nn(ds, kv_nat[c * CHUNK : (c + 1) * CHUNK, :])
+            dk, dv = nn(q_t, ds), nn(da_t, w_keep[at])
+            if i < HEADS - 1:
+                dk, dv = dk + dk_acc[c], dv + dv_acc[c]
+            if c < i:
+                dk_acc[c], dv_acc[c] = dk, dv
+        dq_out[i] = dq.T[:HEAD, :].astype(BF)
         dk, dv = dk.astype(BF), dv.astype(BF)
         for b in range(2):
-            kb = 2 * c + b
+            kb = 2 * i + b
             dk_out[kb] = dk[:, b * TOK : (b + 1) * TOK]
             dv_out[kb] = dv[:, b * TOK : (b + 1) * TOK]
 
@@ -488,10 +495,16 @@
                     dv_out.at[kb], dv_in.at[half, rows64(head)], send.at[8], recv.at[8], (dp, kb)
                 ).start()
 
-        if c == 2:
-            all_colors(stage2, 0)
-        if c == 0:
-            all_colors(stage3, 0)
+        @pl.when(head != i)
+        def _():
+            remote(
+                dq_out.at[i], dq_in.at[rows64(head)], send.at[9], recv.at[9], (dp, block_of(i))
+            ).start()
+
+        if i == HEADS - 1:
+            stage1(0, 0, 0, D, (0, 1, 2))
+    all_colors(stage2, 0)
+    all_colors(stage3, 0)
 
     dq_in[rows64(head), :] = dq_out[pl.ds(head, 1)].reshape(HEAD, TOK)
     dk_in[pl.ds(half, 1), rows64(head), :] = dk_out[pl.ds(cp, 1)]
@@ -516,17 +529,14 @@
     column_back(2, dq_in[...].astype(F32))
     column_back(3, dk_in[0].astype(F32) + dk_in[1].astype(F32))
     stage0(1, 0, 0, 768)
-    all_colors(stage4, 0)
-
     dnormed = nn(joined[...], dh_t[...])
     dembed = column_norm_back(dnormed, normed_t[...], inv_ref[0:1, :]) + cot_t[...]
     exact = lax.Precision.HIGHEST
+    stage1(1, 0, 0, 768, (0, 1))
     proj_grads = nt(cold_t[...], dembed, exact).astype(BF)
     w_ref[LATE + 768 : LATE + 832, :] = proj_grads[0:64]
     w_ref[LATE + 1600 : LATE + 1664, :] = proj_grads[64:128]
     stage0(1, 1, 768, 64)
-    stage1(1, 0, 0, 768, (0, 1))
-    stage1(1, 1, 768, 64, (2,))
 
     cold_event = lax.dot_general(
         proj[...].astype(F32), dembed, (((1,), (0,)), ((), ())),
@@ -539,30 +549,30 @@
             is_hot, part, cold_event if f == 0 else 0.0
         ).astype(BF)
     grad_out[...] = nt(slots_1h[...], pack_ref[...]).astype(BF)
+    grad_in[tile(me), :] = grad_out[tile(me), :]
+
+    def send_grads(group):
+        for to in everyone[group::4]:
+            remote(
+                grad_out.at[tile(to[0] * N_CP + to[1])], grad_in.at[tile(me)],
+                send.at[10], recv.at[10], to,
+            ).start()
+
+    stage1(1, 1, 768, 64, (2,))
+    all_colors(stage4, 0)
+    all_colors(stage2, 1)
     all_colors(stage5, 0)
-    for to in everyone:
-        remote(
-            grad_out.at[tile(to[0] * N_CP + to[1])], grad_in.at[tile(me)],
-            send.at[10], recv.at[10], to,
-        ).start()
-    grad_in[tile(me), :] = grad_out[tile(me), :]
-
-    all_colors(stage2, 1)
     all_colors(stage3, 1)
+    send_grads(0)
+    send_grads(1)
+    all_colors(stage4, 1)
+    send_grads(2)
+    send_grads(3)
+    all_colors(stage5, 1)
     all_colors(stage6, 0)
-    all_colors(stage4, 1)
-    all_colors(stage5, 1)
 
     wait_got(grad_in.at[pl.ds(0, SLOTS - SLOT)], 10)
-    pick32[...] = grad_in[...].astype(F32)
-    for c in range(CAP):
-        for f in range(4):
-            rows_buf[c * DEVICES : (c + 1) * DEVICES, f * 128 : (f + 1) * 128] = pick32[
-                pl.ds(CAP * f + c, DEVICES, stride=SLOT), :
-            ].astype(BF)
-    rows_copy = pltpu.make_async_copy(rows_buf, rows_out, local_sem.at[8])
-    rows_copy.start()
-    all_colors(stage7, 0)
+    by_rank(grad_in, rows_out)
 
     wait_sent(ids_all.at[pl.ds(0, DEVICES - 1)], 0)
     wait_sent(row_in.at[pl.ds(0, SLOTS - SLOT)], 1)
@@ -577,33 +587,16 @@
     wait_sent(grad_in.at[pl.ds(0, SLOTS - SLOT)], 10)
     settle(0, ((0, D),))
     all_colors(stage6, 1)
-    near_copy = pltpu.make_async_copy(total.at[core], sums_out.at[core], local_sem.at[9])
-    near_copy.start()
+    all_colors(stage7, 0)
     all_colors(stage7, 1)
-    far_copy = pltpu.make_async_copy(total.at[1 - core], sums_out.at[1 - core], local_sem.at[10])
-    far_copy.start()
     settle(1, ((0, 768), (1, 64)))
-    req_copy.wait()
-    layer_copy.wait()
-    rows_copy.wait()
-    near_copy.wait()
-    far_copy.wait()
 
 
 def finish_kernel(
-    layer_in, rows_in, req_in, sums_in,
+    layer, rows, req, sums,
     layer_out, hot_out, cold_out, proj_out, joined_out, wout_out,
-    layer, rows, req, sums, hot_buf, cold_buf, sum_buf, in_sem, sem,
+    hot_buf, cold_buf, sum_buf, sem,
 ):
-    loads = [
-        pltpu.make_async_copy(src, dst, in_sem.at[i])
-        for i, (src, dst) in enumerate(
-            ((req_in, req), (rows_in, rows), (sums_in.at[0], sums.at[0]),
-             (sums_in.at[1], sums.at[1]), (layer_in, layer))
-        )
-    ]
-    for load in loads:
-        load.start()
     copies = []
 
     def put(src, dst):
@@ -611,8 +604,7 @@
         copy.start()
         copies.append(copy)
 
-    loads[0].wait()
-    loads[1].wait()
+    put(layer, layer_out)
     picked = rows[...]
 
     def onehot(rows_here, first):
@@ -632,7 +624,6 @@
 
     scale = (TOK * DEVICES) ** -0.5
     for core in range(2):
-        loads[2 + core].wait()
         for n in range(2):
             for k in range(3):
                 count, at = SETS[n][2][k], SETS[n][3][k]
@@ -647,8 +638,6 @@
         if core == 0:
             for b in (0, 1):
                 put(sum_buf.at[pl.ds(b * D, D)], joined_out.at[:, pl.ds(b * D, D)])
-            loads[4].wait()
-            put(layer, layer_out)
     for b in (2, 3):
         put(sum_buf.at[pl.ds(b * D, D)], joined_out.at[:, pl.ds(b * D, D)])
     put(sum_buf.at[pl.ds(4 * D, D)], wout_out)
@@ -678,8 +667,15 @@
     return [pl.BlockSpec(memory_space=pl.ANY)] * n
 
 
+def hbm(n):
+    return [pl.BlockSpec(memory_space=pltpu.HBM)] * n
+
+
 def local(row_owner, slot_row, hot, cold, proj, joined, wout, cot):
     v = pltpu.VMEM
+    operands = [row_owner.reshape(1, TOK), slot_row.reshape(1, TOK)]
+    operands += [hot, cold, proj, joined, wout, cot]
+    operands = [pltpu.with_memory_space_constraint(a, pltpu.HBM) for a in operands]
     layer, rows, req, sums = pl.pallas_call(
         step_kernel,
         out_shape=(
@@ -688,39 +684,44 @@
             jax.ShapeDtypeStruct((8, DEVICES), I32),
             jax.ShapeDtypeStruct((2, 4, 4, PART_ROWS, 128), BF),
         ),
-        in_specs=vmem(2) + anywhere(6),
-        out_specs=tuple(anywhere(4)),
+        in_specs=hbm(8),
+        out_specs=tuple(vmem(4)),
         scratch_shapes=[
-            v((HOT, D), BF), v((COLD, COLD_W), BF), v((COLD_W, D), BF), v((D, 4 * D), BF),
-            v((D, D), BF), v((TOK, D), BF), v((1, TOK), I32),
+            v((HOT, D), BF), v((COLD, COLD_W), BF), v((HOT, 4 * COLD_W), BF),
+            v((COLD_W, D), BF), v((D, 4 * D), BF),
+            v((D, D), BF), v((TOK, D), BF), v((1, TOK), I32), v((1, TOK), I32),
+            v((1, TOK), I32),
             v((DEVICES, 1, TOK), I32), v((SLOTS, 128), F32), v((SLOTS, 128), BF),
-            v((SLOTS, 128), BF), v((TOK, D), F32), v((D, TOK), F32), v((8, TOK), F32),
+            v((SLOTS, 128), BF), v((TOK, CAP * DEVICES), BF), v((CAP * DEVICES, D), BF),
+            v((TOK, D), F32), v((D, TOK), F32), v((8, TOK), F32),
             v((COLD_W, TOK), F32), v((4 * D, D), BF),
             v((4 * D, TOK), F32), v((4 * D, TOK), BF), v((D, TOK), F32), v((D, TOK), F32),
             v((SLOTS, 4 * TOK), BF),
             v((N_CP, HEAD, TOK), BF), v((N_CP, HEAD, TOK), BF), v((HEADS, HEAD, TOK), BF),
+            v((N_CP * TOK, 2 * HEAD), BF),
             v((PAIRS, TOK, CHUNK), BF), v((PAIRS, TOK, CHUNK), F32),
             v((HEADS, HEAD, TOK), BF), v((D, TOK), BF), v((D, TOK), BF),
-            v((HEADS, HEAD, TOK), BF), v((HEADS, TOK, HEAD), BF),
-            v((HEADS, HEAD, TOK), F32), v((HEADS, HEAD, TOK), BF),
+            v((HEADS, HEAD, TOK), BF),
+            v((HEADS, HEAD, CHUNK), F32), v((HEADS, HEAD, CHUNK), F32),
+            v((HEADS, HEAD, TOK), BF),
             v((N_CP, HEAD, TOK), BF), v((N_CP, HEAD, TOK), BF),
             v((D, TOK), BF), v((2, D, TOK), BF), v((2, D, TOK), BF),
             v((4 * D, TOK), BF), v((128, 4 * TOK), BF),
-            v((SLOTS, 128), BF), v((SLOTS, 128), BF), v((CAP * DEVICES, D), BF),
-            v((TOK, D), BF), v((8, DEVICES), I32),
+            v((SLOTS, 128), BF), v((SLOTS, 128), BF),
             v((W_ROWS, D), BF), v((W_ROWS // 2, D), BF), v((W_ROWS // 2, D), BF),
             v((3, PART_ROWS, D), BF), v((4, PART_ROWS, 128), BF),
             v((3, PART_ROWS, 128), BF), v((4, PART_ROWS, 128), BF),
-            v((4, PART_ROWS, 128), BF), v((2, 4, 4, PART_ROWS, 128), BF),
+            v((4, PART_ROWS, 128), BF),
             pltpu.SemaphoreType.DMA((11,)), pltpu.SemaphoreType.DMA((11,)),
+            pltpu.SemaphoreType.DMA((HEADS,)),
             pltpu.SemaphoreType.DMA((2, 7, 3)), pltpu.SemaphoreType.DMA((2, 7, 3)),
-            pltpu.SemaphoreType.DMA((11,)),
+            pltpu.SemaphoreType.DMA((8,)),
         ],
         compiler_params=pltpu.CompilerParams(
-            collective_id=0, has_side_effects=True, vmem_limit_bytes=60 << 20
+            collective_id=0, has_side_effects=True, vmem_limit_bytes=44 << 20
         ),
         name="step",
-    )(row_owner.reshape(1, TOK), slot_row.reshape(1, TOK), hot, cold, proj, joined, wout, cot)
+    )(*operands)
     return pl.pallas_call(
         finish_kernel,
         out_shape=(
@@ -731,15 +732,13 @@
             jax.ShapeDtypeStruct((D, 4 * D), F32),
             jax.ShapeDtypeStruct((D, D), F32),
         ),
-        in_specs=anywhere(4),
-        out_specs=tuple(anywhere(6)),
+        in_specs=vmem(4),
+        out_specs=tuple(hbm(6)),
         scratch_shapes=[
-            v((TOK, D), BF), v((CAP * DEVICES, D), BF), v((8, DEVICES), I32),
-            v((2, 4, 4, PART_ROWS, 128), BF),
             v((HOT, D), F32), v((COLD, COLD_W), F32), v((W_ROWS, D), F32),
-            pltpu.SemaphoreType.DMA((5,)), pltpu.SemaphoreType.DMA((12,)),
+            pltpu.SemaphoreType.DMA((12,)),
         ],
-        compiler_params=pltpu.CompilerParams(vmem_limit_bytes=60 << 20),
+        compiler_params=pltpu.CompilerParams(vmem_limit_bytes=20 << 20),
         name="finish",
     )(layer, rows, req, sums)
 

time: 107 us -> 99.9 us (0.934)
  Pallas kernels: 106 us -> 99 us
    pallas_call x1, Pallas kernels: 101 us -> 95.4 us  [local(): pl.pallas_call(step_kernel, out_shape=(jax.ShapeDtypeStruct((TOK, D), BF)...]
    pallas_call x1, Pallas kernels: 4.78 us -> 3.63 us  [local(): pl.pallas_call(finish_kernel, out_shape=(jax.ShapeDtypeStruct((TOK, D), B...]
where the time goes in v3:
time: 99.9 us; the launch traced here: 99.8 us
  Pallas kernels  99 us (99%)
    pallas_call x1, Pallas kernels, local(): pl.pallas_call(step_kernel, out_shape=(jax.ShapeDtypeStruct((TOK, D), BF)...  95.4 us
    pallas_call x1, Pallas kernels, local(): pl.pallas_call(finish_kernel, out_shape=(jax.ShapeDtypeStruct((TOK, D), B...  3.63 us

profile of v3, /device:TPU:1, one launch (start us, length us, event | category | flops | bytes accessed | tf_op | source)
XLA Modules:
  0.0 99.8 jit_solution(992782008831113791)
XLA Ops:
  0.6 95.4 %step.1 = (bf16[128,512]{1,0:T(8,128)(2,1)S(1)}, bf16[512,512]{1,0:T(8,128)(2,1)S(1)}, s32[8,128]{1,0:T(8,128)S(1)}, bf16[2,4,4,336,128]{4,3,2,1,0:T(8,128)(2,1)S(1)}) custom-call(s32[1,128]{1,0:T(1,128)} %bitcast.2, s32[1,128]{1,0:T(1,128)} %bitcast.3, bf16[512,512]{1,0:T(8,128)(2,1)} %hot_hbm.1, bf16[2048,128]{1,0:T(8,128)(2,1)} %cold_hbm.1, ...), custom_call_target="tpu_custom_call" | custom-call | tf_op jit(solution)/shard_map/step/pallas_call | solution.py:679
  96.0 3.6 %finish.1 = (bf16[128,512]{1,0:T(8,128)(2,1)}, f32[512,512]{1,0:T(8,128)}, f32[2048,128]{1,0:T(8,128)}, f32[128,512]{1,0:T(8,128)}, f32[512,2048]{1,0:T(8,128)}, /*index=5*/f32[512,512]{1,0:T(8,128)}) custom-call(bf16[128,512]{1,0:T(8,128)(2,1)S(1)} %get-tuple-element.10.layer, bf16[512,512]{1,0:T(8,128)(2,1)S(1)} %get-tuple-element.11.rows, ...), custom_call_target="tpu_custom_call" | custom-call | tf_op jit(solution)/shard_map/finish/pallas_call | solution.py:725

commit v4 on v3

--- a/solution.py
+++ b/solution.py
@@ -32,10 +32,17 @@
 W_ROWS = 4 * D + D + COLD_W
 LATE = 2 * D
 SETS = (
-    (0, 512, (48, 48, 32), (0, 48, 96)),
-    (LATE, 832, (64, 64, 80), (128, 192, 256)),
+    (0, D, 0, D, {0: (48, 0), 1: (48, 48), 2: (32, 96)}),
+    (LATE, 832, D, 768, {0: (64, 128), 1: (64, 192), 2: (64, 256)}),
+    (LATE + 768, 832, D + 768, 64, {2: (16, 320)}),
 )
 PART_ROWS = 336
+
+
+def first_row(n, k):
+    return sum(4 * part for color, (part, _) in SETS[n][4].items() if color < k)
+
+
 FAR_FIRST = sorted(
     (
         (dz, dc, dx, dy)
@@ -96,9 +103,9 @@
     ids_all, pick32, pick16, row_in, take_1h, rows_got, emb_nat, normed_t, inv_ref, cold_t, joined_t,
     hidden_t, active_t, dgated_t, cot_t, slots_1h,
     k_in, v_in, q_in, kv_nat, w_keep, slope_keep, att_out, att_in, da_out, da_in,
-    dk_acc, dv_acc, dq_out, dk_out, dv_out, dq_in, dk_in, dv_in, dh_t, pack_ref, grad_out, grad_in,
+    da_nat, da_cat, q_cat, dq_acc, dq_out, dk_out, dv_out, dq_in, dk_in, dv_in, dh_t, pack_ref, grad_out, grad_in,
     w_ref, r0, u1, r1, u2, r2, r3, g2,
-    send, recv, da_recv, ar_send, ar_recv, local_sem,
+    send, recv, da_recv, ar_send, ar_recv, last_recv, local_sem,
 ):
     dp, cp = lax.axis_index("dp"), lax.axis_index("cp")
     me = dp * N_CP + cp
@@ -280,6 +287,10 @@
     def pair(ref, c):
         return jnp.concatenate([ref[2 * c], ref[2 * c + 1]], axis=1)
 
+    def kept(c, i, count):
+        at = sum(HEADS - b for b in range(c)) + i - c
+        return pl.ds(at * TOK, count * TOK)
+
     shrink = 0.5 / math.sqrt(HEAD)
     for i in range(HEADS - 1, -1, -1):
         q_nat = (turned(q_in[i]) * shrink).astype(BF)
@@ -296,9 +307,8 @@
                 w = jnp.where(ok, w, 0.0)
                 slope = jnp.where(ok, slope, 0.0)
             w = w.astype(BF)
-            at = i * (i + 1) // 2 + c
-            w_keep[at] = w
-            slope_keep[at] = slope
+            w_keep[kept(c, i, 1), :] = w
+            slope_keep[kept(c, i, 1), :] = slope
             sums = sums + nt(pair(v_in, c), w)
         att_out[i] = sums.astype(BF)
 
@@ -337,41 +347,31 @@
     def ar_sent(ref, n, stage, k):
         ar(ref, ref, n, stage, k, (dp, cp)).wait_send()
 
-    def core_rows(n, c, first, count):
-        base, rows = SETS[n][:2]
-        return pl.ds(pl.multiple_of(base + c * rows + first, 16), count)
-
-    def set_rows(n, first, count):
-        return pl.ds(SETS[n][0] // 2 + first, count)
-
-    def stage0(n, k, first, count):
-        ar(
-            w_ref.at[core_rows(n, 1 - core, first, count)], r0.at[set_rows(n, first, count)],
-            n, 0, k, sibling,
-        ).start()
-
-    def stage1(n, k, first, count, colors):
-        at = set_rows(n, first, count)
-        ar_got(r0.at[at], n, 0, k)
-        u1[at, :] = (
-            w_ref[core_rows(n, core, first, count), :].astype(F32) + r0[at, :].astype(F32)
-        ).astype(BF)
-        for color in colors:
-            start1(n, color)
+    def core_rows(n, c):
+        return pl.ds(pl.multiple_of(SETS[n][0] + c * SETS[n][1], 16), SETS[n][3])
+
+    def set_rows(n):
+        return pl.ds(SETS[n][2], SETS[n][3])
+
+    def stage0(n):
+        ar(w_ref.at[core_rows(n, 1 - core)], r0.at[set_rows(n)], n, 0, 0, sibling).start()
 
     def piece(n, k):
-        return pl.ds(SETS[n][3][k], SETS[n][2][k])
+        part, at = SETS[n][4][k]
+        return pl.ds(at, part)
 
     def u1_rows(n, k, a):
-        part = SETS[n][2][k]
-        return pl.ds(
-            pl.multiple_of(SETS[n][0] // 2 + sum(SETS[n][2][:k]) * 4 + a * part, 16), part
-        )
-
-    def start1(n, k):
-        for d in (2, 1, 3):
-            a, to = along(k, d)
-            ar(u1.at[u1_rows(n, k, a)], r1.at[d - 1, piece(n, k)], n, 1, k, to).start()
+        part = SETS[n][4][k][0]
+        return pl.ds(pl.multiple_of(SETS[n][2] + first_row(n, k) + a * part, 16), part)
+
+    def stage1(n):
+        at = set_rows(n)
+        ar_got(r0.at[at], n, 0, 0)
+        u1[at, :] = (w_ref[core_rows(n, core), :].astype(F32) + r0[at, :].astype(F32)).astype(BF)
+        for k in SETS[n][4]:
+            for d in (2, 1, 3):
+                a, to = along(k, d)
+                ar(u1.at[u1_rows(n, k, a)], r1.at[d - 1, piece(n, k)], n, 1, k, to).start()
 
     def stage2(n, k):
         at = piece(n, k)
@@ -386,7 +386,7 @@
             ar(u2.at[b, at], r2.at[d - 1, at], n, 2, k, to).start()
 
     def stage3(n, k):
-        at, rows = piece(n, k), SETS[n][2][k]
+        at = piece(n, k)
         ar_got(r2.at[:, at], n, 2, k)
         b_me, c_me = place[(k + 1) % 3], place[(k + 2) % 3]
         part = u2[pl.ds(b_me, 1), at, :].astype(F32)
@@ -409,33 +409,45 @@
             _, to = along((k + 1) % 3, d)
             ar(g2.at[b_me, at], g2.at[b_me, at], n, 4, k, to).start()
 
+    def to_sibling(n, k, a):
+        held = total.at[core, a, :, piece(n, k)]
+        ar(held, held, n, 6, k, sibling).start()
+
     def stage5(n, k):
         at = piece(n, k)
         ar_got(g2.at[pl.ds(0, 3), at], n, 4, k)
         a_me = place[k]
         for d in (2, 1, 3):
             _, to = along(k, d)
-            ar(g2.at[:, at], total.at[core, a_me, :, at], n, 5, k, to).start()
+            remote(
+                g2.at[:, at], total.at[core, a_me, :, at],
+                ar_send.at[n, 5, k], last_recv.at[n, k, d - 1], to,
+            ).start()
         total[pl.ds(core, 1), pl.ds(a_me, 1), :, at, :] = g2[:, at, :].reshape(
-            1, 1, 4, SETS[n][2][k], 128
+            1, 1, 4, SETS[n][4][k][0], 128
         )
-
-    def stage6(n, k):
-        at = piece(n, k)
-        ar_got(total.at[0, pl.ds(0, 3), :, at], n, 5, k)
-        ar(total.at[core, :, :, at], total.at[core, :, :, at], n, 6, k, sibling).start()
+        to_sibling(n, k, a_me)
+
+    def stage6(n):
+        for d in (1, 3, 2):
+            for k in SETS[n][4]:
+                a, _ = along(k, 4 - d)
+                held = total.at[core, a, :, piece(n, k)]
+                remote(
+                    held, held, ar_send.at[n, 5, k], last_recv.at[n, k, d - 1], (dp, cp)
+                ).wait_recv()
+                to_sibling(n, k, a)
 
     def stage7(n, k):
         ar_got(total.at[0, :, :, piece(n, k)], n, 6, k)
 
     def all_colors(stage, n):
-        for k in range(3):
+        for k in SETS[n][4]:
             stage(n, k)
 
-    def settle(n, firsts):
-        for k, count in firsts:
-            ar_sent(r0.at[pl.ds(0, count)], n, 0, k)
-        for k in range(3):
+    def settle(n):
+        ar_sent(r0.at[set_rows(n)], n, 0, 0)
+        for k in SETS[n][4]:
             at = piece(n, k)
             ar_sent(r1.at[:, at], n, 1, k)
             ar_sent(r2.at[:, at], n, 2, k)
@@ -450,39 +462,56 @@
     dh_t[0:D, :] = dh_gate
     w_ref[0:D, :] = nt(low, dh_gate).astype(BF)
     w_ref[D : 2 * D, :] = nn(gated, cot[...]).astype(BF)
-    stage0(0, 0, 0, D)
+    stage0(0)
     branch = nn(turned(gated).astype(BF), wout[...])
     layer_out[...] = (emb_nat[...] + branch).astype(BF)
 
+    for i in range(HEADS):
+        q_cat[:, i * TOK : (i + 1) * TOK] = q_in[i]
     for b in range(N_CP):
         kv_nat[b * TOK : (b + 1) * TOK, :] = turned(
             jnp.concatenate([k_in[b], v_in[b]], axis=0)
         ).astype(BF)
 
-    for i in range(HEADS - 1, -1, -1):
-
-        @pl.when(head != i)
+    for c in range(HEADS - 1, -1, -1):
+
+        @pl.when(head != c)
         def _():
             remote(
-                da_in.at[i], da_in.at[i], send.at[6], da_recv.at[i], (dp, cp)
+                da_in.at[c], da_in.at[c], send.at[6], da_recv.at[c], (dp, cp)
             ).wait_recv()
 
-        da_t, q_t = da_in[i], q_in[i]
-        da_nat = (turned(da_t) * shrink).astype(BF)
-        dq = jnp.zeros((TOK, 2 * HEAD), F32)
-        for c in range(i + 1):
-            at = i * (i + 1) // 2 + c
-            ds = (nn(da_nat, pair(v_in, c)) * slope_keep[at]).astype(BF)
-            dq = dq + nn(ds, kv_nat[c * CHUNK : (c + 1) * CHUNK, :])
-            dk, dv = nn(q_t, ds), nn(da_t, w_keep[at])
-            if i < HEADS - 1:
-                dk, dv = dk + dk_acc[c], dv + dv_acc[c]
-            if c < i:
-                dk_acc[c], dv_acc[c] = dk, dv
-        dq_out[i] = dq.T[:HEAD, :].astype(BF)
+        da_nat[c * TOK : (c + 1) * TOK, :] = (turned(da_in[c]) * shrink).astype(BF)
+        da_cat[:, c * TOK : (c + 1) * TOK] = da_in[c]
+        values, keys_values = pair(v_in, c), kv_nat[c * CHUNK : (c + 1) * CHUNK, :]
+        dk = jnp.zeros((HEAD, CHUNK), F32)
+        dv = jnp.zeros((HEAD, CHUNK), F32)
+        for first, last in ((c, HEADS),) if c else ((HEADS // 2, HEADS), (0, HEADS // 2)):
+            rows = slice(first * TOK, last * TOK)
+            at = kept(c, first, last - first)
+            ds = (nn(da_nat[rows, :], values) * slope_keep[at, :]).astype(BF)
+            dq = nn(ds, keys_values)
+            dk = dk + nn(q_cat[:, rows], ds)
+            dv = dv + nn(da_cat[:, rows], w_keep[at, :])
+            if c < HEADS - 1:
+                after = slice(max(first, c + 1) * TOK, last * TOK)
+                dq_acc[after, :] += dq[after.start - first * TOK :, :]
+            if first == c:
+                dq_acc[c * TOK : (c + 1) * TOK, :] = dq[0:TOK, :]
+            if c == 0:
+                for i in range(last - 1, first - 1, -1):
+                    dq_out[i] = dq_acc[i * TOK : (i + 1) * TOK, :].T[:HEAD, :].astype(BF)
+
+                    @pl.when(head != i)
+                    def _():
+                        remote(
+                            dq_out.at[i], dq_in.at[rows64(head)], send.at[9], recv.at[9],
+                            (dp, block_of(i)),
+                        ).start()
+
         dk, dv = dk.astype(BF), dv.astype(BF)
         for b in range(2):
-            kb = 2 * i + b
+            kb = 2 * c + b
             dk_out[kb] = dk[:, b * TOK : (b + 1) * TOK]
             dv_out[kb] = dv[:, b * TOK : (b + 1) * TOK]
 
@@ -495,16 +524,7 @@
                     dv_out.at[kb], dv_in.at[half, rows64(head)], send.at[8], recv.at[8], (dp, kb)
                 ).start()
 
-        @pl.when(head != i)
-        def _():
-            remote(
-                dq_out.at[i], dq_in.at[rows64(head)], send.at[9], recv.at[9], (dp, block_of(i))
-            ).start()
-
-        if i == HEADS - 1:
-            stage1(0, 0, 0, D, (0, 1, 2))
-    all_colors(stage2, 0)
-    all_colors(stage3, 0)
+    stage1(0)
 
     dq_in[rows64(head), :] = dq_out[pl.ds(head, 1)].reshape(HEAD, TOK)
     dk_in[pl.ds(half, 1), rows64(head), :] = dk_out[pl.ds(cp, 1)]
@@ -528,15 +548,16 @@
     column_back(1, dv_in[0].astype(F32) + dv_in[1].astype(F32))
     column_back(2, dq_in[...].astype(F32))
     column_back(3, dk_in[0].astype(F32) + dk_in[1].astype(F32))
-    stage0(1, 0, 0, 768)
+    stage0(1)
+    all_colors(stage2, 0)
     dnormed = nn(joined[...], dh_t[...])
     dembed = column_norm_back(dnormed, normed_t[...], inv_ref[0:1, :]) + cot_t[...]
     exact = lax.Precision.HIGHEST
-    stage1(1, 0, 0, 768, (0, 1))
+    stage1(1)
     proj_grads = nt(cold_t[...], dembed, exact).astype(BF)
     w_ref[LATE + 768 : LATE + 832, :] = proj_grads[0:64]
     w_ref[LATE + 1600 : LATE + 1664, :] = proj_grads[64:128]
-    stage0(1, 1, 768, 64)
+    stage0(2)
 
     cold_event = lax.dot_general(
         proj[...].astype(F32), dembed, (((1,), (0,)), ((), ())),
@@ -558,18 +579,25 @@
                 send.at[10], recv.at[10], to,
             ).start()
 
-    stage1(1, 1, 768, 64, (2,))
+    stage1(2)
+    all_colors(stage3, 0)
+    all_colors(stage2, 1)
+    all_colors(stage2, 2)
     all_colors(stage4, 0)
-    all_colors(stage2, 1)
-    all_colors(stage5, 0)
-    all_colors(stage3, 1)
     send_grads(0)
     send_grads(1)
+    all_colors(stage3, 1)
+    all_colors(stage3, 2)
+    all_colors(stage5, 0)
+    send_grads(2)
     all_colors(stage4, 1)
-    send_grads(2)
+    all_colors(stage4, 2)
     send_grads(3)
     all_colors(stage5, 1)
-    all_colors(stage6, 0)
+    all_colors(stage5, 2)
+    stage6(0)
+    stage6(1)
+    stage6(2)
 
     wait_got(grad_in.at[pl.ds(0, SLOTS - SLOT)], 10)
     by_rank(grad_in, rows_out)
@@ -585,11 +613,11 @@
     wait_sent(dv_out.at[pl.ds(0, N_CP - 1)], 8)
     wait_sent(dq_in.at[pl.ds(0, D - HEAD)], 9)
     wait_sent(grad_in.at[pl.ds(0, SLOTS - SLOT)], 10)
-    settle(0, ((0, D),))
-    all_colors(stage6, 1)
-    all_colors(stage7, 0)
-    all_colors(stage7, 1)
-    settle(1, ((0, 768), (1, 64)))
+    settle(0)
+    for n in range(3):
+        all_colors(stage7, n)
+    settle(1)
+    settle(2)
 
 
 def finish_kernel(
@@ -624,17 +652,15 @@
 
     scale = (TOK * DEVICES) ** -0.5
     for core in range(2):
-        for n in range(2):
-            for k in range(3):
-                count, at = SETS[n][2][k], SETS[n][3][k]
+        for n in range(3):
+            home = (4 * D * core, D + 768 * core, 5 * D + 64 * core)[n]
+            for k, (count, at) in SETS[n][4].items():
                 for a in range(4):
-                    first = sum(SETS[n][2][:k]) * 4 + a * count
-                    for source, target, length in targets(n, core, first, count):
-                        for b in range(4):
-                            sum_buf[target : target + length, b * 128 : (b + 1) * 128] = (
-                                sums[core, a, b, at + source : at + source + length, :].astype(F32)
-                                * scale
-                            )
+                    top = home + first_row(n, k) + a * count
+                    for b in range(4):
+                        sum_buf[top : top + count, b * 128 : (b + 1) * 128] = (
+                            sums[core, a, b, at : at + count, :].astype(F32) * scale
+                        )
         if core == 0:
             for b in (0, 1):
                 put(sum_buf.at[pl.ds(b * D, D)], joined_out.at[:, pl.ds(b * D, D)])
@@ -644,19 +670,6 @@
     put(sum_buf.at[pl.ds(5 * D, COLD_W)], proj_out)
     for copy in copies:
         copy.wait()
-
-
-def targets(n, core, first, count):
-    if n == 0:
-        return [(0, (4 * D if core else 0) + first, count)]
-    runs = []
-    if first < 768:
-        length = min(count, 768 - first)
-        runs.append((0, D + core * 768 + first, length))
-    if first + count > 768:
-        start = max(first, 768)
-        runs.append((start - first, 5 * D + core * 64 + start - 768, first + count - start))
-    return runs
 
 
 def vmem(n):
@@ -699,10 +712,11 @@
             v((SLOTS, 4 * TOK), BF),
             v((N_CP, HEAD, TOK), BF), v((N_CP, HEAD, TOK), BF), v((HEADS, HEAD, TOK), BF),
             v((N_CP * TOK, 2 * HEAD), BF),
-            v((PAIRS, TOK, CHUNK), BF), v((PAIRS, TOK, CHUNK), F32),
+            v((PAIRS * TOK, CHUNK), BF), v((PAIRS * TOK, CHUNK), F32),
             v((HEADS, HEAD, TOK), BF), v((D, TOK), BF), v((D, TOK), BF),
             v((HEADS, HEAD, TOK), BF),
-            v((HEADS, HEAD, CHUNK), F32), v((HEADS, HEAD, CHUNK), F32),
+            v((HEADS * TOK, HEAD), BF), v((HEAD, HEADS * TOK), BF), v((HEAD, HEADS * TOK), BF),
+            v((HEADS * TOK, 2 * HEAD), F32),
             v((HEADS, HEAD, TOK), BF),
             v((N_CP, HEAD, TOK), BF), v((N_CP, HEAD, TOK), BF),
             v((D, TOK), BF), v((2, D, TOK), BF), v((2, D, TOK), BF),
@@ -714,7 +728,8 @@
             v((4, PART_ROWS, 128), BF),
             pltpu.SemaphoreType.DMA((11,)), pltpu.SemaphoreType.DMA((11,)),
             pltpu.SemaphoreType.DMA((HEADS,)),
-            pltpu.SemaphoreType.DMA((2, 7, 3)), pltpu.SemaphoreType.DMA((2, 7, 3)),
+            pltpu.SemaphoreType.DMA((3, 7, 3)), pltpu.SemaphoreType.DMA((3, 7, 3)),
+            pltpu.SemaphoreType.DMA((3, 3, 3)),
             pltpu.SemaphoreType.DMA((8,)),
         ],
         compiler_params=pltpu.CompilerParams(

time: 99.9 us -> 98 us (0.981)
  Pallas kernels: 99 us -> 97.1 us
    pallas_call x1, Pallas kernels: 95.4 us -> 93.5 us  [local(): pl.pallas_call(step_kernel, out_shape=(jax.ShapeDtypeStruct((TOK, D), BF)...]
where the time goes in v4:
time: 98 us; the launch traced here: 97.9 us
  Pallas kernels  97.1 us (99%)
    pallas_call x1, Pallas kernels, local(): pl.pallas_call(step_kernel, out_shape=(jax.ShapeDtypeStruct((TOK, D), BF)...  93.5 us
    pallas_call x1, Pallas kernels, local(): pl.pallas_call(finish_kernel, out_shape=(jax.ShapeDtypeStruct((TOK, D), B...  3.63 us

profile of v4, /device:TPU:1, one launch (start us, length us, event | category | flops | bytes accessed | tf_op | source)
XLA Modules:
  0.0 97.9 jit_solution(16511831704089963012)
XLA Ops:
  0.6 93.5 %step.1 = (bf16[128,512]{1,0:T(8,128)(2,1)S(1)}, bf16[512,512]{1,0:T(8,128)(2,1)S(1)}, s32[8,128]{1,0:T(8,128)S(1)}, bf16[2,4,4,336,128]{4,3,2,1,0:T(8,128)(2,1)S(1)}) custom-call(s32[1,128]{1,0:T(1,128)} %bitcast.2, s32[1,128]{1,0:T(1,128)} %bitcast.3, bf16[512,512]{1,0:T(8,128)(2,1)} %hot_hbm.1, bf16[2048,128]{1,0:T(8,128)(2,1)} %cold_hbm.1, ...), custom_call_target="tpu_custom_call" | custom-call | tf_op jit(solution)/shard_map/step/pallas_call | solution.py:692
  94.1 3.6 %finish.1 = (bf16[128,512]{1,0:T(8,128)(2,1)}, f32[512,512]{1,0:T(8,128)}, f32[2048,128]{1,0:T(8,128)}, f32[128,512]{1,0:T(8,128)}, f32[512,2048]{1,0:T(8,128)}, /*index=5*/f32[512,512]{1,0:T(8,128)}) custom-call(bf16[128,512]{1,0:T(8,128)(2,1)S(1)} %get-tuple-element.10.layer, bf16[512,512]{1,0:T(8,128)(2,1)S(1)} %get-tuple-element.11.rows, ...), custom_call_target="tpu_custom_call" | custom-call | tf_op jit(solution)/shard_map/finish/pallas_call | solution.py:740

commit v5 on v4

--- a/solution.py
+++ b/solution.py
@@ -98,12 +98,12 @@
 
 def step_kernel(
     owner_in, slot_in, hot_hbm, cold_hbm, proj_hbm, joined_hbm, wout_hbm, cot_hbm,
-    layer_out, rows_out, req_out, total,
+    layer_out, hot_sum, cold_sum, total,
     hot, cold, cold_wide, proj, joined, wout, cot, owner_ref, slot_ref, code_row,
     ids_all, pick32, pick16, row_in, take_1h, rows_got, emb_nat, normed_t, inv_ref, cold_t, joined_t,
     hidden_t, active_t, dgated_t, cot_t, slots_1h,
     k_in, v_in, q_in, kv_nat, w_keep, slope_keep, att_out, att_in, da_out, da_in,
-    da_nat, da_cat, q_cat, dq_acc, dq_out, dk_out, dv_out, dq_in, dk_in, dv_in, dh_t, pack_ref, grad_out, grad_in,
+    da_nat, da_cat, q_cat, dq_acc, dq_out, dk_out, dv_out, dq_in, dk_in, dv_in, dh_t, pack_ref, grad_out, grad_in, req,
     w_ref, r0, u1, r1, u2, r2, r3, g2,
     send, recv, da_recv, ar_send, ar_recv, last_recv, local_sem,
 ):
@@ -204,19 +204,22 @@
     upper = jnp.where(iota((TOK, TOK), 0) < iota((TOK, TOK), 1), 1.0, 0.0).astype(BF)
     earlier = nn(jnp.where(asked, 1.0, 0.0).astype(BF), upper)
     asks = [jnp.where(asked & (earlier == float(c)), slot_plus, 0.0) for c in range(CAP)]
-    for c in range(CAP):
-        wanted = jnp.sum(asks[c], axis=1, keepdims=True).astype(I32) - 1
-        group = jnp.where(wanted < 0, -1, wanted // HOT)
-        row = jnp.where(wanted < 0, -1, wanted % HOT)
-        chosen = jnp.where(iota((DEVICES, HOT), 1) == row, 1.0, 0.0).astype(BF)
-        hot_rows = nn(chosen, hot[...])
-        cold_rows = nn(chosen, cold_wide[...])
-        for f in range(4):
-            part = jnp.where(group == 0, hot_rows[:, f * 128 : (f + 1) * 128], 0.0)
-            if f == 0:
-                for g in range(4):
-                    part = jnp.where(group == g + 1, cold_rows[:, g * 128 : (g + 1) * 128], part)
-            pick32[pl.ds(CAP * f + c, DEVICES, stride=SLOT), :] = part
+    wanted = jnp.concatenate([jnp.sum(ask, axis=1, keepdims=True) for ask in asks], axis=0)
+    wanted = wanted.astype(I32) - 1
+    group = jnp.where(wanted < 0, -1, wanted // HOT)
+    row = jnp.where(wanted < 0, -1, wanted % HOT)
+    chosen = jnp.where(iota((CAP * DEVICES, HOT), 1) == row, 1.0, 0.0).astype(BF)
+    hot_rows = nn(chosen, hot[...])
+    cold_rows = nn(chosen, cold_wide[...])
+    for f in range(4):
+        part = jnp.where(group == 0, hot_rows[:, f * 128 : (f + 1) * 128], 0.0)
+        if f == 0:
+            for g in range(4):
+                part = jnp.where(group == g + 1, cold_rows[:, g * 128 : (g + 1) * 128], part)
+        for c in range(CAP):
+            pick32[pl.ds(CAP * f + c, DEVICES, stride=SLOT), :] = part[
+                c * DEVICES : (c + 1) * DEVICES, :
+            ]
     pick16[...] = pick32[...].astype(BF)
 
     for to in everyone:
@@ -224,10 +227,9 @@
             pick16.at[tile(to[0] * N_CP + to[1])], row_in.at[tile(me)], send.at[1], recv.at[1], to
         ).start()
     row_in[tile(me), :] = pick16[tile(me), :]
-    req_out[...] = jnp.zeros(req_out.shape, I32)
     for c in range(CAP):
         wanted_row = jnp.sum(asks[c].T, axis=0, keepdims=True)
-        req_out[c : c + 1, :] = wanted_row.astype(I32) - 1
+        req[c : c + 1, :] = wanted_row.astype(I32) - 1
 
     wait_got(row_in.at[pl.ds(0, SLOTS - SLOT)], 1)
 
@@ -292,7 +294,7 @@
         return pl.ds(at * TOK, count * TOK)
 
     shrink = 0.5 / math.sqrt(HEAD)
-    for i in range(HEADS - 1, -1, -1):
+    def attend(i):
         q_nat = (turned(q_in[i]) * shrink).astype(BF)
         sums = jnp.zeros((HEAD, TOK), F32)
         for c in range(i + 1):
@@ -312,11 +314,17 @@
             sums = sums + nt(pair(v_in, c), w)
         att_out[i] = sums.astype(BF)
 
-        @pl.when(head != i)
-        def _():
-            remote(
-                att_out.at[i], att_in.at[rows64(head)], send.at[5], recv.at[5], (dp, block_of(i))
-            ).start()
+    for group in ((7, 6, 5), (4, 3, 2, 1, 0)):
+        for i in group:
+            attend(i)
+        for i in group:
+
+            @pl.when(head != i)
+            def _():
+                remote(
+                    att_out.at[i], att_in.at[rows64(head)], send.at[5], recv.at[5],
+                    (dp, block_of(i)),
+                ).start()
 
     att_in[rows64(head), :] = att_out[pl.ds(head, 1)].reshape(HEAD, TOK)
     wait_got(att_in.at[pl.ds(0, D - HEAD)], 5)
@@ -473,47 +481,39 @@
             jnp.concatenate([k_in[b], v_in[b]], axis=0)
         ).astype(BF)
 
-    for c in range(HEADS - 1, -1, -1):
-
-        @pl.when(head != c)
-        def _():
-            remote(
-                da_in.at[c], da_in.at[c], send.at[6], da_recv.at[c], (dp, cp)
-            ).wait_recv()
-
+    def backward(c):
         da_nat[c * TOK : (c + 1) * TOK, :] = (turned(da_in[c]) * shrink).astype(BF)
         da_cat[:, c * TOK : (c + 1) * TOK] = da_in[c]
-        values, keys_values = pair(v_in, c), kv_nat[c * CHUNK : (c + 1) * CHUNK, :]
-        dk = jnp.zeros((HEAD, CHUNK), F32)
-        dv = jnp.zeros((HEAD, CHUNK), F32)
-        for first, last in ((c, HEADS),) if c else ((HEADS // 2, HEADS), (0, HEADS // 2)):
-            rows = slice(first * TOK, last * TOK)
-            at = kept(c, first, last - first)
-            ds = (nn(da_nat[rows, :], values) * slope_keep[at, :]).astype(BF)
-            dq = nn(ds, keys_values)
-            dk = dk + nn(q_cat[:, rows], ds)
-            dv = dv + nn(da_cat[:, rows], w_keep[at, :])
-            if c < HEADS - 1:
-                after = slice(max(first, c + 1) * TOK, last * TOK)
-                dq_acc[after, :] += dq[after.start - first * TOK :, :]
-            if first == c:
-                dq_acc[c * TOK : (c + 1) * TOK, :] = dq[0:TOK, :]
-            if c == 0:
-                for i in range(last - 1, first - 1, -1):
-                    dq_out[i] = dq_acc[i * TOK : (i + 1) * TOK, :].T[:HEAD, :].astype(BF)
-
-                    @pl.when(head != i)
-                    def _():
-                        remote(
-                            dq_out.at[i], dq_in.at[rows64(head)], send.at[9], recv.at[9],
-                            (dp, block_of(i)),
-                        ).start()
-
-        dk, dv = dk.astype(BF), dv.astype(BF)
+        rows = slice(c * TOK, HEADS * TOK)
+        at = kept(c, c, HEADS - c)
+        ds = (nn(da_nat[rows, :], pair(v_in, c)) * slope_keep[at, :]).astype(BF)
+        dk = nn(q_cat[:, rows], ds).astype(BF)
+        dv = nn(da_cat[:, rows], w_keep[at, :]).astype(BF)
         for b in range(2):
-            kb = 2 * c + b
-            dk_out[kb] = dk[:, b * TOK : (b + 1) * TOK]
-            dv_out[kb] = dv[:, b * TOK : (b + 1) * TOK]
+            dk_out[2 * c + b] = dk[:, b * TOK : (b + 1) * TOK]
+            dv_out[2 * c + b] = dv[:, b * TOK : (b + 1) * TOK]
+        dq = nn(ds, kv_nat[c * CHUNK : (c + 1) * CHUNK, :])
+        if c < HEADS - 1:
+            dq_acc[(c + 1) * TOK :, :] += dq[TOK:, :]
+        dq_acc[c * TOK : (c + 1) * TOK, :] = dq[0:TOK, :]
+
+    for group in ((7, 6, 5), (4, 3), (2, 1), (0,)):
+        for c in group:
+
+            @pl.when(head != c)
+            def _():
+                remote(
+                    da_in.at[c], da_in.at[c], send.at[6], da_recv.at[c], (dp, cp)
+                ).wait_recv()
+
+        for c in group:
+            backward(c)
+        if group == (0,):
+            for i in range(HEADS):
+                dq_out[i] = dq_acc[i * TOK : (i + 1) * TOK, :].T[:HEAD, :].astype(BF)
+        if group == (7, 6, 5):
+            stage1(0)
+        for kb in [2 * c + b for c in group for b in range(2)]:
 
             @pl.when(cp != kb)
             def _():
@@ -524,7 +524,15 @@
                     dv_out.at[kb], dv_in.at[half, rows64(head)], send.at[8], recv.at[8], (dp, kb)
                 ).start()
 
-    stage1(0)
+    for i in range(HEADS):
+
+        @pl.when(head != i)
+        def _():
+            remote(
+                dq_out.at[i], dq_in.at[rows64(head)], send.at[9], recv.at[9], (dp, block_of(i))
+            ).start()
+
+    all_colors(stage2, 0)
 
     dq_in[rows64(head), :] = dq_out[pl.ds(head, 1)].reshape(HEAD, TOK)
     dk_in[pl.ds(half, 1), rows64(head), :] = dk_out[pl.ds(cp, 1)]
@@ -549,10 +557,10 @@
     column_back(2, dq_in[...].astype(F32))
     column_back(3, dk_in[0].astype(F32) + dk_in[1].astype(F32))
     stage0(1)
-    all_colors(stage2, 0)
     dnormed = nn(joined[...], dh_t[...])
     dembed = column_norm_back(dnormed, normed_t[...], inv_ref[0:1, :]) + cot_t[...]
     exact = lax.Precision.HIGHEST
+    all_colors(stage3, 0)
     stage1(1)
     proj_grads = nt(cold_t[...], dembed, exact).astype(BF)
     w_ref[LATE + 768 : LATE + 832, :] = proj_grads[0:64]
@@ -580,15 +588,14 @@
             ).start()
 
     stage1(2)
-    all_colors(stage3, 0)
+    all_colors(stage4, 0)
     all_colors(stage2, 1)
     all_colors(stage2, 2)
-    all_colors(stage4, 0)
+    all_colors(stage5, 0)
     send_grads(0)
-    send_grads(1)
     all_colors(stage3, 1)
     all_colors(stage3, 2)
-    all_colors(stage5, 0)
+    send_grads(1)
     send_grads(2)
     all_colors(stage4, 1)
     all_colors(stage4, 2)
@@ -600,7 +607,19 @@
     stage6(2)
 
     wait_got(grad_in.at[pl.ds(0, SLOTS - SLOT)], 10)
-    by_rank(grad_in, rows_out)
+    by_rank(grad_in, rows_got)
+
+    def onehot(rows_here, first):
+        index = iota((rows_here, DEVICES), 0) + first
+        return jnp.concatenate(
+            [jnp.where(index == req[c : c + 1, :], 1.0, 0.0).astype(BF) for c in range(CAP)],
+            axis=1,
+        )
+
+    hot_sum[...] = nn(onehot(HOT, 0), rows_got[...])
+    for t in range(4):
+        part = slice(t * HOT, (t + 1) * HOT)
+        cold_sum[part, :] = nn(onehot(HOT, HOT + t * HOT), rows_got[:, 0:COLD_W])
 
     wait_sent(ids_all.at[pl.ds(0, DEVICES - 1)], 0)
     wait_sent(row_in.at[pl.ds(0, SLOTS - SLOT)], 1)
@@ -621,9 +640,9 @@
 
 
 def finish_kernel(
-    layer, rows, req, sums,
+    layer, hot_sum, cold_sum, sums,
     layer_out, hot_out, cold_out, proj_out, joined_out, wout_out,
-    hot_buf, cold_buf, sum_buf, sem,
+    sum_buf, sem,
 ):
     copies = []
 
@@ -633,40 +652,34 @@
         copies.append(copy)
 
     put(layer, layer_out)
-    picked = rows[...]
-
-    def onehot(rows_here, first):
-        index = iota((rows_here, DEVICES), 0) + first
-        return jnp.concatenate(
-            [jnp.where(index == req[c : c + 1, :], 1.0, 0.0).astype(BF) for c in range(CAP)],
-            axis=1,
-        )
-
-    hot_buf[...] = nn(onehot(HOT, 0), picked)
-    put(hot_buf, hot_out)
-    low = picked[:, 0:COLD_W]
-    for t in range(4):
-        part = pl.ds(t * (COLD // 4), COLD // 4)
-        cold_buf[part, :] = nn(onehot(COLD // 4, HOT + t * (COLD // 4)), low)
-        put(cold_buf.at[part], cold_out.at[part])
-
+    put(hot_sum, hot_out)
+    put(cold_sum, cold_out)
     scale = (TOK * DEVICES) ** -0.5
-    for core in range(2):
-        for n in range(3):
-            home = (4 * D * core, D + 768 * core, 5 * D + 64 * core)[n]
-            for k, (count, at) in SETS[n][4].items():
-                for a in range(4):
-                    top = home + first_row(n, k) + a * count
-                    for b in range(4):
-                        sum_buf[top : top + count, b * 128 : (b + 1) * 128] = (
-                            sums[core, a, b, at : at + count, :].astype(F32) * scale
-                        )
-        if core == 0:
-            for b in (0, 1):
-                put(sum_buf.at[pl.ds(b * D, D)], joined_out.at[:, pl.ds(b * D, D)])
-    for b in (2, 3):
+
+    def scaled(n, core):
+        home = (4 * D * core, D + 768 * core, 5 * D + 64 * core)[n]
+        for k, (count, at) in SETS[n][4].items():
+            for a in range(4):
+                top = home + first_row(n, k) + a * count
+                for b in range(4):
+                    sum_buf[top : top + count, b * 128 : (b + 1) * 128] = (
+                        sums[core, a, b, at : at + count, :].astype(F32) * scale
+                    )
+
+    def put_joined(b):
         put(sum_buf.at[pl.ds(b * D, D)], joined_out.at[:, pl.ds(b * D, D)])
+
+    scaled(0, 0)
+    put_joined(0)
+    scaled(1, 0)
+    put_joined(1)
+    scaled(1, 1)
+    put_joined(2)
+    put_joined(3)
+    scaled(0, 1)
     put(sum_buf.at[pl.ds(4 * D, D)], wout_out)
+    scaled(2, 0)
+    scaled(2, 1)
     put(sum_buf.at[pl.ds(5 * D, COLD_W)], proj_out)
     for copy in copies:
         copy.wait()
@@ -689,12 +702,12 @@
     operands = [row_owner.reshape(1, TOK), slot_row.reshape(1, TOK)]
     operands += [hot, cold, proj, joined, wout, cot]
     operands = [pltpu.with_memory_space_constraint(a, pltpu.HBM) for a in operands]
-    layer, rows, req, sums = pl.pallas_call(
+    layer, hot_sum, cold_sum, sums = pl.pallas_call(
         step_kernel,
         out_shape=(
             jax.ShapeDtypeStruct((TOK, D), BF),
-            jax.ShapeDtypeStruct((CAP * DEVICES, D), BF),
-            jax.ShapeDtypeStruct((8, DEVICES), I32),
+            jax.ShapeDtypeStruct((HOT, D), F32),
+            jax.ShapeDtypeStruct((COLD, COLD_W), F32),
             jax.ShapeDtypeStruct((2, 4, 4, PART_ROWS, 128), BF),
         ),
         in_specs=hbm(8),
@@ -721,7 +734,7 @@
             v((N_CP, HEAD, TOK), BF), v((N_CP, HEAD, TOK), BF),
             v((D, TOK), BF), v((2, D, TOK), BF), v((2, D, TOK), BF),
             v((4 * D, TOK), BF), v((128, 4 * TOK), BF),
-            v((SLOTS, 128), BF), v((SLOTS, 128), BF),
+            v((SLOTS, 128), BF), v((SLOTS, 128), BF), v((8, DEVICES), I32),
             v((W_ROWS, D), BF), v((W_ROWS // 2, D), BF), v((W_ROWS // 2, D), BF),
             v((3, PART_ROWS, D), BF), v((4, PART_ROWS, 128), BF),
             v((3, PART_ROWS, 128), BF), v((4, PART_ROWS, 128), BF),
@@ -750,12 +763,12 @@
         in_specs=vmem(4),
         out_specs=tuple(hbm(6)),
         scratch_shapes=[
-            v((HOT, D), F32), v((COLD, COLD_W), F32), v((W_ROWS, D), F32),
-            pltpu.SemaphoreType.DMA((12,)),
+            v((W_ROWS, D), F32),
+            pltpu.SemaphoreType.DMA((9,)),
         ],
         compiler_params=pltpu.CompilerParams(vmem_limit_bytes=20 << 20),
         name="finish",
-    )(layer, rows, req, sums)
+    )(layer, hot_sum, cold_sum, sums)
 
 
 def solution(mesh):

time: 98 us -> 97 us (0.990)
  Pallas kernels: 97.1 us -> 96.1 us
where the time goes in v5:
time: 97 us; the launch traced here: 96.9 us
  Pallas kernels  96.1 us (99%)
    pallas_call x1, Pallas kernels, local(): pl.pallas_call(step_kernel, out_shape=(jax.ShapeDtypeStruct((TOK, D), BF)...  92.9 us
    pallas_call x1, Pallas kernels, local(): pl.pallas_call(finish_kernel, out_shape=(jax.ShapeDtypeStruct((TOK, D), B...  3.15 us

profile of v5, /device:TPU:1, one launch (start us, length us, event | category | flops | bytes accessed | tf_op | source)
XLA Modules:
  0.0 96.9 jit_solution(493858311898243963)
XLA Ops:
  0.6 92.9 %step.1 = (bf16[128,512]{1,0:T(8,128)(2,1)S(1)}, f32[512,512]{1,0:T(8,128)S(1)}, f32[2048,128]{1,0:T(8,128)S(1)}, bf16[2,4,4,336,128]{4,3,2,1,0:T(8,128)(2,1)S(1)}) custom-call(s32[1,128]{1,0:T(1,128)} %bitcast.2, s32[1,128]{1,0:T(1,128)} %bitcast.3, bf16[512,512]{1,0:T(8,128)(2,1)} %hot_hbm.1, bf16[2048,128]{1,0:T(8,128)(2,1)} %cold_hbm.1, ...), custom_call_target="tpu_custom_call" | custom-call | tf_op jit(solution)/shard_map/step/pallas_call | solution.py:705
  93.6 3.2 %finish.1 = (bf16[128,512]{1,0:T(8,128)(2,1)}, f32[512,512]{1,0:T(8,128)}, f32[2048,128]{1,0:T(8,128)}, f32[128,512]{1,0:T(8,128)}, f32[512,2048]{1,0:T(8,128)}, /*index=5*/f32[512,512]{1,0:T(8,128)}) custom-call(bf16[128,512]{1,0:T(8,128)(2,1)S(1)} %get-tuple-element.10.layer, f32[512,512]{1,0:T(8,128)S(1)} %get-tuple-element.11.hot_sum, ...), custom_call_target="tpu_custom_call" | custom-call | tf_op jit(solution)/shard_map/finish/pallas_call | solution.py:753

commit v6 on v5

--- a/solution.py
+++ b/solution.py
@@ -26,7 +26,8 @@
 DEVICES = N_DP * N_CP
 SLOT = 16
 SLOTS = DEVICES * SLOT
-SHIFT = 4096
+BITS = 12
+SHIFT = 1 << BITS
 CHUNK = 256
 PAIRS = HEADS * (HEADS + 1) // 2
 W_ROWS = 4 * D + D + COLD_W
@@ -37,6 +38,7 @@
     (LATE + 768, 832, D + 768, 64, {2: (16, 320)}),
 )
 PART_ROWS = 336
+SENT_KIB = 2 * 4 * (DEVICES - 1) + 16 * (4 * (N_CP - 1) + 4 * (HEADS - 1))
 
 
 def first_row(n, k):
@@ -103,7 +105,7 @@
     ids_all, pick32, pick16, row_in, take_1h, rows_got, emb_nat, normed_t, inv_ref, cold_t, joined_t,
     hidden_t, active_t, dgated_t, cot_t, slots_1h,
     k_in, v_in, q_in, kv_nat, w_keep, slope_keep, att_out, att_in, da_out, da_in,
-    da_nat, da_cat, q_cat, dq_acc, dq_out, dk_out, dv_out, dq_in, dk_in, dv_in, dh_t, pack_ref, grad_out, grad_in, req,
+    da_nat, da_cat, q_cat, dq_acc, dq_out, dk_out, dv_out, dq_in, dk_in, dv_in, dh_t, pack_ref, grad_out, grad_in, named,
     w_ref, r0, u1, r1, u2, r2, r3, g2,
     send, recv, da_recv, ar_send, ar_recv, last_recv, local_sem,
 ):
@@ -125,11 +127,8 @@
             device_id=to, device_id_type=MESH,
         )
 
-    def wait_sent(ref, i):
-        remote(ref, ref, send.at[i], recv.at[i], (dp, cp)).wait_send()
-
     def wait_got(ref, i):
-        remote(ref, ref, send.at[i], recv.at[i], (dp, cp)).wait_recv()
+        remote(ref, ref, send.at[0], recv.at[i], (dp, cp)).wait_recv()
 
     def rows64(h):
         return pl.ds(pl.multiple_of(h * HEAD, HEAD), HEAD)
@@ -199,15 +198,15 @@
     wait_got(ids_all.at[pl.ds(0, DEVICES - 1)], 0)
 
     ids = ids_all[:, 0, :]
-    asked = (ids // SHIFT) == me
-    slot_plus = ((ids % SHIFT) + 1).astype(F32)
+    asked = (ids >> BITS) == me
+    slot_plus = ((ids & (SHIFT - 1)) + 1).astype(F32)
     upper = jnp.where(iota((TOK, TOK), 0) < iota((TOK, TOK), 1), 1.0, 0.0).astype(BF)
     earlier = nn(jnp.where(asked, 1.0, 0.0).astype(BF), upper)
     asks = [jnp.where(asked & (earlier == float(c)), slot_plus, 0.0) for c in range(CAP)]
     wanted = jnp.concatenate([jnp.sum(ask, axis=1, keepdims=True) for ask in asks], axis=0)
     wanted = wanted.astype(I32) - 1
-    group = jnp.where(wanted < 0, -1, wanted // HOT)
-    row = jnp.where(wanted < 0, -1, wanted % HOT)
+    group = wanted >> 9
+    row = jnp.where(wanted < 0, -1, wanted & (HOT - 1))
     chosen = jnp.where(iota((CAP * DEVICES, HOT), 1) == row, 1.0, 0.0).astype(BF)
     hot_rows = nn(chosen, hot[...])
     cold_rows = nn(chosen, cold_wide[...])
@@ -229,7 +228,9 @@
     row_in[tile(me), :] = pick16[tile(me), :]
     for c in range(CAP):
         wanted_row = jnp.sum(asks[c].T, axis=0, keepdims=True)
-        req[c : c + 1, :] = wanted_row.astype(I32) - 1
+        named[:, c * DEVICES : (c + 1) * DEVICES] = jnp.where(
+            iota((HOT + COLD, DEVICES), 0) == wanted_row.astype(I32) - 1, 1.0, 0.0
+        ).astype(BF)
 
     wait_got(row_in.at[pl.ds(0, SLOTS - SLOT)], 1)
 
@@ -265,15 +266,15 @@
     project(3)
     for dx, dy in plane:
         pcp = cps[dx][dy]
-        remote(active_t.at[k_rows(pcp // 2)], k_in.at[cp], send.at[2], recv.at[2], (dp, pcp)).start()
+        remote(active_t.at[k_rows(pcp // 2)], k_in.at[cp], send.at[1], recv.at[2], (dp, pcp)).start()
     project(1)
     for dx, dy in plane:
         pcp = cps[dx][dy]
-        remote(active_t.at[v_rows(pcp // 2)], v_in.at[cp], send.at[3], recv.at[3], (dp, pcp)).start()
+        remote(active_t.at[v_rows(pcp // 2)], v_in.at[cp], send.at[1], recv.at[3], (dp, pcp)).start()
     project(2)
     for d in range(1, HEADS):
         h, to = same_half(d)
-        remote(active_t.at[q_rows(h)], q_in.at[head], send.at[4], recv.at[4], to).start()
+        remote(active_t.at[q_rows(h)], q_in.at[head], send.at[1], recv.at[4], to).start()
     k_in[pl.ds(cp, 1)] = active_t[k_rows(head), :].reshape(1, HEAD, TOK)
     v_in[pl.ds(cp, 1)] = active_t[v_rows(head), :].reshape(1, HEAD, TOK)
     q_in[pl.ds(head, 1)] = active_t[q_rows(head), :].reshape(1, HEAD, TOK)
@@ -322,7 +323,7 @@
             @pl.when(head != i)
             def _():
                 remote(
-                    att_out.at[i], att_in.at[rows64(head)], send.at[5], recv.at[5],
+                    att_out.at[i], att_in.at[rows64(head)], send.at[1], recv.at[5],
                     (dp, block_of(i)),
                 ).start()
 
@@ -335,7 +336,7 @@
     da_out[...] = column_norm_back(dgated * gate, mixed, inv_mix).astype(BF)
     for d in range(1, HEADS):
         h, to = same_half(d)
-        remote(da_out.at[rows64(h)], da_in.at[head], send.at[6], da_recv.at[head], to).start()
+        remote(da_out.at[rows64(h)], da_in.at[head], send.at[1], da_recv.at[head], to).start()
     da_in[pl.ds(head, 1)] = da_out[rows64(head), :].reshape(1, HEAD, TOK)
 
     sibling = (z * 2 + (1 - core), cp)
@@ -347,13 +348,15 @@
         return moved[dim], (moved[2] * 2 + core, moved[0] * 4 + moved[1])
 
     def ar(src, dst, n, stage, k, to):
-        return remote(src, dst, ar_send.at[n, stage, k], ar_recv.at[n, stage, k], to)
+        at = (0, 14, 28)[n]
+        if stage in (1, 2, 3, 4):
+            at += stage if n == 2 else 3 * stage - 2 + k
+        elif stage == 6:
+            at += 5 if n == 2 else 13
+        return remote(src, dst, ar_send.at[n], ar_recv.at[at], to)
 
     def ar_got(ref, n, stage, k):
         ar(ref, ref, n, stage, k, (dp, cp)).wait_recv()
-
-    def ar_sent(ref, n, stage, k):
-        ar(ref, ref, n, stage, k, (dp, cp)).wait_send()
 
     def core_rows(n, c):
         return pl.ds(pl.multiple_of(SETS[n][0] + c * SETS[n][1], 16), SETS[n][3])
@@ -429,40 +432,34 @@
             _, to = along(k, d)
             remote(
                 g2.at[:, at], total.at[core, a_me, :, at],
-                ar_send.at[n, 5, k], last_recv.at[n, k, d - 1], to,
+                ar_send.at[n], last_recv.at[n, d - 1], to,
             ).start()
         total[pl.ds(core, 1), pl.ds(a_me, 1), :, at, :] = g2[:, at, :].reshape(
             1, 1, 4, SETS[n][4][k][0], 128
         )
         to_sibling(n, k, a_me)
 
+    def set_pieces(n):
+        return pl.ds(min(at for _, at in SETS[n][4].values()), SETS[n][3] // 4)
+
     def stage6(n):
         for d in (1, 3, 2):
+            held = total.at[0, 0, :, set_pieces(n)]
+            remote(held, held, ar_send.at[n], last_recv.at[n, d - 1], (dp, cp)).wait_recv()
             for k in SETS[n][4]:
-                a, _ = along(k, 4 - d)
-                held = total.at[core, a, :, piece(n, k)]
-                remote(
-                    held, held, ar_send.at[n, 5, k], last_recv.at[n, k, d - 1], (dp, cp)
-                ).wait_recv()
-                to_sibling(n, k, a)
-
-    def stage7(n, k):
-        ar_got(total.at[0, :, :, piece(n, k)], n, 6, k)
+                to_sibling(n, k, along(k, 4 - d)[0])
+
+    def stage7(n):
+        ar_got(total.at[0, :, :, set_pieces(n)], n, 6, 0)
 
     def all_colors(stage, n):
         for k in SETS[n][4]:
             stage(n, k)
 
     def settle(n):
-        ar_sent(r0.at[set_rows(n)], n, 0, 0)
-        for k in SETS[n][4]:
-            at = piece(n, k)
-            ar_sent(r1.at[:, at], n, 1, k)
-            ar_sent(r2.at[:, at], n, 2, k)
-            ar_sent(r3.at[pl.ds(0, 3), at], n, 3, k)
-            ar_sent(g2.at[pl.ds(0, 3), at], n, 4, k)
-            ar_sent(total.at[0, pl.ds(0, 3), :, at], n, 5, k)
-            ar_sent(total.at[0, :, :, at], n, 6, k)
+        kib = SETS[n][3] * 65 // 16
+        sent = pick32.at[pl.ds(0, 2 * kib)] if n == 2 else slope_keep.at[pl.ds(0, kib)]
+        remote(sent, sent, ar_send.at[n], ar_recv.at[0], (dp, cp)).wait_send()
 
     gated = (mixed * gate).astype(BF)
     low = normed_t[...].astype(BF)
@@ -503,7 +500,7 @@
             @pl.when(head != c)
             def _():
                 remote(
-                    da_in.at[c], da_in.at[c], send.at[6], da_recv.at[c], (dp, cp)
+                    da_in.at[c], da_in.at[c], send.at[1], da_recv.at[c], (dp, cp)
                 ).wait_recv()
 
         for c in group:
@@ -518,10 +515,10 @@
             @pl.when(cp != kb)
             def _():
                 remote(
-                    dk_out.at[kb], dk_in.at[half, rows64(head)], send.at[7], recv.at[7], (dp, kb)
+                    dk_out.at[kb], dk_in.at[half, rows64(head)], send.at[1], recv.at[7], (dp, kb)
                 ).start()
                 remote(
-                    dv_out.at[kb], dv_in.at[half, rows64(head)], send.at[8], recv.at[8], (dp, kb)
+                    dv_out.at[kb], dv_in.at[half, rows64(head)], send.at[1], recv.at[8], (dp, kb)
                 ).start()
 
     for i in range(HEADS):
@@ -529,7 +526,7 @@
         @pl.when(head != i)
         def _():
             remote(
-                dq_out.at[i], dq_in.at[rows64(head)], send.at[9], recv.at[9], (dp, block_of(i))
+                dq_out.at[i], dq_in.at[rows64(head)], send.at[1], recv.at[9], (dp, block_of(i))
             ).start()
 
     all_colors(stage2, 0)
@@ -584,15 +581,15 @@
         for to in everyone[group::4]:
             remote(
                 grad_out.at[tile(to[0] * N_CP + to[1])], grad_in.at[tile(me)],
-                send.at[10], recv.at[10], to,
+                send.at[1], recv.at[10], to,
             ).start()
 
     stage1(2)
     all_colors(stage4, 0)
+    send_grads(0)
     all_colors(stage2, 1)
     all_colors(stage2, 2)
     all_colors(stage5, 0)
-    send_grads(0)
     all_colors(stage3, 1)
     all_colors(stage3, 2)
     send_grads(1)
@@ -609,32 +606,16 @@
     wait_got(grad_in.at[pl.ds(0, SLOTS - SLOT)], 10)
     by_rank(grad_in, rows_got)
 
-    def onehot(rows_here, first):
-        index = iota((rows_here, DEVICES), 0) + first
-        return jnp.concatenate(
-            [jnp.where(index == req[c : c + 1, :], 1.0, 0.0).astype(BF) for c in range(CAP)],
-            axis=1,
-        )
-
-    hot_sum[...] = nn(onehot(HOT, 0), rows_got[...])
-    for t in range(4):
-        part = slice(t * HOT, (t + 1) * HOT)
-        cold_sum[part, :] = nn(onehot(HOT, HOT + t * HOT), rows_got[:, 0:COLD_W])
-
-    wait_sent(ids_all.at[pl.ds(0, DEVICES - 1)], 0)
-    wait_sent(row_in.at[pl.ds(0, SLOTS - SLOT)], 1)
-    wait_sent(k_in.at[pl.ds(0, N_CP - 1)], 2)
-    wait_sent(v_in.at[pl.ds(0, N_CP - 1)], 3)
-    wait_sent(q_in.at[pl.ds(0, HEADS - 1)], 4)
-    wait_sent(att_in.at[pl.ds(0, D - HEAD)], 5)
-    wait_sent(da_in.at[pl.ds(0, HEADS - 1)], 6)
-    wait_sent(dk_out.at[pl.ds(0, N_CP - 1)], 7)
-    wait_sent(dv_out.at[pl.ds(0, N_CP - 1)], 8)
-    wait_sent(dq_in.at[pl.ds(0, D - HEAD)], 9)
-    wait_sent(grad_in.at[pl.ds(0, SLOTS - SLOT)], 10)
+    hot_sum[...] = nn(named[0:HOT, :], rows_got[...])
+    cold_sum[...] = nn(named[HOT:, :], rows_got[:, 0:COLD_W])
+
+    sent = ids_all.at[pl.ds(0, DEVICES - 1)]
+    remote(sent, sent, send.at[0], recv.at[0], (dp, cp)).wait_send()
+    sent = slope_keep.at[pl.ds(0, SENT_KIB)]
+    remote(sent, sent, send.at[1], recv.at[0], (dp, cp)).wait_send()
     settle(0)
     for n in range(3):
-        all_colors(stage7, n)
+        stage7(n)
     settle(1)
     settle(2)
 
@@ -734,15 +715,15 @@
             v((N_CP, HEAD, TOK), BF), v((N_CP, HEAD, TOK), BF),
             v((D, TOK), BF), v((2, D, TOK), BF), v((2, D, TOK), BF),
             v((4 * D, TOK), BF), v((128, 4 * TOK), BF),
-            v((SLOTS, 128), BF), v((SLOTS, 128), BF), v((8, DEVICES), I32),
+            v((SLOTS, 128), BF), v((SLOTS, 128), BF), v((HOT + COLD, CAP * DEVICES), BF),
             v((W_ROWS, D), BF), v((W_ROWS // 2, D), BF), v((W_ROWS // 2, D), BF),
             v((3, PART_ROWS, D), BF), v((4, PART_ROWS, 128), BF),
             v((3, PART_ROWS, 128), BF), v((4, PART_ROWS, 128), BF),
             v((4, PART_ROWS, 128), BF),
-            pltpu.SemaphoreType.DMA((11,)), pltpu.SemaphoreType.DMA((11,)),
+            pltpu.SemaphoreType.DMA((2,)), pltpu.SemaphoreType.DMA((11,)),
             pltpu.SemaphoreType.DMA((HEADS,)),
-            pltpu.SemaphoreType.DMA((3, 7, 3)), pltpu.SemaphoreType.DMA((3, 7, 3)),
-            pltpu.SemaphoreType.DMA((3, 3, 3)),
+            pltpu.SemaphoreType.DMA((3,)), pltpu.SemaphoreType.DMA((34,)),
+            pltpu.SemaphoreType.DMA((3, 3)),
             pltpu.SemaphoreType.DMA((8,)),
         ],
         compiler_params=pltpu.CompilerParams(

time: 97 us -> 95.9 us (0.989)
  Pallas kernels: 96.1 us -> 95 us
    pallas_call x1, Pallas kernels: 92.9 us -> 91.8 us  [local(): pl.pallas_call(step_kernel, out_shape=(jax.ShapeDtypeStruct((TOK, D), BF)...]
where the time goes in v6:
time: 95.9 us; the launch traced here: 95.8 us
  Pallas kernels  95 us (99%)
    pallas_call x1, Pallas kernels, local(): pl.pallas_call(step_kernel, out_shape=(jax.ShapeDtypeStruct((TOK, D), BF)...  91.8 us
    pallas_call x1, Pallas kernels, local(): pl.pallas_call(finish_kernel, out_shape=(jax.ShapeDtypeStruct((TOK, D), B...  3.15 us

profile of v6, /device:TPU:1, one launch (start us, length us, event | category | flops | bytes accessed | tf_op | source)
XLA Modules:
  0.0 95.8 jit_solution(1786252814912762432)
XLA Ops:
  0.6 91.8 %step.1 = (bf16[128,512]{1,0:T(8,128)(2,1)S(1)}, f32[512,512]{1,0:T(8,128)S(1)}, f32[2048,128]{1,0:T(8,128)S(1)}, bf16[2,4,4,336,128]{4,3,2,1,0:T(8,128)(2,1)S(1)}) custom-call(s32[1,128]{1,0:T(1,128)} %bitcast.2, s32[1,128]{1,0:T(1,128)} %bitcast.3, bf16[512,512]{1,0:T(8,128)(2,1)} %hot_hbm.1, bf16[2048,128]{1,0:T(8,128)(2,1)} %cold_hbm.1, ...), custom_call_target="tpu_custom_call" | custom-call | tf_op jit(solution)/shard_map/step/pallas_call | solution.py:686
  92.5 3.2 %finish.1 = (bf16[128,512]{1,0:T(8,128)(2,1)}, f32[512,512]{1,0:T(8,128)}, f32[2048,128]{1,0:T(8,128)}, f32[128,512]{1,0:T(8,128)}, f32[512,2048]{1,0:T(8,128)}, /*index=5*/f32[512,512]{1,0:T(8,128)}) custom-call(bf16[128,512]{1,0:T(8,128)(2,1)S(1)} %get-tuple-element.10.layer, f32[512,512]{1,0:T(8,128)S(1)} %get-tuple-element.11.hot_sum, ...), custom_call_target="tpu_custom_call" | custom-call | tf_op jit(solution)/shard_map/finish/pallas_call | solution.py:734

commit v7 on v6

--- a/solution.py
+++ b/solution.py
@@ -587,12 +587,12 @@
     stage1(2)
     all_colors(stage4, 0)
     send_grads(0)
+    send_grads(1)
     all_colors(stage2, 1)
     all_colors(stage2, 2)
     all_colors(stage5, 0)
     all_colors(stage3, 1)
     all_colors(stage3, 2)
-    send_grads(1)
     send_grads(2)
     all_colors(stage4, 1)
     all_colors(stage4, 2)

time: 95.9 us -> 95.3 us (level)
  no operation moved by 1% of the time
where the time goes in v7:
time: 95.3 us; the launch traced here: 95.2 us
  Pallas kernels  94.3 us (99%)
    pallas_call x1, Pallas kernels, local(): pl.pallas_call(step_kernel, out_shape=(jax.ShapeDtypeStruct((TOK, D), BF)...  91.2 us
    pallas_call x1, Pallas kernels, local(): pl.pallas_call(finish_kernel, out_shape=(jax.ShapeDtypeStruct((TOK, D), B...  3.15 us

profile of v7, /device:TPU:1, one launch (start us, length us, event | category | flops | bytes accessed | tf_op | source)
XLA Modules:
  0.0 95.2 jit_solution(13485609087195411615)
XLA Ops:
  0.6 91.2 %step.1 = (bf16[128,512]{1,0:T(8,128)(2,1)S(1)}, f32[512,512]{1,0:T(8,128)S(1)}, f32[2048,128]{1,0:T(8,128)S(1)}, bf16[2,4,4,336,128]{4,3,2,1,0:T(8,128)(2,1)S(1)}) custom-call(s32[1,128]{1,0:T(1,128)} %bitcast.2, s32[1,128]{1,0:T(1,128)} %bitcast.3, bf16[512,512]{1,0:T(8,128)(2,1)} %hot_hbm.1, bf16[2048,128]{1,0:T(8,128)(2,1)} %cold_hbm.1, ...), custom_call_target="tpu_custom_call" | custom-call | tf_op jit(solution)/shard_map/step/pallas_call | solution.py:686
  91.8 3.2 %finish.1 = (bf16[128,512]{1,0:T(8,128)(2,1)}, f32[512,512]{1,0:T(8,128)}, f32[2048,128]{1,0:T(8,128)}, f32[128,512]{1,0:T(8,128)}, f32[512,2048]{1,0:T(8,128)}, /*index=5*/f32[512,512]{1,0:T(8,128)}) custom-call(bf16[128,512]{1,0:T(8,128)(2,1)S(1)} %get-tuple-element.10.layer, f32[512,512]{1,0:T(8,128)S(1)} %get-tuple-element.11.hot_sum, ...), custom_call_target="tpu_custom_call" | custom-call | tf_op jit(solution)/shard_map/finish/pallas_call | solution.py:734
